TPU v7x, 128 devices: a whole 4x4x4 slice. The times are simulated.
128 devices in a mesh: dp: 16 (over z, y), ep: 8 (over x, core).
Axes of the slice: x: 4, y: 4, z: 4, core: 2. Of those that a mesh axis runs over, the one named last changes fastest.
Arguments:
- x_tokens: bfloat16 [196608, 768], P(('dp', 'ep'))
- modality: int32 [196608], P(('dp', 'ep'))
- router: float32 [768, 8], replicated
- expert_ids: int32 [196608], P(('dp', 'ep'))
- priority: int32 [196608], P(('dp', 'ep'))
- w_in: bfloat16 [8, 768, 3072], P('ep')
- b_in: bfloat16 [8, 3072], P('ep')
- w_out: bfloat16 [8, 3072, 768], P('ep')
- b_out: bfloat16 [8, 768], P('ep')
- dy_out: bfloat16 [196608, 768], P(('dp', 'ep'))
Outputs:
- output 1: bfloat16 [196608, 768], P(('dp', 'ep'))
- output 2: float32 [], replicated
- output 3: bfloat16 [196608, 768], P(('dp', 'ep'))
- output 4: float32 [768, 8], replicated
- output 5: bfloat16 [8, 768, 3072], P('ep')
- output 6: bfloat16 [8, 3072], P('ep')
- output 7: bfloat16 [8, 3072, 768], P('ep')
- output 8: bfloat16 [8, 768], P('ep')
All inputs are finite; a program needn't handle non-finite values.
Results may differ from a plain program's by a relative error of at most 0.0160492.
Values are sent between devices in bfloat16 or wider.
A program may use at most 1 GiB of HBM per device.

v0:
```python
import jax
import jax.numpy as jnp
from jax import lax
from jax.sharding import PartitionSpec as P

ALL_AXES = ("dp", "ep")


def route_tokens(expert_ids, priority, num_experts, capacity):
    num_tokens = expert_ids.shape[0]
    sort_order = jnp.argsort(expert_ids * num_tokens + priority)
    sorted_rank = jnp.argsort(sort_order)
    counts = jnp.sum((expert_ids[:, None] == jnp.arange(num_experts)[None, :]).astype(jnp.int32), axis=0)
    starts = jnp.cumsum(counts) - counts
    slot_rank = jnp.arange(capacity)
    slot_token = sort_order[jnp.minimum(starts[:, None] + slot_rank[None, :], num_tokens - 1)]
    slot_valid = slot_rank[None, :] < counts[:, None]
    position = sorted_rank - starts[expert_ids]
    keep_mask = position < capacity
    token_slot = expert_ids * capacity + jnp.minimum(position, capacity - 1)
    return slot_token, slot_valid, token_slot, keep_mask


def router_forward(x_loc, modality, router, expert_ids):
    num_experts = router.shape[1]
    logits = jnp.dot(x_loc, router, precision=lax.Precision.HIGHEST, preferred_element_type=jnp.float32)
    log_probs = jax.nn.log_softmax(logits, axis=-1)
    router_probs = jnp.exp(log_probs)
    expert_onehot = (expert_ids[:, None] == jnp.arange(num_experts)[None, :]).astype(jnp.float32)
    gate_prob = jnp.sum(router_probs * expert_onehot, axis=-1)
    mod_mask = jnp.stack([modality == 0, modality == 1]).astype(jnp.float32)
    entropy = -jnp.sum(router_probs * log_probs, axis=-1)
    local_stats = jnp.concatenate([jnp.dot(mod_mask, router_probs), jnp.dot(mod_mask, entropy)[:, None], jnp.sum(mod_mask, axis=1, keepdims=True)], axis=1)
    return log_probs, router_probs, expert_onehot, gate_prob, mod_mask, local_stats


def aux_from_stats(stats, num_experts):
    mod_count = stats[:, num_experts + 1]
    mean_probs = stats[:, :num_experts] / mod_count[:, None]
    aux_loss = jnp.sum(stats[:, num_experts] / mod_count) + jnp.sum(mean_probs * jnp.log(mean_probs))
    return aux_loss, mean_probs, mod_count


def router_backward(x_loc, router, log_probs, router_probs, expert_onehot, mod_mask, mean_probs, mod_count, d_gate):
    inv_count = jnp.dot(1.0 / mod_count, mod_mask)
    global_part = jnp.einsum("mt,me->te", mod_mask, jnp.log(mean_probs) / mod_count[:, None])
    d_probs = expert_onehot * d_gate[:, None] + global_part - log_probs * inv_count[:, None]
    d_logits = router_probs * (d_probs - jnp.sum(d_probs * router_probs, axis=-1, keepdims=True))
    d_router_part = jnp.einsum("tw,te->we", x_loc, d_logits, precision=lax.Precision.HIGHEST, preferred_element_type=jnp.float32)
    dx_router = jnp.einsum("te,we->tw", d_logits, router, precision=lax.Precision.HIGHEST, preferred_element_type=jnp.float32)
    return d_router_part, dx_router.astype(jnp.bfloat16)


def solution(mesh):
    token_spec = P(ALL_AXES)
    expert_spec = P("ep")

    def local_step(x_loc, modality, router, expert_ids, priority, w_in, b_in, w_out, b_out, dy_loc):
        num_tokens, model_width = x_loc.shape
        num_experts = router.shape[1]
        capacity = num_tokens // num_experts
        slot_token, slot_valid, token_slot, keep_mask = route_tokens(expert_ids, priority, num_experts, capacity)
        log_probs, router_probs, expert_onehot, gate_prob, mod_mask, local_stats = router_forward(x_loc, modality, router, expert_ids)
        aux_loss, mean_probs, mod_count = aux_from_stats(lax.psum(local_stats, ALL_AXES), num_experts)
        keep_col = keep_mask[:, None]
        slot_col = slot_valid[:, :, None]
        send_rows = jnp.where(slot_col, x_loc[slot_token], 0).astype(jnp.bfloat16)
        recv_rows = lax.all_to_all(send_rows, "ep", 0, 1, tiled=True)
        act_in = jnp.einsum("ecw,ewf->ecf", recv_rows, w_in, preferred_element_type=jnp.float32) + b_in[:, None, :].astype(jnp.float32)
        act_out, gelu_pullback = jax.vjp(jax.nn.gelu, act_in)
        hidden = act_out.astype(jnp.bfloat16)
        expert_out = jnp.einsum("ecf,efw->ecw", hidden, w_out, preferred_element_type=jnp.float32) + b_out[:, None, :].astype(jnp.float32)
        back_rows = lax.all_to_all(expert_out.astype(jnp.bfloat16), "ep", 1, 0, tiled=True)
        y_tok = back_rows.reshape(num_experts * capacity, model_width)[token_slot].astype(jnp.float32)
        out_tokens = jnp.where(keep_col, gate_prob[:, None] * y_tok, 0.0).astype(jnp.bfloat16)
        dy_f32 = dy_loc.astype(jnp.float32)
        d_gate = jnp.where(keep_mask, jnp.sum(dy_f32 * y_tok, axis=-1), 0.0)
        d_ytok = jnp.where(keep_col, gate_prob[:, None] * dy_f32, 0.0).astype(jnp.bfloat16)
        d_send = jnp.where(slot_col, d_ytok[slot_token], 0).astype(jnp.bfloat16)
        d_recv = lax.all_to_all(d_send, "ep", 0, 1, tiled=True)
        d_b_out = jnp.sum(d_recv.astype(jnp.float32), axis=1)
        d_w_out = jnp.einsum("ecf,ecw->efw", hidden, d_recv, preferred_element_type=jnp.float32)
        d_hidden = jnp.einsum("ecw,efw->ecf", d_recv, w_out, preferred_element_type=jnp.float32).astype(jnp.bfloat16)
        d_act = gelu_pullback(d_hidden.astype(jnp.float32))[0]
        d_b_in = jnp.sum(d_act, axis=1)
        d_act_bf = d_act.astype(jnp.bfloat16)
        d_w_in = jnp.einsum("ecw,ecf->ewf", recv_rows, d_act_bf, preferred_element_type=jnp.float32)
        d_rows = jnp.einsum("ecf,ewf->ecw", d_act_bf, w_in, preferred_element_type=jnp.float32).astype(jnp.bfloat16)
        d_back = lax.all_to_all(d_rows, "ep", 1, 0, tiled=True)
        dx_expert = jnp.where(keep_col, d_back.reshape(num_experts * capacity, model_width)[token_slot], 0).astype(jnp.bfloat16)
        d_router_part, dx_router = router_backward(x_loc, router, log_probs, router_probs, expert_onehot, mod_mask, mean_probs, mod_count, d_gate)
        d_router = lax.psum(d_router_part, ALL_AXES)
        expert_grads = lax.psum((d_w_in, d_b_in, d_w_out, d_b_out), "dp")
        return (out_tokens, aux_loss, dx_expert + dx_router, d_router) + tuple(grad_sum.astype(jnp.bfloat16) for grad_sum in expert_grads)

    return jax.shard_map(
        local_step,
        mesh=mesh,
        in_specs=(token_spec, token_spec, P(), token_spec, token_spec, expert_spec, expert_spec, expert_spec, expert_spec, token_spec),
        out_specs=(token_spec, P(), token_spec, P(), expert_spec, expert_spec, expert_spec, expert_spec),
        check_vma=False,
    )
```

profile of v0, /device:TPU:0, one launch (start us, length us, event | category | flops | bytes accessed | tf_op | source)
XLA Modules:
  0.0 953.6 jit_solution(1968027991692130932)
XLA Ops:
  0.6 0.0 copy-start
  0.6 1.0 convert_reduce_fusion.1
  1.6 0.7 multiply_add_fusion
  2.3 0.1 iota_compare_fusion.1
  2.4 0.2 reduce-window.7
  2.6 0.1 compare_select_fusion.2
  2.7 0.1 reshape.261
  2.8 5.0 sort.31
  7.8 8.4 gather_fusion
  16.2 0.1 gather.22
  16.3 0.1 reshape.269
  16.4 5.6 gather_fusion.1
  22.0 3.4 broadcast_select_fusion.1
  25.4 5.0 all-to-all-start
  30.4 29.9 %all-to-all-done = bf16[8,192,768]{2,1,0:T(8,128)(2,1)} async-done(((bf16[8,192,768]{2,1,0:T(8,128)(2,1)}), bf16[8,192,768]{2,1,0:T(8,128)(2,1)}, u32[]{:S(2)}, u32[]{:S(2)}) %all-to-all-start) | async-done | bytes 2359328 | tf_op jit(solution)/shard_map/all_to_all | solution.py:68
  60.3 17.6 %multiply_convert_fusion = (bf16[1536,3072]{1,0:T(8,128)(2,1)S(1)}, f32[1536,3072]{1,0:T(8,128)}) fusion(f32[3072]{0:T(1024)S(1)} %bitcast.102, bf16[1536,768]{1,0:T(8,128)(2,1)} %bitcast.11, bf16[1,768,3072]{2,1,0:T(8,128)(2,1)} %param.15), kind=kOutput, calls=%fused_computation.18 | convolution fusion | flops 7294943232 | bytes 35401728 | tf_op jit(solution)/shard_map/ecw,ewf->ecf/dot_general | solution.py:69
  77.9 13.4 %fusion.38 = bf16[1,1536,768]{2,1,0:T(8,128)(2,1)S(1)} fusion(bf16[1536,3072]{1,0:T(8,128)(2,1)S(1)} %get-tuple-element.38, bf16[1,3072,768]{2,1,0:T(8,128)(2,1)} %param.17, f32[768]{0:T(1024)S(1)} %convert_reduce_fusion.3), kind=kOutput, calls=%fused_computation.45 | convolution fusion | flops 7250116608 | bytes 16518144 | tf_op jit(solution)/shard_map/ecf,efw->ecw/dot_general | solution.py:72
  91.3 33.9 %copy.43 = bf16[1,1536,768]{2,0,1:T(2,128)(2,1)} copy(bf16[1,1536,768]{2,1,0:T(8,128)(2,1)S(1)} %fusion.38) | data formatting | bytes 4718592 | tf_op jit(solution)/shard_map/convert_element_type | solution.py:73
  125.2 0.5 broadcast.299
  125.7 25.5 %reduce.11 = bf16[1536,768]{1,0:T(8,128)(2,1)} reduce(bf16[1536,1,768]{2,1,0:T(2,128)(2,1)} %bitcast.96, bf16[]{:T(256)} %broadcast.299), dimensions={1}, to_apply=%bitcast.93.reduce_sub_computation | reduce | bytes 4718594
  151.3 5.9 reshape.314
  157.2 4.5 all-to-all-start.1
  161.7 1.9 fusion.52
  163.8 0.1 convert_reduce_fusion.2
  163.9 0.1 copy.32
  164.1 0.1 convolution_bitcast_fusion.3
  164.2 0.1 fusion.42
  164.3 0.1 pad_maximum_fusion
  164.4 83.7 %psum.42 = f32[2,10]{1,0:T(2,128)S(1)} all-reduce(f32[2,10]{1,0:T(2,128)S(1)} %pad_maximum_fusion), channel_id=1, replica_groups=mesh['dp'=16,'ep'=8] {'dp','ep'}, use_global_device_ids=true, to_apply=%region_9.10 | all-reduce | flops 20 | bytes 160 | tf_op jit(solution)/shard_map/psum | solution.py:64
  248.2 5.0 sort.32
  253.2 0.2 slice_reduce_fusion
  253.4 0.6 fusion.51
  254.0 5.0 compare_select_fusion
  259.0 0.1 convolution_reduce_fusion
  259.2 7.0 reshape.315
  266.2 4.1 copy.41
  270.3 8.7 gather_fusion.2
  279.0 3.2 fusion.13
  282.2 5.0 broadcast_select_fusion.2
  287.1 0.3 fusion.46
  287.5 3.0 fusion.12
  290.4 8.7 gather_fusion.3
  299.1 3.3 broadcast_select_fusion
  302.4 4.6 all-to-all-start.2
  307.0 0.6 divide_reduce_fusion
  307.6 0.7 fusion.47
  309.6 1.0 convolution_bitcast_fusion.2
  310.6 81.3 %psum.43 = f32[768,8]{0,1:T(8,128)} all-reduce(f32[768,8]{0,1:T(8,128)S(1)} %convolution_bitcast_fusion.2), channel_id=1, replica_groups=mesh['dp'=16,'ep'=8] {'dp','ep'}, use_global_device_ids=true, to_apply=%region_14.15 | all-reduce | flops 6144 | bytes 49152 | tf_op jit(solution)/shard_map/psum | solution.py:92
  391.9 0.0 all-to-all-done.2
  391.9 23.5 %fusion.53 = (f32[3072]{0:T(1024)S(1)}, bf16[1536,3072]{1,0:T(8,128)(2,1)S(1)}) fusion(f32[1536,3072]{1,0:T(8,128)} %get-tuple-element.39, f32[3072]{0:T(1024)S(1)} %bitcast.103, bf16[1536,768]{1,0:T(8,128)(2,1)} %bitcast.20, bf16[1,3072,768]{2,1,0:T(8,128)(2,1)} %param.17), kind=kOutput, calls=%fused_computation.100 | convolution fusion | flops 7361000448 | bytes 35414016 | tf_op jit(solution)/shard_map/ecw,efw->ecf/dot_general | solution.py:83
  415.4 0.0 slice-start.1
  415.4 10.4 %fusion.33 = bf16[1,1536,768]{2,1,0:T(8,128)(2,1)S(1)} fusion(bf16[1,768,3072]{2,1,0:T(8,128)(2,1)} %param.15, bf16[1536,3072]{1,0:T(8,128)(2,1)S(1)} %get-tuple-element.42), kind=kOutput, calls=%fused_computation.44 | convolution fusion | flops 7248936960 | bytes 16515072 | tf_op jit(solution)/shard_map/ecf,ewf->ecw/dot_general | solution.py:88
  425.8 12.3 %convolution_bitcast_fusion.1 = f32[1,768,3072]{2,1,0:T(8,128)} fusion(bf16[1536,768]{1,0:T(8,128)(2,1)} %bitcast.11, bf16[1536,3072]{1,0:T(8,128)(2,1)S(1)} %get-tuple-element.42), kind=kOutput, calls=%fused_computation.24 | convolution fusion | flops 7247757312 | bytes 21233664 | tf_op jit(solution)/shard_map/ecw,ecf->ewf/dot_general | solution.py:87
  438.1 11.9 %convolution_bitcast_fusion = f32[1,3072,768]{2,1,0:T(8,128)} fusion(bf16[1536,3072]{1,0:T(8,128)(2,1)S(1)} %bitcast.108, bf16[1536,768]{1,0:T(8,128)(2,1)} %bitcast.20), kind=kOutput, calls=%fused_computation.23 | convolution fusion | flops 7247757312 | bytes 21233664 | tf_op jit(solution)/shard_map/ecf,ecw->efw/dot_general | solution.py:82
  450.0 33.6 %copy.42 = bf16[1,1536,768]{2,0,1:T(2,128)(2,1)} copy(bf16[1,1536,768]{2,1,0:T(8,128)(2,1)S(1)} %fusion.33) | data formatting | bytes 4718592 | tf_op jit(solution)/shard_map/convert_element_type | solution.py:88
  483.7 24.3 %reduce.12 = bf16[1536,768]{1,0:T(8,128)(2,1)S(1)} reduce(bf16[1536,1,768]{2,1,0:T(2,128)(2,1)} %bitcast.97, bf16[]{:T(256)} %broadcast.299), dimensions={1}, to_apply=%bitcast.92.reduce_sub_computation | reduce | bytes 4718594
  508.0 3.3 reshape.316
  511.2 3.6 all-to-all-start.3
  514.8 2.1 convert_reduce_fusion
  516.9 411.1 %all-reduce.2 = (bf16[1,768,3072]{2,1,0:T(8,128)(2,1)}, bf16[1,3072]{1,0:T(2,128)(2,1)}, bf16[1,3072,768]{2,1,0:T(8,128)(2,1)}, bf16[1,768]{1,0:T(2,128)(2,1)}) all-reduce(f32[1,768,3072]{2,1,0:T(8,128)} %convolution_bitcast_fusion.1, f32[1,3072]{1,0:T(1,128)S(1)} %bitcast.104, ...), channel_id=1, replica_groups=mesh['dp'=16,'ep'=8] {'dp'}, use_global_device_ids=true, to_apply=%region_15.16 | all-reduce | flops 4722432 | bytes 28334592 | tf_op jit(solution)/shard_map/psum | solution.py:93
  928.1 4.6 reshape.317
  932.6 4.1 copy.40
  936.8 8.8 gather_fusion.4
  945.6 6.6 fusion.32
  (45 shorter events, 0.2 us)
Async XLA Ops:
  0.6 15.7 %copy-start = (bf16[1536,768]{1,0:T(8,128)(2,1)S(1)}, bf16[1536,768]{1,0:T(8,128)(2,1)}, u32[]{:S(2)}) copy-start(bf16[1536,768]{1,0:T(8,128)(2,1)} %param.10) | copy-start | bytes 7077892
  22.0 8.4 copy-start.6
  22.0 8.4 copy-start.8
  25.4 35.0 %all-to-all-start = ((bf16[8,192,768]{2,1,0:T(8,128)(2,1)}), bf16[8,192,768]{2,1,0:T(8,128)(2,1)}, u32[]{:S(2)}, u32[]{:S(2)}) async-start(bf16[8,192,768]{2,1,0:T(8,128)(2,1)} %broadcast_select_fusion.1), calls=%async_computation | async-start | bytes 4718592 | tf_op jit(solution)/shard_map/all_to_all | solution.py:68
  77.9 13.4 %copy-start.9 = (bf16[1536,3072]{1,0:T(8,128)(2,1)}, bf16[1536,3072]{1,0:T(8,128)(2,1)S(1)}, u32[]{:S(2)}) copy-start(bf16[1536,3072]{1,0:T(8,128)(2,1)S(1)} %get-tuple-element.38) | copy-start | bytes 28311556
  151.3 10.4 %copy-start.5 = (f32[768,8]{0,1:T(8,128)S(1)}, f32[768,8]{0,1:T(8,128)}, u32[]{:S(2)}) copy-start(f32[768,8]{0,1:T(8,128)} %param.12) | copy-start | bytes 73732
  157.2 6.5 copy-start.7
  157.2 96.8 %copy-start.4 = (s32[1536]{0:T(1024)S(1)}, s32[1536]{0:T(1024)}, u32[]{:S(2)}) copy-start(s32[1536]{0:T(1024)} %param.13) | copy-start | bytes 18436
  157.2 102.0 %all-to-all-start.1 = ((bf16[8,2,73728]{2,1,0:T(2,128)(2,1)}), bf16[8,2,73728]{2,1,0:T(2,128)(2,1)}, u32[]{:S(2)}, u32[]{:S(2)}) async-start(bf16[8,2,73728]{2,1,0:T(2,128)(2,1)} %reshape.314), calls=%async_computation.1 | async-start | bytes 4718592 | tf_op jit(solution)/shard_map/all_to_all | solution.py:73
  279.0 8.5 copy-start.2
  279.0 8.5 copy-start.3
  302.4 89.5 %all-to-all-start.2 = ((bf16[8,192,768]{2,1,0:T(8,128)(2,1)}), bf16[8,192,768]{2,1,0:T(8,128)(2,1)}, u32[]{:S(2)}, u32[]{:S(2)}) async-start(bf16[8,192,768]{2,1,0:T(8,128)(2,1)} %broadcast_select_fusion), calls=%async_computation.2 | async-start | bytes 4718592 | tf_op jit(solution)/shard_map/all_to_all | solution.py:80
  415.4 22.7 %slice-start = ((s8[9437184]{0:T(1024)(128)(4,1)}), s8[4194304]{0:T(1024)(128)(4,1)S(1)}, s32[]{:S(2)}) async-start(s8[9437184]{0:T(1024)(128)(4,1)} %bitcast.107), calls=%async_computation.4 | async-start | bytes 8388608
  415.4 22.7 %slice-start.1 = ((s8[9437184]{0:T(1024)(128)(4,1)}), s8[4194304]{0:T(1024)(128)(4,1)S(1)}, s32[]{:S(2)}) async-start(s8[9437184]{0:T(1024)(128)(4,1)} %bitcast.107), calls=%async_computation.5 | async-start | bytes 8388608
  425.8 12.3 %slice-start.2 = ((s8[9437184]{0:T(1024)(128)(4,1)}), s8[1048576]{0:T(1024)(128)(4,1)S(1)}, s32[]{:S(2)}) async-start(s8[9437184]{0:T(1024)(128)(4,1)} %bitcast.107), calls=%async_computation.6 | async-start | bytes 2097152
  511.2 416.8 %all-to-all-start.3 = ((bf16[8,2,73728]{2,1,0:T(2,128)(2,1)}), bf16[8,2,73728]{2,1,0:T(2,128)(2,1)S(1)}, u32[]{:S(2)}, u32[]{:S(2)}) async-start(bf16[8,2,73728]{2,1,0:T(2,128)(2,1)} %reshape.316), calls=%async_computation.3 | async-start | bytes 4718592 | tf_op jit(solution)/shard_map/all_to_all | solution.py:89
  936.8 15.5 %copy-start.1 = (bf16[1536,768]{1,0:T(8,128)(2,1)S(1)}, bf16[1536,768]{1,0:T(8,128)(2,1)}, u32[]{:S(2)}) copy-start(bf16[1536,768]{1,0:T(8,128)(2,1)} %param.10) | copy-start | bytes 7077892
where the time goes:
time: 957 us; the launch traced here: 954 us
  blocking collectives  576 us (60%)
  local copies, waits for them, and re-layouts  138 us (14%)
  matrix products  99.3 us (10%)
  other arithmetic  88.5 us (9%)
  waiting for transfers between devices  29.9 us (3%)
  starting transfers between devices  17.7 us (2%)
    psum x1, blocking collectives, local_step(): expert_grads = lax.psum((d_w_in, d_b_in, d_w_out, d_b_out), 'dp')  411 us
    psum x1, blocking collectives, local_step(): lax.psum(local_stats, ALL_AXES)  83.7 us
    psum x1, blocking collectives, local_step(): d_router = lax.psum(d_router_part, ALL_AXES)  81.3 us
    unnamed x3, other arithmetic  49.8 us
    convert_element_type x1, local copies, waits for them, and re-layouts, local_step(): expert_out.astype(jnp.bfloat16)  33.9 us
    convert_element_type x1, local copies, waits for them, and re-layouts, local_step(): jnp.einsum('ecf,ewf->ecw', d_act_bf, w_in, preferred_element_type=jnp.flo...  33.6 us
    all_to_all x1, waiting for transfers between devices, local_step(): recv_rows = lax.all_to_all(send_rows, 'ep', 0, 1, tiled=True)  29.9 us
    unnamed x33, local copies, waits for them, and re-layouts  29.6 us
  transfers between devices with their start and end apart: 4, of which 1 were waited for; matrix products, arithmetic and copies ran while one was open for 2% of the time, Pallas kernels for 0%

commit v1 on v0

v1 whole, which is shorter than its diff:
```python
import functools

import jax
import jax.numpy as jnp
from jax import lax
from jax.experimental import pallas as pl
from jax.experimental.pallas import tpu as pltpu
from jax.sharding import PartitionSpec as P

ALL_AXES = ("dp", "ep")
MESH = pl.DeviceIdType.MESH
F32 = jnp.float32
BF16 = jnp.bfloat16
NOWHERE = -1.0


def col_of(row):
    return jnp.transpose(jnp.broadcast_to(row, (8, row.shape[1])))


def row_of(col):
    return jnp.transpose(jnp.broadcast_to(col, (col.shape[0], 8)))


def split3(a):
    hi = a.astype(BF16)
    rest = a - hi.astype(F32)
    mid = rest.astype(BF16)
    lo = (rest - mid.astype(F32)).astype(BF16)
    return hi, mid, lo


def nt(a, b):
    return lax.dot_general(a, b, (((1,), (1,)), ((), ())), preferred_element_type=F32)


def tn(a, b):
    return lax.dot_general(a, b, (((0,), (0,)), ((), ())), preferred_element_type=F32)


def nn(a, b):
    return jnp.dot(a, b, preferred_element_type=F32)


def route_kernel(capacity, ids_ref, prio_ref, x_ref, slot_ref, send_ref, keycol):
    n = ids_ref.shape[1]
    experts = n // capacity
    ids = ids_ref[...].astype(F32)
    key = ids * n + prio_ref[...].astype(F32)
    low = ids * n
    keycol[...] = col_of(key)

    def count(j, acc):
        col = keycol[pl.ds(pl.multiple_of(j * 128, 128), 128), :][:, 0:1]
        before = jnp.logical_and(col < key, col >= low)
        return acc + jnp.sum(before.astype(F32), axis=0, keepdims=True)

    position = lax.fori_loop(0, n // 128, count, jnp.zeros((1, n), F32))
    slot = jnp.where(position < capacity, ids * capacity + position, NOWHERE)
    slot_ref[...] = jnp.broadcast_to(slot, slot_ref.shape)

    def gather(e, carry):
        index = (lax.broadcasted_iota(jnp.int32, (capacity, n), 0) + e * capacity).astype(F32)
        pick = (index == slot).astype(BF16)
        send_ref[e] = nn(pick, x_ref[...]).astype(BF16)
        return carry

    lax.fori_loop(0, experts, gather, 0)


def router_kernel(capacity, ids_ref, mod_ref, slot_ref, x_ref, dy_ref, router3_ref, logp_ref, stats_ref, send_ref, dyt):
    n = ids_ref.shape[1]
    experts = n // capacity
    logits3 = nt(router3_ref[...], x_ref[...])
    logits = logits3[0:experts] + logits3[experts:2 * experts] + logits3[2 * experts:3 * experts]
    shifted = logits - jnp.max(logits, axis=0, keepdims=True)
    logp = shifted - jnp.log(jnp.sum(jnp.exp(shifted), axis=0, keepdims=True))
    logp_ref[...] = logp
    probs = jnp.exp(logp)
    onehot = (lax.broadcasted_iota(jnp.int32, (experts, n), 0) == ids_ref[...]).astype(F32)
    gate = jnp.sum(probs * onehot, axis=0, keepdims=True)
    entropy = -jnp.sum(probs * logp, axis=0, keepdims=True)
    stats = []
    for m in range(2):
        mask = (mod_ref[...] == m).astype(F32)
        stats.append(jnp.broadcast_to(jnp.sum(probs * mask, axis=1, keepdims=True), (experts, 128)))
        stats.append(jnp.broadcast_to(jnp.sum(entropy * mask, axis=1, keepdims=True), (8, 128)))
        stats.append(jnp.broadcast_to(jnp.sum(mask, axis=1, keepdims=True), (8, 128)))
    stats_ref[...] = jnp.concatenate(stats, axis=0)
    dyt[...] = (col_of(gate)[:, 0:1] * dy_ref[...].astype(F32)).astype(BF16)
    slot = slot_ref[0:1, :]

    def gather(e, carry):
        index = (lax.broadcasted_iota(jnp.int32, (capacity, n), 0) + e * capacity).astype(F32)
        pick = (index == slot).astype(BF16)
        send_ref[e] = nn(pick, dyt[...]).astype(BF16)
        return carry

    lax.fori_loop(0, experts, gather, 0)


def forward_kernel(steps, chunks, rows_ref, w_in_ref, b_in_ref, w_out_ref, b_out_ref, hidden_ref, slope_ref, y_ref, acc):
    step = pl.program_id(0)
    n = rows_ref.shape[0]
    size = n // chunks

    @pl.when(step == 0)
    def _():
        acc[...] = jnp.broadcast_to(b_out_ref[...].astype(F32), acc.shape)

    for c in range(chunks):
        part = pl.ds(c * size, size)
        a = nn(rows_ref[part, :], w_in_ref[...]) + b_in_ref[...].astype(F32)
        root = 0.7978845608028654
        sq = a * a
        t = jnp.tanh(root * (a + 0.044715 * (sq * a)))
        half = 0.5 * (1.0 + t)
        hidden = (a * half).astype(BF16)
        slope_ref[part, :] = half + (0.5 * root) * a * (1.0 - t * t) * (1.0 + (3 * 0.044715) * sq)
        hidden_ref[part, :] = hidden
        acc[part, :] += nn(hidden, w_out_ref[...])

    @pl.when(step == steps - 1)
    def _():
        y_ref[...] = acc[...].astype(BF16)


def dwout_kernel(hidden_ref, d_ref, dw_ref):
    dw_ref[...] = tn(hidden_ref[...], d_ref[...])


def backward_kernel(steps, chunks, rows_ref, d_ref, slope_ref, w_in_ref, w_out_ref, dw_ref, db_in_ref, db_out_ref, d_rows_ref, acc, act):
    step = pl.program_id(0)
    n = rows_ref.shape[0]
    size = n // chunks

    @pl.when(step == 0)
    def _():
        db_out_ref[...] = jnp.sum(d_ref[...].astype(F32), axis=0, keepdims=True)
        acc[...] = jnp.zeros_like(acc)

    total = jnp.zeros(db_in_ref.shape, F32)
    for c in range(chunks):
        part = pl.ds(c * size, size)
        d_hidden = nt(d_ref[part, :], w_out_ref[...]).astype(BF16)
        d_act = d_hidden.astype(F32) * slope_ref[part, :]
        total += jnp.sum(d_act, axis=0, keepdims=True)
        d_act_bf = d_act.astype(BF16)
        act[part, :] = d_act_bf
        acc[part, :] += nt(d_act_bf, w_in_ref[...])
    db_in_ref[...] = total
    dw_ref[...] = tn(rows_ref[...], act[...])

    @pl.when(step == steps - 1)
    def _():
        d_rows_ref[...] = acc[...].astype(BF16)


def global_terms(stats, experts):
    loss = jnp.zeros((1, 128), F32)
    terms = []
    inv = []
    for m in range(2):
        base = 24 * m
        count = stats[base + 16:base + 17]
        mean = stats[base:base + 8] / count
        log_mean = jnp.log(mean)
        loss = loss + stats[base + 8:base + 9] / count + jnp.sum(mean * log_mean, axis=0, keepdims=True)
        terms.append(log_mean / count)
        inv.append(1.0 / count)
    return loss, terms, inv


def combine_kernel(capacity, chunks, ids_ref, mod_ref, slot_ref, logp_ref, back_ref, dy_ref, x_ref, stats_ref, out_ref, dlog_ref, dr_ref, loss_ref):
    n = ids_ref.shape[1]
    experts = n // capacity
    size = n // chunks
    loss, terms, inv = global_terms(stats_ref[...], experts)
    loss_ref[...] = jnp.broadcast_to(loss, loss_ref.shape)
    dr = jnp.zeros((3 * experts, x_ref.shape[1]), F32)
    for c in range(chunks):
        part = pl.ds(c * size, size)
        lanes = pl.ds(c * size, size)
        slot_col = col_of(slot_ref[0:1, lanes])[:, 0:1]
        pick = (lax.broadcasted_iota(jnp.int32, (size, n), 1).astype(F32) == slot_col).astype(BF16)
        y = nn(pick, back_ref[...])
        logp = logp_ref[:, lanes]
        probs = jnp.exp(logp)
        onehot = (lax.broadcasted_iota(jnp.int32, (experts, size), 0) == ids_ref[:, lanes]).astype(F32)
        gate = jnp.sum(probs * onehot, axis=0, keepdims=True)
        out_ref[part, :] = (col_of(gate)[:, 0:1] * y).astype(BF16)
        d_gate = row_of(jnp.sum(dy_ref[part, :].astype(F32) * y, axis=1, keepdims=True))[0:1]
        is_text = mod_ref[:, lanes] == 1
        global_part = jnp.where(is_text, terms[1][:, 0:1], terms[0][:, 0:1])
        inv_count = jnp.where(is_text, inv[1][:, 0:1], inv[0][:, 0:1])
        d_probs = onehot * d_gate + global_part - logp * inv_count
        d_log = probs * (d_probs - jnp.sum(d_probs * probs, axis=0, keepdims=True))
        dlog_ref[:, lanes] = d_log
        dr += nn(jnp.concatenate(split3(d_log), axis=0), x_ref[part, :])
    dr_ref[...] = dr[0:experts] + dr[experts:2 * experts] + dr[2 * experts:]


def token_grad_kernel(chunks, slot_ref, dlog_ref, back_ref, router_ref, dx_ref):
    n = slot_ref.shape[1]
    size = n // chunks
    r = split3(router_ref[...])
    rights = jnp.concatenate([r[0], r[1], r[0], r[1], r[2], r[0]], axis=0)
    for c in range(chunks):
        part = pl.ds(c * size, size)
        lanes = pl.ds(c * size, size)
        slot_col = col_of(slot_ref[0:1, lanes])[:, 0:1]
        pick = (lax.broadcasted_iota(jnp.int32, (size, n), 1).astype(F32) == slot_col).astype(BF16)
        d = split3(dlog_ref[:, lanes])
        lefts = jnp.concatenate([d[0], d[0], d[1], d[1], d[0], d[2]], axis=0)
        routed = tn(lefts, rights).astype(BF16)
        expert = nn(pick, back_ref[...])
        dx_ref[part, :] = (expert + routed.astype(F32)).astype(BF16)


def reduce_kernel(whole_rows, a_ref, o_ref, bufs, send_sem, recv_sem, pair_send, pair_recv, work):
    dp = lax.axis_index("dp")
    ep = lax.axis_index("ep")
    z, y = dp // 4, lax.rem(dp, 4)
    x, core = ep // 2, lax.rem(ep, 2)
    partner = (dp, x * 2 + 1 - core)
    rings = []
    for axis in range(3):
        me = (x, y, z)[axis]
        peers = []
        for k in range(1, 4):
            to = lax.rem(me + k, 4)
            peers.append(((dp, to * 2 + core), (z * 4 + to, ep), (to * 4 + y, ep))[axis])
        rings.append((me, peers))

    barrier = pltpu.get_barrier_semaphore()
    everyone = [partner] + [p for _, peers in rings for p in peers]
    for p in everyone:
        pl.semaphore_signal(barrier, inc=1, device_id=p, device_id_type=MESH)
    pl.semaphore_wait(barrier, len(everyone))

    head = pl.ds(0, whole_rows)
    work[0] = a_ref[...]
    pair = pltpu.make_async_remote_copy(
        src_ref=work.at[0, head], dst_ref=work.at[1, head], send_sem=pair_send, recv_sem=pair_recv,
        device_id=partner, device_id_type=MESH)
    pair.start()
    pair.wait()
    work[2] = a_ref[...]
    work[2, head, :] = work[0, head, :] + work[1, head, :]
    for axis in range(3):
        me, peers = rings[axis]
        rows = head if axis == 0 else pl.ds(0, a_ref.shape[0])
        bufs[axis, me] = work[axis + 2]
        copies = []
        for k in range(3):
            copy = pltpu.make_async_remote_copy(
                src_ref=work.at[axis + 2, rows], dst_ref=bufs.at[axis, me, rows], send_sem=send_sem.at[axis, k],
                recv_sem=recv_sem.at[axis, k], device_id=peers[k], device_id_type=MESH)
            copy.start()
            copies.append(copy)
        for copy in copies:
            copy.wait()
        total = bufs[axis, 0, rows, :] + bufs[axis, 1, rows, :] + bufs[axis, 2, rows, :] + bufs[axis, 3, rows, :]
        if axis == 2:
            o_ref[...] = total
        else:
            work[axis + 3] = work[axis + 2]
            work[axis + 3, rows, :] = total


def small_reduce(a, whole_rows, collective_id):
    rows, cols = a.shape
    return pl.pallas_call(
        functools.partial(reduce_kernel, whole_rows),
        out_shape=jax.ShapeDtypeStruct((rows, cols), F32),
        in_specs=[pl.BlockSpec(memory_space=pltpu.VMEM)],
        out_specs=pl.BlockSpec(memory_space=pltpu.VMEM),
        scratch_shapes=[
            pltpu.VMEM((3, 4, rows, cols), F32),
            pltpu.SemaphoreType.DMA((3, 3)),
            pltpu.SemaphoreType.DMA((3, 3)),
            pltpu.SemaphoreType.DMA,
            pltpu.SemaphoreType.DMA,
            pltpu.VMEM((5, rows, cols), F32),
        ],
        compiler_params=pltpu.CompilerParams(collective_id=collective_id, has_side_effects=True),
        cost_estimate=pl.CostEstimate(flops=2_000_000_000, bytes_accessed=100_000, transcendentals=0),
        name=f"small_reduce_{collective_id}",
    )(a)


def vmem(count):
    return [pl.BlockSpec(memory_space=pltpu.VMEM)] * count


def params():
    return pltpu.CompilerParams(vmem_limit_bytes=60 * 1024 * 1024)


def cost(flops, size):
    return pl.CostEstimate(flops=int(flops), bytes_accessed=int(size), transcendentals=0)


def solution(mesh):
    token_spec = P(ALL_AXES)
    expert_spec = P("ep")

    def local_step(x, modality, router, expert_ids, priority, w_in, b_in, w_out, b_out, dy):
        n, width = x.shape
        experts = router.shape[1]
        hid = w_in.shape[2]
        capacity = n // experts
        w_in, w_out = w_in[0], w_out[0]
        ids = expert_ids.reshape(1, n)
        prio = priority.reshape(1, n)
        mod = modality.reshape(1, n)
        router_t = jnp.transpose(router)
        router3 = jnp.concatenate(split3_outside(router_t), axis=0)
        shape = jax.ShapeDtypeStruct
        gather_flops = 2 * n * n * width

        slot, send_rows = pl.pallas_call(
            functools.partial(route_kernel, capacity),
            out_shape=(shape((8, n), F32), shape((experts, capacity, width), BF16)),
            in_specs=vmem(3), out_specs=tuple(vmem(2)),
            scratch_shapes=[pltpu.VMEM((n, 8), F32)],
            compiler_params=params(), cost_estimate=cost(gather_flops, 4 * n * width), name="route",
        )(ids, prio, x)
        recv_rows = lax.all_to_all(send_rows, "ep", 0, 0, tiled=True).reshape(n, width)

        logp, stats_part, send_d = pl.pallas_call(
            functools.partial(router_kernel, capacity),
            out_shape=(shape((experts, n), F32), shape((48, 128), F32), shape((experts, capacity, width), BF16)),
            in_specs=vmem(6), out_specs=tuple(vmem(3)),
            scratch_shapes=[pltpu.VMEM((n, width), BF16)],
            compiler_params=params(), cost_estimate=cost(gather_flops, 6 * n * width), name="router",
        )(ids, mod, slot, x, dy, router3)
        d_recv = lax.all_to_all(send_d, "ep", 0, 0, tiled=True).reshape(n, width)
        stats = small_reduce(stats_part, 48, 1)

        tile = 512
        steps = hid // tile
        whole = pl.BlockSpec((n, width), lambda i: (0, 0))
        w_in_spec = pl.BlockSpec((width, tile), lambda i: (0, i))
        w_out_spec = pl.BlockSpec((tile, width), lambda i: (i, 0))
        act_spec = pl.BlockSpec((n, tile), lambda i: (0, i))
        hid_row = pl.BlockSpec((1, tile), lambda i: (0, i))
        width_row = pl.BlockSpec((1, width), lambda i: (0, 0))
        mm = 2 * n * width * hid

        hidden, slope, y = pl.pallas_call(
            functools.partial(forward_kernel, steps, 4),
            grid=(steps,),
            out_shape=(shape((n, hid), BF16), shape((n, hid), F32), shape((n, width), BF16)),
            in_specs=[whole, w_in_spec, hid_row, w_out_spec, width_row],
            out_specs=(act_spec, act_spec, whole),
            scratch_shapes=[pltpu.VMEM((n, width), F32)],
            compiler_params=params(), cost_estimate=cost(2 * mm, 6 * n * hid), name="expert_forward",
        )(recv_rows, w_in, b_in, w_out, b_out)
        back_y = lax.all_to_all(y.reshape(experts, capacity, width), "ep", 0, 0, tiled=True).reshape(n, width)

        d_w_out = pl.pallas_call(
            dwout_kernel,
            grid=(steps,),
            out_shape=shape((hid, width), F32),
            in_specs=[act_spec, whole],
            out_specs=w_out_spec,
            compiler_params=params(), cost_estimate=cost(mm, 2 * n * hid), name="expert_dwout",
        )(hidden, d_recv)
        d_w_out = gather_sum(d_w_out)

        d_w_in, d_b_in, d_b_out, d_rows = pl.pallas_call(
            functools.partial(backward_kernel, steps, 4),
            grid=(steps,),
            out_shape=(shape((width, hid), F32), shape((1, hid), F32), shape((1, width), F32), shape((n, width), BF16)),
            in_specs=[whole, whole, act_spec, w_in_spec, w_out_spec],
            out_specs=(w_in_spec, hid_row, width_row, whole),
            scratch_shapes=[pltpu.VMEM((n, width), F32), pltpu.VMEM((n, tile), BF16)],
            compiler_params=params(), cost_estimate=cost(3 * mm, 6 * n * hid), name="expert_backward",
        )(recv_rows, d_recv, slope, w_in, w_out)
        d_w_in = gather_sum(d_w_in)
        d_back = lax.all_to_all(d_rows.reshape(experts, capacity, width), "ep", 0, 0, tiled=True).reshape(n, width)

        out, d_log, d_router_part, loss = pl.pallas_call(
            functools.partial(combine_kernel, capacity, 4),
            out_shape=(shape((n, width), BF16), shape((experts, n), F32), shape((experts, width), F32), shape((8, 128), F32)),
            in_specs=vmem(8), out_specs=tuple(vmem(4)),
            compiler_params=params(), cost_estimate=cost(gather_flops, 8 * n * width), name="combine",
        )(ids, mod, slot, logp, back_y, dy, x, stats)

        d_x = pl.pallas_call(
            functools.partial(token_grad_kernel, 4),
            out_shape=shape((n, width), BF16),
            in_specs=vmem(4), out_specs=vmem(1)[0],
            compiler_params=params(), cost_estimate=cost(gather_flops, 6 * n * width), name="token_grad",
        )(slot, d_log, d_back, router_t)

        small = jnp.concatenate([d_router_part, d_b_in.reshape(hid // width, width), d_b_out, jnp.zeros((3, width), F32)], axis=0)
        small = small_reduce(small, experts, 2)
        d_router = jnp.transpose(small[0:experts])
        d_b_in = small[experts:experts + hid // width].reshape(1, hid).astype(BF16)
        d_b_out = small[experts + hid // width:experts + hid // width + 1].astype(BF16)
        return out, loss[0, 0], d_x, d_router, d_w_in[None], d_b_in, d_w_out[None], d_b_out

    def gather_sum(part):
        own = lax.psum_scatter(part, "dp", scatter_dimension=0, tiled=True)
        return lax.all_gather(own.astype(BF16), "dp", axis=0, tiled=True)

    def split3_outside(a):
        hi = lax.reduce_precision(a, 8, 7)
        mid = lax.reduce_precision(a - hi, 8, 7)
        return hi.astype(BF16), mid.astype(BF16), (a - hi - mid).astype(BF16)

    return jax.shard_map(
        local_step,
        mesh=mesh,
        in_specs=(token_spec, token_spec, P(), token_spec, token_spec, expert_spec, expert_spec, expert_spec, expert_spec, token_spec),
        out_specs=(token_spec, P(), token_spec, P(), expert_spec, expert_spec, expert_spec, expert_spec),
        check_vma=False,
    )
```

time: 957 us -> 445 us (0.46)
  blocking collectives: 576 us -> 34.2 us
  Pallas kernels: 0 us -> 174 us
  waiting for transfers between devices: 29.9 us -> 184 us
  local copies, waits for them, and re-layouts: 138 us -> 17.6 us
  matrix products: 99.3 us -> 0 us
  other arithmetic: 88.5 us -> 7.14 us
  between operations: 3.58 us -> 13.9 us
    psum x3 -> x0, blocking collectives: 576 us -> none  [the longest x1 411 us: local_step(): expert_grads = lax.psum((d_w_in, d_b_in, d_w_out, d_b_out), 'dp')]
    pallas_call x0 -> x9, Pallas kernels: none -> 174 us  [the longest x2 60.3 us: small_reduce(): pl.pallas_call(functools.partial(reduce_kernel, whole_rows), out_shape=ja...]
    reduce_scatter x0 -> x2, waiting for transfers between devices: none -> 164 us  [gather_sum(): own = lax.psum_scatter(part, 'dp', scatter_dimension=0, tiled=True)]
    dot_general x13 -> x0, matrix products: 99.3 us -> none  [the longest x1 23.5 us: local_step(): jnp.einsum('ecw,efw->ecf', d_recv, w_out, preferred_element_type=jnp.floa...]
    convert_element_type x2 -> x0, local copies, waits for them, and re-layouts: 67.5 us -> none  [the longest x1 33.9 us: local_step(): expert_out.astype(jnp.bfloat16)]
    unnamed x3 -> x0, other arithmetic: 49.8 us -> none
    gather x7 -> x0, local copies, waits for them, and re-layouts: 40.8 us -> none  [the longest x1 8.83 us: local_step(): d_back.reshape(num_experts * capacity, model_width)[token_slot]]
    all_to_all x0 -> x1, blocking collectives: none -> 34.2 us  [local_step(): lax.all_to_all(y.reshape(experts, capacity, width), 'ep', 0, 0, tiled=True)]
  transfers between devices with their start and end apart: 4 -> 7, of which waited for: 1 -> 4; matrix products, arithmetic and copies ran while one was open for 2% -> 3% of each run, Pallas kernels for 0% -> 30%
where the time goes in v1:
time: 445 us; the launch traced here: 444 us
  waiting for transfers between devices  184 us (41%)
  Pallas kernels  174 us (39%)
  blocking collectives  34.2 us (8%)
  local copies, waits for them, and re-layouts  17.6 us (4%)
  between operations  13.9 us (3%)
  starting transfers between devices  12.9 us (3%)
  other arithmetic  7.14 us (2%)
    reduce_scatter x2, waiting for transfers between devices, gather_sum(): own = lax.psum_scatter(part, 'dp', scatter_dimension=0, tiled=True)  164 us
    pallas_call x2, Pallas kernels, small_reduce(): pl.pallas_call(functools.partial(reduce_kernel, whole_rows), out_shape=ja...  60.3 us
    all_to_all x1, blocking collectives, local_step(): lax.all_to_all(y.reshape(experts, capacity, width), 'ep', 0, 0, tiled=True)  34.2 us
    pallas_call x1, Pallas kernels, local_step(): pl.pallas_call(functools.partial(backward_kernel, steps, 4), grid=(steps,...  31.9 us
    pallas_call x1, Pallas kernels, local_step(): pl.pallas_call(functools.partial(forward_kernel, steps, 4), grid=(steps,)...  28.6 us
    all_to_all x1, waiting for transfers between devices, local_step(): lax.all_to_all(send_rows, 'ep', 0, 0, tiled=True).reshape(n, width)  18.5 us
    pallas_call x1, Pallas kernels, local_step(): pl.pallas_call(dwout_kernel, grid=(steps,), out_shape=shape((hid, width),...  13.4 us
    pallas_call x1, Pallas kernels, local_step(): pl.pallas_call(functools.partial(route_kernel, capacity), out_shape=(shap...  11 us
  transfers between devices with their start and end apart: 7, of which 4 were waited for; matrix products, arithmetic and copies ran while one was open for 3% of the time, Pallas kernels for 30%

profile of v1, /device:TPU:0, one launch (start us, length us, event | category | flops | bytes accessed | tf_op | source)
XLA Modules:
  0.0 444.2 jit_solution(10704913090382672711)
XLA Ops:
  7.2 1.3 reshape.60.ids_ref
  8.5 1.3 reshape.62.prio_ref
  9.8 11.0 %route.1 = (f32[8,1536]{1,0:T(8,128)}, bf16[8,192,768]{2,1,0:T(8,128)(2,1)}) custom-call(s32[1,1536]{1,0:T(1,128)} %reshape.60.ids_ref, s32[1,1536]{1,0:T(1,128)} %reshape.62.prio_ref, bf16[1536,768]{1,0:T(8,128)(2,1)} %x_ref.5), custom_call_target="tpu_custom_call" | custom-call | flops 3623878656 | bytes 4718592 | tf_op jit(solution)/shard_map/route/pallas_call | solution.py:322
  20.8 0.0 copy-start.6
  20.8 0.0 copy-start.4
  20.8 4.6 %all-to-all-start = ((bf16[8,192,768]{2,1,0:T(8,128)(2,1)}), bf16[8,192,768]{2,1,0:T(8,128)(2,1)S(1)}, u32[]{:S(2)}, u32[]{:S(2)}) async-start(bf16[8,192,768]{2,1,0:T(8,128)(2,1)} %get-tuple-element.26), calls=%async_computation | async-start | bytes 4718592 | tf_op jit(solution)/shard_map/all_to_all | solution.py:329
  25.4 0.0 copy-done.6
  25.4 0.6 reshape.61.mod_ref
  26.0 0.0 copy-done.4
  26.0 0.6 pad_maximum_fusion.router3_ref
  26.6 10.2 %router.1 = (f32[8,1536]{1,0:T(8,128)}, f32[48,128]{1,0:T(8,128)}, bf16[8,192,768]{2,1,0:T(8,128)(2,1)}) custom-call(s32[1,1536]{1,0:T(1,128)} %reshape.60.ids_ref, s32[1,1536]{1,0:T(1,128)} %reshape.61.mod_ref, f32[8,1536]{1,0:T(8,128)} %get-tuple-element.24.slot_ref, bf16[1536,768]{1,0:T(8,128)(2,1)} %x_ref.5, bf16[1536,768]{1,0:T(8,128)(2,1)} %dy_ref.3, ...), custom_call_target="tpu_custom_call" | custom-call | flops 3623878656 | bytes 7077888 | tf_op jit(solution)/shard_map/router/pallas_call | solution.py:331
  36.8 18.5 %all-to-all-done = bf16[8,192,768]{2,1,0:T(8,128)(2,1)S(1)} async-done(((bf16[8,192,768]{2,1,0:T(8,128)(2,1)}), bf16[8,192,768]{2,1,0:T(8,128)(2,1)S(1)}, u32[]{:S(2)}, u32[]{:S(2)}) %all-to-all-start) | async-done | bytes 2359328 | tf_op jit(solution)/shard_map/all_to_all | solution.py:329
  55.4 0.0 copy-start.3
  55.4 1.4 copy-done.3
  56.8 4.4 all-to-all-start.2
  61.1 0.0 reduce-scatter.3.cloned.1.call-start
  61.2 28.6 %expert_forward.1 = (bf16[1536,3072]{1,0:T(8,128)(2,1)}, f32[1536,3072]{1,0:T(8,128)}, bf16[1536,768]{1,0:T(8,128)(2,1)}) custom-call(bf16[1536,768]{1,0:T(8,128)(2,1)} %bitcast.25, bf16[768,3072]{1,0:T(8,128)(2,1)} %bitcast.30, bf16[1,3072]{1,0:T(2,128)(2,1)} %b_in_ref.1, bf16[3072,768]{1,0:T(8,128)(2,1)} %bitcast.32, bf16[1,768]{1,0:T(2,128)(2,1)} %b_out_ref.1), custom_call_target="tpu_custom_call" | custom-call | flops 14495514624 | bytes 28311552 | tf_op jit(solution)/shard_map/expert_forward/pallas_call | solution.py:351
  89.8 1.3 all-to-all-done.2
  91.0 31.9 %expert_backward.1 = (f32[768,3072]{1,0:T(8,128)}, f32[1,3072]{1,0:T(1,128)}, f32[1,768]{1,0:T(1,128)}, bf16[1536,768]{1,0:T(8,128)(2,1)}) custom-call(bf16[1536,768]{1,0:T(8,128)(2,1)} %bitcast.26, bf16[1536,768]{1,0:T(8,128)(2,1)} %bitcast.7.d_ref, f32[1536,3072]{1,0:T(8,128)} %get-tuple-element.33.slope_ref, bf16[768,3072]{1,0:T(8,128)(2,1)} %bitcast.31, ...), custom_call_target="tpu_custom_call" | custom-call | flops 21743271936 | bytes 28311552 | tf_op jit(solution)/shard_map/expert_backward/pallas_call | solution.py:372
  123.0 0.0 reduce-scatter.3.cloned.1.call-update
  123.0 0.2 reduce-scatter.5.cloned.1.call-start
  123.2 13.4 %expert_dwout.1 = f32[3072,768]{1,0:T(8,128)} custom-call(bf16[1536,3072]{1,0:T(8,128)(2,1)} %get-tuple-element.39.hidden_ref, bf16[1536,768]{1,0:T(8,128)(2,1)} %bitcast.7.d_ref), custom_call_target="tpu_custom_call" | custom-call | flops 7247757312 | bytes 9437184 | tf_op jit(solution)/shard_map/expert_dwout/pallas_call | solution.py:362
  136.6 0.0 reduce-scatter.5.cloned.1.call-update
  136.6 0.0 copy-start.1
  136.6 0.0 all-gather.3.cloned.1.call-start
  136.7 75.8 %reduce-scatter.3.cloned.1.call-done = f32[48,3072]{1,0:T(8,128)} async-done(((f32[768,3072]{1,0:T(8,128)}), f32[48,3072]{1,0:T(8,128)}) %reduce-scatter.3.cloned.1.call-update) | async-done | bytes 589840 | tf_op jit(solution)/shard_map/reduce_scatter | solution.py:406
  212.5 1.8 convert_element_type.31
  214.3 0.0 all-gather.3.cloned.1.call-update
  214.3 0.0 all-gather.5.cloned.1.call-start
  214.3 88.7 %reduce-scatter.5.cloned.1.call-done = f32[192,768]{1,0:T(8,128)} async-done(((f32[3072,768]{1,0:T(8,128)}), f32[192,768]{1,0:T(8,128)}) %reduce-scatter.5.cloned.1.call-update) | async-done | bytes 589840 | tf_op jit(solution)/shard_map/reduce_scatter | solution.py:406
  303.1 1.8 convert_element_type.33
  304.9 0.0 all-gather.5.cloned.1.call-update
  304.9 0.0 copy-done.1
  304.9 34.2 %all_to_all.20 = bf16[8,192,768]{2,1,0:T(8,128)(2,1)} all-to-all(bf16[8,192,768]{2,1,0:T(8,128)(2,1)S(1)} %bitcast.23), channel_id=1, replica_groups=mesh['dp'=16,'ep'=8] {'ep'}, dimensions={0} | all-to-all | bytes 4718592 | tf_op jit(solution)/shard_map/all_to_all | solution.py:360
  339.1 3.6 all-to-all-start.3
  342.7 0.1 pad.3.clone
  342.8 0.0 copy-start.5
  342.8 40.3 %small_reduce_1.1.stats_ref = f32[48,128]{1,0:T(8,128)} custom-call(f32[48,128]{1,0:T(8,128)} %get-tuple-element.28.a_ref), custom_call_target="tpu_custom_call" | custom-call | flops 2000000000 | bytes 100000 | tf_op jit(solution)/shard_map/small_reduce_1/pallas_call | solution.py:273
  383.0 0.5 broadcast.5
  383.6 0.0 copy-done.5
  383.6 0.7 reduce.3
  384.3 0.0 copy-start.7
  384.3 10.9 %combine.1 = (bf16[1536,768]{1,0:T(8,128)(2,1)}, f32[8,1536]{1,0:T(8,128)}, f32[8,768]{1,0:T(8,128)}, f32[8,128]{1,0:T(8,128)}) custom-call(s32[1,1536]{1,0:T(1,128)} %reshape.60.ids_ref, s32[1,1536]{1,0:T(1,128)} %reshape.61.mod_ref, f32[8,1536]{1,0:T(8,128)} %get-tuple-element.24.slot_ref, f32[8,1536]{1,0:T(8,128)} %get-tuple-element.25.logp_ref, ...), custom_call_target="tpu_custom_call" | custom-call | flops 3623878656 | bytes 9437184 | tf_op jit(solution)/shard_map/combine/pallas_call | solution.py:384
  395.2 1.2 slice.14
  396.4 0.0 copy-done.7
  396.4 1.4 maximum_maximum_fusion.a_ref
  397.8 20.0 %small_reduce_2.1 = f32[16,768]{1,0:T(8,128)} custom-call(f32[16,768]{1,0:T(8,128)} %maximum_maximum_fusion.a_ref), custom_call_target="tpu_custom_call" | custom-call | flops 2000000000 | bytes 100000 | tf_op jit(solution)/shard_map/small_reduce_2/pallas_call | solution.py:273
  417.8 0.8 convert.4
  418.6 0.6 slice.19
  419.2 0.6 copy.18
  419.8 1.3 slice_bitcast_fusion
  421.2 0.0 all-to-all-done.3
  421.2 0.0 copy-start.2
  421.2 1.4 copy-done.2
  422.6 7.8 %token_grad.1 = bf16[1536,768]{1,0:T(8,128)(2,1)} custom-call(f32[8,1536]{1,0:T(8,128)} %get-tuple-element.24.slot_ref, f32[8,1536]{1,0:T(8,128)} %get-tuple-element.31.dlog_ref, bf16[1536,768]{1,0:T(8,128)(2,1)} %bitcast.24, f32[8,768]{1,0:T(8,128)} %bitcast.28), custom_call_target="tpu_custom_call" | custom-call | flops 3623878656 | bytes 7077888 | tf_op jit(solution)/shard_map/token_grad/pallas_call | solution.py:391
  430.5 0.0 all-gather.3.cloned.1.call-done
  430.5 0.0 all-gather.5.cloned.1.call-done
  430.5 0.0 copy-start
  430.5 5.0 %copy.21 = bf16[1,768,3072]{2,1,0:T(8,128)(2,1)} copy(bf16[1,768,3072]{2,1,0:T(8,128)(2,1)} %bitcast.21) | data formatting | bytes 9437184
  435.5 0.0 copy-done
  435.5 2.2 copy.22
  (4 shorter events, 0.0 us)
Async XLA Ops:
  20.8 4.6 %copy-start.6 = (s32[1536]{0:T(1024)S(1)}, s32[1536]{0:T(1024)}, u32[]{:S(2)}) copy-start(s32[1536]{0:T(1024)} %param.11) | copy-start | bytes 18436
  20.8 5.2 %copy-start.4 = (f32[768,8]{0,1:T(8,128)S(1)}, f32[768,8]{0,1:T(8,128)}, u32[]{:S(2)}) copy-start(f32[768,8]{0,1:T(8,128)} %param.12) | copy-start | bytes 73732
  20.8 34.6 %all-to-all-start = ((bf16[8,192,768]{2,1,0:T(8,128)(2,1)}), bf16[8,192,768]{2,1,0:T(8,128)(2,1)S(1)}, u32[]{:S(2)}, u32[]{:S(2)}) async-start(bf16[8,192,768]{2,1,0:T(8,128)(2,1)} %get-tuple-element.26), calls=%async_computation | async-start | bytes 4718592 | tf_op jit(solution)/shard_map/all_to_all | solution.py:329
  55.4 1.4 copy-start.3
  56.8 34.3 %all-to-all-start.2 = ((bf16[8,192,768]{2,1,0:T(8,128)(2,1)}), bf16[8,192,768]{2,1,0:T(8,128)(2,1)}, u32[]{:S(2)}, u32[]{:S(2)}) async-start(bf16[8,192,768]{2,1,0:T(8,128)(2,1)} %get-tuple-element.32), calls=%async_computation.2 | async-start | bytes 4718592 | tf_op jit(solution)/shard_map/all_to_all | solution.py:338
  61.1 151.3 %reduce-scatter.3.cloned.1.call-start = ((), (), s32[]{:S(2)}) async-start(), calls=%async_computation.6 | async-start | bytes 10027008 | tf_op jit(solution)/shard_map/reduce_scatter | solution.py:406
  123.0 180.1 %reduce-scatter.5.cloned.1.call-start = ((), (), s32[]{:S(2)}) async-start(), calls=%async_computation.8 | async-start | bytes 10027008 | tf_op jit(solution)/shard_map/reduce_scatter | solution.py:406
  136.6 168.3 %copy-start.1 = (bf16[1536,768]{1,0:T(8,128)(2,1)S(1)}, bf16[1536,768]{1,0:T(8,128)(2,1)}, u32[]{:S(2)}) copy-start(bf16[1536,768]{1,0:T(8,128)(2,1)} %get-tuple-element.27) | copy-start | bytes 7077892
  136.6 293.8 %all-gather.3.cloned.1.call-start = ((), (), s32[]{:S(2)}) async-start(), calls=%async_computation.7 | async-start | bytes 5013504 | tf_op jit(solution)/shard_map/all_gather | solution.py:407
  214.3 216.2 %all-gather.5.cloned.1.call-start = ((), (), s32[]{:S(2)}) async-start(), calls=%async_computation.9 | async-start | bytes 5013504 | tf_op jit(solution)/shard_map/all_gather | solution.py:407
  339.1 82.1 %all-to-all-start.3 = ((bf16[8,192,768]{2,1,0:T(8,128)(2,1)}), bf16[8,192,768]{2,1,0:T(8,128)(2,1)S(1)}, u32[]{:S(2)}, u32[]{:S(2)}) async-start(bf16[8,192,768]{2,1,0:T(8,128)(2,1)} %bitcast.8), calls=%async_computation.3 | async-start | bytes 4718592 | tf_op jit(solution)/shard_map/all_to_all | solution.py:382
  342.8 40.8 %copy-start.5 = (f32[1,3072]{1,0:T(1,128)S(1)}, f32[1,3072]{1,0:T(1,128)}, u32[]{:S(2)}) copy-start(f32[1,3072]{1,0:T(1,128)} %get-tuple-element.36) | copy-start | bytes 36868
  384.3 12.1 %copy-start.7 = (f32[1,768]{1,0:T(1,128)S(1)}, f32[1,768]{1,0:T(1,128)}, u32[]{:S(2)}) copy-start(f32[1,768]{1,0:T(1,128)} %get-tuple-element.37) | copy-start | bytes 9220
  421.2 1.4 copy-start.2
  430.5 5.0 %copy-start = (bf16[3072,768]{1,0:T(8,128)(2,1)S(1)}, bf16[3072,768]{1,0:T(8,128)(2,1)}, u32[]{:S(2)}) copy-start(bf16[3072,768]{1,0:T(8,128)(2,1)} %all-gather.5.cloned.1.call-done) | copy-start | bytes 14155780
Sparse Core Ops, SparseCore 0:
  123.1 89.3 reduce-scatter.2
  215.9 87.0 reduce-scatter.4
  305.2 52.8 all-gather.2
  360.1 55.7 all-gather.4

commit v2 on v1

--- a/solution.py
+++ b/solution.py
@@ -12,6 +12,7 @@
 F32 = jnp.float32
 BF16 = jnp.bfloat16
 NOWHERE = -1.0
+TILE = 256
 
 
 def col_of(row):
@@ -99,7 +100,7 @@
     lax.fori_loop(0, experts, gather, 0)
 
 
-def forward_kernel(steps, chunks, rows_ref, w_in_ref, b_in_ref, w_out_ref, b_out_ref, hidden_ref, slope_ref, y_ref, acc):
+def forward_kernel(steps, chunks, rows_ref, w_in_ref, b_in_ref, w_out_ref, b_out_ref, hidden_t_ref, slope_ref, rows_t_ref, y_ref, acc):
     step = pl.program_id(0)
     n = rows_ref.shape[0]
     size = n // chunks
@@ -107,6 +108,7 @@
     @pl.when(step == 0)
     def _():
         acc[...] = jnp.broadcast_to(b_out_ref[...].astype(F32), acc.shape)
+        rows_t_ref[...] = jnp.transpose(rows_ref[...])
 
     for c in range(chunks):
         part = pl.ds(c * size, size)
@@ -116,8 +118,10 @@
         t = jnp.tanh(root * (a + 0.044715 * (sq * a)))
         half = 0.5 * (1.0 + t)
         hidden = (a * half).astype(BF16)
-        slope_ref[part, :] = half + (0.5 * root) * a * (1.0 - t * t) * (1.0 + (3 * 0.044715) * sq)
-        hidden_ref[part, :] = hidden
+        slope = half + (0.5 * root) * a * (1.0 - t * t) * (1.0 + (3 * 0.044715) * sq)
+        for j in range(slope_ref.shape[0]):
+            slope_ref[j, part, :] = slope[:, j * TILE:(j + 1) * TILE]
+        hidden_t_ref[:, part] = jnp.transpose(hidden)
         acc[part, :] += nn(hidden, w_out_ref[...])
 
     @pl.when(step == steps - 1)
@@ -125,35 +129,212 @@
         y_ref[...] = acc[...].astype(BF16)
 
 
-def dwout_kernel(hidden_ref, d_ref, dw_ref):
-    dw_ref[...] = tn(hidden_ref[...], d_ref[...])
-
-
-def backward_kernel(steps, chunks, rows_ref, d_ref, slope_ref, w_in_ref, w_out_ref, dw_ref, db_in_ref, db_out_ref, d_rows_ref, acc, act):
-    step = pl.program_id(0)
-    n = rows_ref.shape[0]
+def grads_kernel(
+    hidden_t, slope, w_in, w_out, rows_t, d_rows_in, y, summed, db_in, db_out, back_y, back_d,
+    part_sum, land_a, land_b, own, hbuf, sbuf, ibuf, obuf, act, acc, d_out,
+    send_sem, recv_sem, own_sem, load_sem, load2_sem, y_send, y_recv, d_send, d_recv, self_sem,
+):
+    dp = lax.axis_index("dp")
+    ep = lax.axis_index("ep")
+    z, yy = dp // 4, lax.rem(dp, 4)
+    tiles = part_sum.shape[0]
+    units = tiles // 4
+    half = tiles // 2
+    experts = y.shape[0]
+    n, width = acc.shape
+    chunks = 4
     size = n // chunks
 
-    @pl.when(step == 0)
-    def _():
-        db_out_ref[...] = jnp.sum(d_ref[...].astype(F32), axis=0, keepdims=True)
-        acc[...] = jnp.zeros_like(acc)
-
-    total = jnp.zeros(db_in_ref.shape, F32)
-    for c in range(chunks):
-        part = pl.ds(c * size, size)
-        d_hidden = nt(d_ref[part, :], w_out_ref[...]).astype(BF16)
-        d_act = d_hidden.astype(F32) * slope_ref[part, :]
-        total += jnp.sum(d_act, axis=0, keepdims=True)
-        d_act_bf = d_act.astype(BF16)
-        act[part, :] = d_act_bf
-        acc[part, :] += nt(d_act_bf, w_in_ref[...])
-    db_in_ref[...] = total
-    dw_ref[...] = tn(rows_ref[...], act[...])
-
-    @pl.when(step == steps - 1)
-    def _():
-        d_rows_ref[...] = acc[...].astype(BF16)
+    def place(stream):
+        way = 1 - 2 * lax.rem(stream, 2)
+        first_z = stream // 2
+        pa = yy * (1 - first_z) + z * first_z
+        pb = z * (1 - first_z) + yy * first_z
+        y_next, z_next = lax.rem(yy + way + 4, 4), lax.rem(z + way + 4, 4)
+        along_y, along_z = z * 4 + y_next, z_next * 4 + yy
+        next_a = along_y * (1 - first_z) + along_z * first_z
+        next_b = along_z * (1 - first_z) + along_y * first_z
+        return way, pa, pb, next_a, next_b
+
+    def wrap(v):
+        return lax.rem(v + 16, 4)
+
+    def send(tile, k):
+        way, pa, pb, next_a, next_b = place(lax.rem(tile, 4))
+        if k < 3:
+            src, dst, to = part_sum.at[tile, wrap(pa - way * (k + 1))], land_a.at[tile, k], next_a
+        elif k < 6:
+            src, dst, to = part_sum.at[tile, pa, wrap(pb - way * (k - 2))], land_b.at[tile, k - 3], next_b
+        elif k == 6:
+            src, dst, to = own.at[tile], summed.at[tile, pa, pb], next_b
+        elif k < 9:
+            src = summed.at[tile, pa, wrap(pb - way * (k - 6))]
+            dst, to = src, next_b
+        else:
+            src = summed.at[tile, wrap(pa - way * (k - 9))]
+            dst, to = src, next_a
+        return pltpu.make_async_remote_copy(
+            src_ref=src, dst_ref=dst, send_sem=send_sem.at[tile, k], recv_sem=recv_sem.at[tile, k],
+            device_id=(to, ep), device_id_type=MESH)
+
+    def keep(tile):
+        way, pa, pb, _, _ = place(lax.rem(tile, 4))
+        return pltpu.make_async_copy(own.at[tile], summed.at[tile, pa, pb], own_sem.at[tile])
+
+    def advance(tile, k):
+        way, pa, pb, _, _ = place(lax.rem(tile, 4))
+        send(tile, k - 1).wait_recv()
+        if k <= 3:
+            block = wrap(pa - way * (k + 1))
+            part_sum[tile, block] = part_sum[tile, block] + land_a[tile, k - 1]
+        elif k <= 6:
+            block = wrap(pb - way * (k - 2))
+            total = part_sum[tile, pa, block] + land_b[tile, k - 4]
+            if k < 6:
+                part_sum[tile, pa, block] = total
+            else:
+                own[tile] = total.astype(BF16)
+                keep(tile).start()
+        elif k == 9:
+            keep(tile).wait()
+        if k < 12:
+            send(tile, k).start()
+
+    def wave(t, stream):
+        for k in range(12, 0, -1):
+            unit = t - k
+
+            @pl.when(jnp.logical_and(unit >= 0, unit < units))
+            def _():
+                advance(unit * 4 + stream, k)
+
+    def exchange(src, dst, send_sems, recv_sems):
+        copies = []
+        for j in range(1, experts):
+            to = lax.rem(ep + j, experts)
+            copies.append(pltpu.make_async_remote_copy(
+                src_ref=src.at[to], dst_ref=dst.at[ep], send_sem=send_sems.at[j - 1], recv_sem=recv_sems.at[j - 1],
+                device_id=(dp, to), device_id_type=MESH))
+        return copies
+
+    def load_hidden(i):
+        slot = lax.rem(i, 2)
+        return pltpu.make_async_copy(hidden_t.at[pl.ds(pl.multiple_of(i * TILE, TILE), TILE)], hbuf.at[slot], load_sem.at[slot])
+
+    def load_rest(i):
+        slot = lax.rem(i, 2)
+        at = pl.ds(pl.multiple_of(i * TILE, TILE), TILE)
+        return (
+            pltpu.make_async_copy(slope.at[i], sbuf.at[slot], load2_sem.at[slot, 0]),
+            pltpu.make_async_copy(w_in.at[:, at], ibuf.at[slot], load2_sem.at[slot, 1]),
+            pltpu.make_async_copy(w_out.at[at], obuf.at[slot], load2_sem.at[slot, 2]),
+        )
+
+    load_hidden(0).start()
+    for copy in load_rest(0):
+        copy.start()
+
+    barrier = pltpu.get_barrier_semaphore()
+    peers = [(z * 4 + wrap(yy + 1), ep), (z * 4 + wrap(yy - 1), ep), (wrap(z + 1) * 4 + yy, ep), (wrap(z - 1) * 4 + yy, ep)]
+    peers += [(dp, lax.rem(ep + j, experts)) for j in range(1, experts)]
+    for peer in peers:
+        pl.semaphore_signal(barrier, inc=1, device_id=peer, device_id_type=MESH)
+    pl.semaphore_wait(barrier, len(peers))
+
+    send_y = exchange(y, back_y, y_send, y_recv)
+    for copy in send_y:
+        copy.start()
+    self_y = pltpu.make_async_copy(y.at[ep], back_y.at[ep], self_sem.at[0])
+    self_y.start()
+    acc[...] = jnp.zeros_like(acc)
+    db_out[...] = jnp.sum(d_rows_in[...].astype(F32), axis=0, keepdims=True)
+
+    def out_tile(i, carry):
+        wave(i // 4, lax.rem(i, 4))
+        slot = lax.rem(i, 2)
+        load_hidden(i).wait()
+
+        @pl.when(i + 1 < half)
+        def _():
+            load_hidden(i + 1).start()
+
+        grad = nn(hbuf[slot], d_rows_in[...])
+        part_sum[i] = grad.reshape(part_sum.shape[1:])
+        send(i, 0).start()
+        return carry
+
+    lax.fori_loop(0, half, out_tile, 0)
+
+    def in_tile(i, carry):
+        g = i + half
+        wave(g // 4, lax.rem(g, 4))
+        slot = lax.rem(i, 2)
+        for copy in load_rest(i):
+            copy.wait()
+
+        @pl.when(i + 1 < half)
+        def _():
+            for copy in load_rest(i + 1):
+                copy.start()
+
+        total = jnp.zeros((1, TILE), F32)
+        for c in range(chunks):
+            part = pl.ds(c * size, size)
+            d_hidden = nt(d_rows_in[part, :], obuf[slot]).astype(BF16)
+            d_act = d_hidden.astype(F32) * sbuf[slot, part, :]
+            total += jnp.sum(d_act, axis=0, keepdims=True)
+            d_act_bf = d_act.astype(BF16)
+            act[part, :] = d_act_bf
+            acc[part, :] += nt(d_act_bf, ibuf[slot])
+        db_in[:, pl.ds(pl.multiple_of(i * TILE, TILE), TILE)] = total
+        rows = width // 4
+        for a in range(4):
+            grad = nn(rows_t[pl.ds(a * rows, rows), :], act[...])
+            for b in range(4):
+                for j in range(3):
+                    at = b * (rows // 4) + j * 16
+                    part_sum[g, a, b, :, j * TILE:(j + 1) * TILE] = grad[at:at + 16, :]
+        send(g, 0).start()
+        return carry
+
+    lax.fori_loop(0, half, in_tile, 0)
+
+    d_out[...] = acc[...].astype(BF16).reshape(d_out.shape)
+    send_d = exchange(d_out, back_d, d_send, d_recv)
+    for copy in send_d:
+        copy.start()
+    self_d = pltpu.make_async_copy(d_out.at[ep], back_d.at[ep], self_sem.at[1])
+    self_d.start()
+
+    def rest(t, carry):
+        def streams(s, inner):
+            wave(t, s)
+            return inner
+
+        return lax.fori_loop(0, 4, streams, carry)
+
+    lax.fori_loop(units, units + 12, rest, 0)
+
+    def drain(tile, carry):
+        for k in range(12):
+            send(tile, k).wait_send()
+        return carry
+
+    lax.fori_loop(0, tiles, drain, 0)
+    for copy in send_y + send_d:
+        copy.wait()
+    self_y.wait()
+    self_d.wait()
+
+
+def unpack_kernel(sum_ref, dw_ref):
+    width = dw_ref.shape[0]
+    rows = width // 4
+    for a in range(4):
+        for b in range(4):
+            for j in range(3):
+                at = a * rows + b * (rows // 4) + j * 16
+                dw_ref[at:at + 16, :] = sum_ref[0, a, b, :, j * TILE:(j + 1) * TILE]
 
 
 def global_terms(stats, experts):
@@ -343,43 +524,66 @@
         whole = pl.BlockSpec((n, width), lambda i: (0, 0))
         w_in_spec = pl.BlockSpec((width, tile), lambda i: (0, i))
         w_out_spec = pl.BlockSpec((tile, width), lambda i: (i, 0))
-        act_spec = pl.BlockSpec((n, tile), lambda i: (0, i))
         hid_row = pl.BlockSpec((1, tile), lambda i: (0, i))
         width_row = pl.BlockSpec((1, width), lambda i: (0, 0))
         mm = 2 * n * width * hid
 
-        hidden, slope, y = pl.pallas_call(
+        tiles = hid // TILE
+        recv_rows, stats = lax.optimization_barrier((recv_rows, stats))
+        hidden_t, slope, rows_t, y = pl.pallas_call(
             functools.partial(forward_kernel, steps, 4),
             grid=(steps,),
-            out_shape=(shape((n, hid), BF16), shape((n, hid), F32), shape((n, width), BF16)),
+            out_shape=(shape((hid, n), BF16), shape((tiles, n, TILE), F32), shape((width, n), BF16), shape((n, width), BF16)),
             in_specs=[whole, w_in_spec, hid_row, w_out_spec, width_row],
-            out_specs=(act_spec, act_spec, whole),
+            out_specs=(
+                pl.BlockSpec((tile, n), lambda i: (i, 0)),
+                pl.BlockSpec((tile // TILE, n, TILE), lambda i: (i, 0, 0)),
+                pl.BlockSpec((width, n), lambda i: (0, 0)),
+                whole,
+            ),
             scratch_shapes=[pltpu.VMEM((n, width), F32)],
             compiler_params=params(), cost_estimate=cost(2 * mm, 6 * n * hid), name="expert_forward",
         )(recv_rows, w_in, b_in, w_out, b_out)
-        back_y = lax.all_to_all(y.reshape(experts, capacity, width), "ep", 0, 0, tiled=True).reshape(n, width)
-
-        d_w_out = pl.pallas_call(
-            dwout_kernel,
-            grid=(steps,),
-            out_shape=shape((hid, width), F32),
-            in_specs=[act_spec, whole],
-            out_specs=w_out_spec,
-            compiler_params=params(), cost_estimate=cost(mm, 2 * n * hid), name="expert_dwout",
-        )(hidden, d_recv)
-        d_w_out = gather_sum(d_w_out)
-
-        d_w_in, d_b_in, d_b_out, d_rows = pl.pallas_call(
-            functools.partial(backward_kernel, steps, 4),
-            grid=(steps,),
-            out_shape=(shape((width, hid), F32), shape((1, hid), F32), shape((1, width), F32), shape((n, width), BF16)),
-            in_specs=[whole, whole, act_spec, w_in_spec, w_out_spec],
-            out_specs=(w_in_spec, hid_row, width_row, whole),
-            scratch_shapes=[pltpu.VMEM((n, width), F32), pltpu.VMEM((n, tile), BF16)],
-            compiler_params=params(), cost_estimate=cost(3 * mm, 6 * n * hid), name="expert_backward",
-        )(recv_rows, d_recv, slope, w_in, w_out)
-        d_w_in = gather_sum(d_w_in)
-        d_back = lax.all_to_all(d_rows.reshape(experts, capacity, width), "ep", 0, 0, tiled=True).reshape(n, width)
+
+        anywhere = pl.BlockSpec(memory_space=pl.ANY)
+        dma = pltpu.SemaphoreType.DMA
+        slots = (experts, capacity, width)
+        summed, d_b_in, d_b_out, back_y, d_back = pl.pallas_call(
+            grads_kernel,
+            out_shape=(
+                shape((2 * tiles, 4, 4, 16, width), BF16), shape((1, hid), F32), shape((1, width), F32),
+                shape(slots, BF16), shape(slots, BF16),
+            ),
+            in_specs=[anywhere] * 4 + vmem(2) + [anywhere],
+            out_specs=(anywhere, *vmem(2), anywhere, anywhere),
+            scratch_shapes=[
+                pltpu.VMEM((2 * tiles, 4, 4, 16, width), F32),
+                pltpu.VMEM((2 * tiles, 3, 4, 16, width), F32),
+                pltpu.VMEM((2 * tiles, 3, 16, width), F32),
+                pltpu.VMEM((2 * tiles, 16, width), BF16),
+                pltpu.VMEM((2, TILE, n), BF16),
+                pltpu.VMEM((2, n, TILE), F32),
+                pltpu.VMEM((2, width, TILE), BF16),
+                pltpu.VMEM((2, TILE, width), BF16),
+                pltpu.VMEM((n, TILE), BF16),
+                pltpu.VMEM((n, width), F32),
+                pltpu.VMEM(slots, BF16),
+                dma((2 * tiles, 12)), dma((2 * tiles, 12)), dma((2 * tiles,)), dma((2,)), dma((2, 3)),
+                dma((experts - 1,)), dma((experts - 1,)), dma((experts - 1,)), dma((experts - 1,)), dma((2,)),
+            ],
+            compiler_params=pltpu.CompilerParams(collective_id=3, has_side_effects=True, vmem_limit_bytes=67_000_000),
+            cost_estimate=cost(4 * mm, 6 * n * hid), name="expert_grads",
+        )(hidden_t, slope, w_in, w_out, rows_t, d_recv, y.reshape(slots))
+        back_y, d_back = back_y.reshape(n, width), d_back.reshape(n, width)
+        d_w_out = summed[:tiles].reshape(hid, width)
+        d_w_in = pl.pallas_call(
+            unpack_kernel,
+            grid=(tiles,),
+            out_shape=shape((width, hid), BF16),
+            in_specs=[pl.BlockSpec((1, 4, 4, 16, width), lambda i: (i + tiles, 0, 0, 0, 0))],
+            out_specs=pl.BlockSpec((width, TILE), lambda i: (0, i)),
+            name="unpack",
+        )(summed)
 
         out, d_log, d_router_part, loss = pl.pallas_call(
             functools.partial(combine_kernel, capacity, 4),
@@ -401,10 +605,6 @@
         d_b_in = small[experts:experts + hid // width].reshape(1, hid).astype(BF16)
         d_b_out = small[experts + hid // width:experts + hid // width + 1].astype(BF16)
         return out, loss[0, 0], d_x, d_router, d_w_in[None], d_b_in, d_w_out[None], d_b_out
-
-    def gather_sum(part):
-        own = lax.psum_scatter(part, "dp", scatter_dimension=0, tiled=True)
-        return lax.all_gather(own.astype(BF16), "dp", axis=0, tiled=True)
 
     def split3_outside(a):
         hi = lax.reduce_precision(a, 8, 7)

time: 445 us -> 363 us (0.82)
  waiting for transfers between devices: 184 us -> 18.6 us
  Pallas kernels: 174 us -> 314 us
  blocking collectives: 34.2 us -> 0 us
  between operations: 13.9 us -> 0.72 us
    reduce_scatter x2 -> x0, waiting for transfers between devices: 164 us -> none  [gather_sum(): own = lax.psum_scatter(part, 'dp', scatter_dimension=0, tiled=True)]
    pallas_call x2, Pallas kernels: 45.3 us -> 181 us  [the longest x1 172 us: local_step(): pl.pallas_call(grads_kernel, out_shape=(shape((2 * tiles, 4, 4, 16, width...]
    all_to_all x1 -> x0, blocking collectives: 34.2 us -> none  [local_step(): lax.all_to_all(y.reshape(experts, capacity, width), 'ep', 0, 0, tiled=True)]
    unnamed x20 -> x10, local copies, waits for them, and re-layouts: 10.7 us -> 2.03 us
    slice x0 -> x1, local copies, waits for them, and re-layouts: none -> 5.06 us  [local_step(): d_w_out = summed[:tiles].reshape(hid, width)]
  transfers between devices with their start and end apart: 7 -> 2, of which waited for: 4 -> 1; matrix products, arithmetic and copies ran while one was open for 3% -> 0% of each run, Pallas kernels for 30% -> 23%
where the time goes in v2:
time: 363 us; the launch traced here: 361 us
  Pallas kernels  314 us (87%)
  waiting for transfers between devices  18.6 us (5%)
  local copies, waits for them, and re-layouts  14 us (4%)
  starting transfers between devices  9.14 us (3%)
  other arithmetic  4.25 us (1%)
    pallas_call x1, Pallas kernels, local_step(): pl.pallas_call(grads_kernel, out_shape=(shape((2 * tiles, 4, 4, 16, width...  172 us
    pallas_call x2, Pallas kernels, small_reduce(): pl.pallas_call(functools.partial(reduce_kernel, whole_rows), out_shape=ja...  63 us
    pallas_call x1, Pallas kernels, local_step(): pl.pallas_call(functools.partial(forward_kernel, steps, 4), grid=(steps,)...  30.4 us
    all_to_all x1, waiting for transfers between devices, local_step(): lax.all_to_all(send_rows, 'ep', 0, 0, tiled=True).reshape(n, width)  18.6 us
    pallas_call x1, Pallas kernels, local_step(): pl.pallas_call(functools.partial(route_kernel, capacity), out_shape=(shap...  11 us
    pallas_call x1, Pallas kernels, local_step(): pl.pallas_call(functools.partial(combine_kernel, capacity, 4), out_shape=...  10.9 us
    pallas_call x1, Pallas kernels, local_step(): pl.pallas_call(functools.partial(router_kernel, capacity), out_shape=(sha...  10.2 us
    pallas_call x1, Pallas kernels, local_step(): pl.pallas_call(unpack_kernel, grid=(tiles,), out_shape=shape((width, hid)...  8.52 us
  transfers between devices with their start and end apart: 2, of which 1 were waited for; matrix products, arithmetic and copies ran while one was open for 0% of the time, Pallas kernels for 23%

profile of v2, /device:TPU:0, one launch (start us, length us, event | category | flops | bytes accessed | tf_op | source)
XLA Modules:
  0.0 361.1 jit_solution(12194350823467957178)
XLA Ops:
  0.6 1.3 reshape.57.ids_ref
  1.9 1.3 reshape.59.prio_ref
  3.2 11.0 %route.1 = (f32[8,1536]{1,0:T(8,128)}, bf16[8,192,768]{2,1,0:T(8,128)(2,1)}) custom-call(s32[1,1536]{1,0:T(1,128)} %reshape.57.ids_ref, s32[1,1536]{1,0:T(1,128)} %reshape.59.prio_ref, bf16[1536,768]{1,0:T(8,128)(2,1)} %x_ref.5), custom_call_target="tpu_custom_call" | custom-call | flops 3623878656 | bytes 4718592 | tf_op jit(solution)/shard_map/route/pallas_call | solution.py:503
  14.3 0.0 copy-start.2
  14.3 0.0 copy-start.1
  14.3 4.6 %all-to-all-start = ((bf16[8,192,768]{2,1,0:T(8,128)(2,1)}), bf16[8,192,768]{2,1,0:T(8,128)(2,1)S(1)}, u32[]{:S(2)}, u32[]{:S(2)}) async-start(bf16[8,192,768]{2,1,0:T(8,128)(2,1)} %get-tuple-element.30), calls=%async_computation | async-start | bytes 4718592 | tf_op jit(solution)/shard_map/all_to_all | solution.py:510
  18.8 0.0 copy-done.2
  18.8 0.6 reshape.58.mod_ref
  19.4 0.0 copy-done.1
  19.4 0.6 pad_maximum_fusion.router3_ref
  20.1 10.2 %router.1 = (f32[8,1536]{1,0:T(8,128)}, f32[48,128]{1,0:T(8,128)}, bf16[8,192,768]{2,1,0:T(8,128)(2,1)}) custom-call(s32[1,1536]{1,0:T(1,128)} %reshape.57.ids_ref, s32[1,1536]{1,0:T(1,128)} %reshape.58.mod_ref, f32[8,1536]{1,0:T(8,128)} %get-tuple-element.28.slot_ref, bf16[1536,768]{1,0:T(8,128)(2,1)} %x_ref.5, bf16[1536,768]{1,0:T(8,128)(2,1)} %dy_ref.3, ...), custom_call_target="tpu_custom_call" | custom-call | flops 3623878656 | bytes 7077888 | tf_op jit(solution)/shard_map/router/pallas_call | solution.py:512
  30.3 18.6 %all-to-all-done = bf16[8,192,768]{2,1,0:T(8,128)(2,1)S(1)} async-done(((bf16[8,192,768]{2,1,0:T(8,128)(2,1)}), bf16[8,192,768]{2,1,0:T(8,128)(2,1)S(1)}, u32[]{:S(2)}, u32[]{:S(2)}) %all-to-all-start) | async-done | bytes 2359328 | tf_op jit(solution)/shard_map/all_to_all | solution.py:510
  48.8 0.0 copy-start
  48.8 1.4 copy-done
  50.2 4.6 %all-to-all-start.1 = ((bf16[8,192,768]{2,1,0:T(8,128)(2,1)}), bf16[8,192,768]{2,1,0:T(8,128)(2,1)}, u32[]{:S(2)}, u32[]{:S(2)}) async-start(bf16[8,192,768]{2,1,0:T(8,128)(2,1)} %get-tuple-element.36), calls=%async_computation.1 | async-start | bytes 4718592 | tf_op jit(solution)/shard_map/all_to_all | solution.py:519
  54.8 0.1 pad.3.clone
  54.9 42.7 %small_reduce_1.1.stats_ref = f32[48,128]{1,0:T(8,128)} custom-call(f32[48,128]{1,0:T(8,128)} %get-tuple-element.31.a_ref), custom_call_target="tpu_custom_call" | custom-call | flops 2000000000 | bytes 100000 | tf_op jit(solution)/shard_map/small_reduce_1/pallas_call | solution.py:454
  97.6 30.4 %expert_forward.1 = (bf16[3072,1536]{1,0:T(8,128)(2,1)}, f32[12,1536,256]{2,1,0:T(8,128)}, bf16[768,1536]{1,0:T(8,128)(2,1)}, bf16[1536,768]{1,0:T(8,128)(2,1)}) custom-call(bf16[1536,768]{1,0:T(8,128)(2,1)} %bitcast.22, bf16[768,3072]{1,0:T(8,128)(2,1)} %bitcast.25, bf16[1,3072]{1,0:T(2,128)(2,1)} %b_in_ref.1, bf16[3072,768]{1,0:T(8,128)(2,1)} %bitcast.27, ...), custom_call_target="tpu_custom_call" | custom-call | flops 14495514624 | bytes 28311552 | tf_op jit(solution)/shard_map/expert_forward/pallas_call | solution.py:533
  128.0 0.0 all-to-all-done.1
  128.0 172.5 %expert_grads.1 = (bf16[24,4,4,16,768]{4,3,2,1,0:T(8,128)(2,1)}, f32[1,3072]{1,0:T(1,128)}, f32[1,768]{1,0:T(1,128)}, bf16[8,192,768]{2,1,0:T(8,128)(2,1)}, bf16[8,192,768]{2,1,0:T(8,128)(2,1)}) custom-call(bf16[3072,1536]{1,0:T(8,128)(2,1)} %get-tuple-element.33.hidden_t, f32[12,1536,256]{2,1,0:T(8,128)} %get-tuple-element.34.slope, ...), custom_call_target="tpu_custom_call" | custom-call | flops 28991029248 | bytes 28311552 | tf_op jit(solution)/shard_map/expert_grads/pallas_call | solution.py:551
  300.5 0.5 broadcast.5
  301.0 1.4 reduce.3
  302.4 0.0 copy-start.3
  302.5 10.9 %combine.1 = (bf16[1536,768]{1,0:T(8,128)(2,1)}, f32[8,1536]{1,0:T(8,128)}, f32[8,768]{1,0:T(8,128)}, f32[8,128]{1,0:T(8,128)}) custom-call(s32[1,1536]{1,0:T(1,128)} %reshape.57.ids_ref, s32[1,1536]{1,0:T(1,128)} %reshape.58.mod_ref, f32[8,1536]{1,0:T(8,128)} %get-tuple-element.28.slot_ref, f32[8,1536]{1,0:T(8,128)} %get-tuple-element.29.logp_ref, ...), custom_call_target="tpu_custom_call" | custom-call | flops 3623878656 | bytes 9437184 | tf_op jit(solution)/shard_map/combine/pallas_call | solution.py:588
  313.3 0.0 copy-done.3
  313.3 1.4 maximum_maximum_fusion.a_ref
  314.8 20.3 %small_reduce_2.1 = f32[16,768]{1,0:T(8,128)} custom-call(f32[16,768]{1,0:T(8,128)} %maximum_maximum_fusion.a_ref), custom_call_target="tpu_custom_call" | custom-call | flops 2000000000 | bytes 100000 | tf_op jit(solution)/shard_map/small_reduce_2/pallas_call | solution.py:454
  335.1 1.3 slice_bitcast_fusion
  336.5 0.8 convert.4
  337.3 8.5 %unpack.1 = bf16[768,3072]{1,0:T(8,128)(2,1)} custom-call(bf16[24,4,4,16,768]{4,3,2,1,0:T(8,128)(2,1)} %get-tuple-element.47.sum_ref), custom_call_target="tpu_custom_call" | custom-call | tf_op jit(solution)/shard_map/unpack/pallas_call | solution.py:579
  345.8 5.1 %slice.20 = bf16[12,4,4,16,768]{4,3,2,1,0:T(8,128)(2,1)} slice(bf16[24,4,4,16,768]{4,3,2,1,0:T(8,128)(2,1)} %get-tuple-element.47.sum_ref), slice={[0:12], [0:4], [0:4], [0:16], [0:768]} | slice | bytes 9437184 | tf_op jit(solution)/shard_map/slice | solution.py:578
  350.9 0.6 slice.23
  351.4 1.2 slice.17
  352.6 0.6 copy.18
  353.2 7.9 %token_grad.1 = bf16[1536,768]{1,0:T(8,128)(2,1)} custom-call(f32[8,1536]{1,0:T(8,128)} %get-tuple-element.28.slot_ref, f32[8,1536]{1,0:T(8,128)} %get-tuple-element.42.dlog_ref, bf16[1536,768]{1,0:T(8,128)(2,1)} %bitcast.29, f32[8,768]{1,0:T(8,128)} %bitcast.23), custom_call_target="tpu_custom_call" | custom-call | flops 3623878656 | bytes 7077888 | tf_op jit(solution)/shard_map/token_grad/pallas_call | solution.py:595
  (4 shorter events, 0.0 us)
Async XLA Ops:
  14.3 4.6 %copy-start.2 = (s32[1536]{0:T(1024)S(1)}, s32[1536]{0:T(1024)}, u32[]{:S(2)}) copy-start(s32[1536]{0:T(1024)} %param.11) | copy-start | bytes 18436
  14.3 5.2 %copy-start.1 = (f32[768,8]{0,1:T(8,128)S(1)}, f32[768,8]{0,1:T(8,128)}, u32[]{:S(2)}) copy-start(f32[768,8]{0,1:T(8,128)} %param.12) | copy-start | bytes 73732
  14.3 34.6 %all-to-all-start = ((bf16[8,192,768]{2,1,0:T(8,128)(2,1)}), bf16[8,192,768]{2,1,0:T(8,128)(2,1)S(1)}, u32[]{:S(2)}, u32[]{:S(2)}) async-start(bf16[8,192,768]{2,1,0:T(8,128)(2,1)} %get-tuple-element.30), calls=%async_computation | async-start | bytes 4718592 | tf_op jit(solution)/shard_map/all_to_all | solution.py:510
  48.8 1.4 copy-start
  50.2 77.8 %all-to-all-start.1 = ((bf16[8,192,768]{2,1,0:T(8,128)(2,1)}), bf16[8,192,768]{2,1,0:T(8,128)(2,1)}, u32[]{:S(2)}, u32[]{:S(2)}) async-start(bf16[8,192,768]{2,1,0:T(8,128)(2,1)} %get-tuple-element.36), calls=%async_computation.1 | async-start | bytes 4718592 | tf_op jit(solution)/shard_map/all_to_all | solution.py:519
  302.4 10.9 %copy-start.3 = (f32[1,768]{1,0:T(1,128)S(1)}, f32[1,768]{1,0:T(1,128)}, u32[]{:S(2)}) copy-start(f32[1,768]{1,0:T(1,128)} %get-tuple-element.46) | copy-start | bytes 9220

commit v3 on v2

v3 whole, which is shorter than its diff:
```python
import functools

import jax
import jax.numpy as jnp
from jax import lax
from jax.experimental import pallas as pl
from jax.experimental.pallas import tpu as pltpu
from jax.sharding import PartitionSpec as P

ALL_AXES = ("dp", "ep")
MESH = pl.DeviceIdType.MESH
F32 = jnp.float32
BF16 = jnp.bfloat16
NOWHERE = -1.0
TILE = 256
CHUNK = 256


def col_of(row):
    return jnp.transpose(jnp.broadcast_to(row, (8, row.shape[1])))


def row_of(col):
    return jnp.transpose(jnp.broadcast_to(col, (col.shape[0], 8)))


def split3(a):
    hi = a.astype(BF16)
    rest = a - hi.astype(F32)
    mid = rest.astype(BF16)
    lo = (rest - mid.astype(F32)).astype(BF16)
    return hi, mid, lo


def nt(a, b):
    return lax.dot_general(a, b, (((1,), (1,)), ((), ())), preferred_element_type=F32)


def tn(a, b):
    return lax.dot_general(a, b, (((0,), (0,)), ((), ())), preferred_element_type=F32)


def nn(a, b):
    return jnp.dot(a, b, preferred_element_type=F32)


def wide(ref):
    v = ref[...].astype(F32)
    return jnp.concatenate([v[i:i + 1, :] for i in range(v.shape[0])], axis=1)


def greet(peers):
    barrier = pltpu.get_barrier_semaphore()
    for peer in peers:
        pl.semaphore_signal(barrier, inc=1, device_id=peer, device_id_type=MESH)
    return lambda: pl.semaphore_wait(barrier, len(peers))


def dispatch_kernel(
    ids_ref, prio_ref, mod_ref, x_ref, dy_ref, router3_ref, w_in, b_in_ref, w_out, b_out_ref,
    ids_row_ref, mod_row_ref, slot_ref, logp_ref, stats_ref, hidden_t, slope, rows_t_ref, y_ref, d_rows,
    keycol, dyt, out_x, out_d, rows, acc, ibuf, obuf, hbuf, sbuf,
    x_send, x_recv, d_send, d_recv, self_sem, load_sem, store_sem,
):
    dp = lax.axis_index("dp")
    ep = lax.axis_index("ep")
    x, core = ep // 2, lax.rem(ep, 2)
    experts, capacity, width = out_x.shape
    n = experts * capacity
    hid = hidden_t.shape[0]
    tiles = hid // TILE
    chunks = 4
    size = n // chunks

    enter = greet([(dp, lax.rem(ep + j, experts)) for j in range(1, experts)])

    def loads(i):
        slot = lax.rem(i, 2)
        at = pl.ds(pl.multiple_of(i * TILE, TILE), TILE)
        return (
            pltpu.make_async_copy(w_in.at[:, at], ibuf.at[slot], load_sem.at[slot, 0]),
            pltpu.make_async_copy(w_out.at[at], obuf.at[slot], load_sem.at[slot, 1]),
        )

    def stores(i):
        slot = lax.rem(i, 2)
        at = pl.ds(pl.multiple_of(i * TILE, TILE), TILE)
        return (
            pltpu.make_async_copy(hbuf.at[slot], hidden_t.at[at], store_sem.at[slot, 0]),
            pltpu.make_async_copy(sbuf.at[slot], slope.at[i], store_sem.at[slot, 1]),
        )

    for copy in loads(0):
        copy.start()

    ids = wide(ids_ref)
    key = ids * n + wide(prio_ref)
    low = ids * n
    keycol[...] = col_of(key)

    def count(j, total):
        col = keycol[pl.ds(pl.multiple_of(j * 128, 128), 128), :][:, 0:1]
        before = jnp.logical_and(col < key, col >= low)
        return total + jnp.sum(before.astype(F32), axis=0, keepdims=True)

    position = lax.fori_loop(0, n // 128, count, jnp.zeros((1, n), F32))
    slot_row = jnp.where(position < capacity, ids * capacity + position, NOWHERE)
    slot_ref[...] = jnp.broadcast_to(slot_row, slot_ref.shape)
    mod_row = wide(mod_ref)
    ids_row_ref[...] = jnp.broadcast_to(ids, ids_row_ref.shape)
    mod_row_ref[...] = jnp.broadcast_to(mod_row, mod_row_ref.shape)

    def target(j):
        return lax.rem(x + j // 2 + 1, 4) * 2 + lax.rem(core + 1 - lax.rem(j, 2), 2)

    def pick(e):
        index = (lax.broadcasted_iota(jnp.int32, (capacity, n), 0) + e * capacity).astype(F32)
        return (index == slot_ref[0:1, :]).astype(BF16)

    def send(j, src, dst, send_sems, recv_sems):
        to = target(j)
        return pltpu.make_async_remote_copy(
            src_ref=src.at[to], dst_ref=dst.at[ep], send_sem=send_sems.at[j], recv_sem=recv_sems.at[j],
            device_id=(dp, to), device_id_type=MESH)

    enter()

    def send_x(j, carry):
        out_x[target(j)] = nn(pick(target(j)), x_ref[...]).astype(BF16)
        send(j, out_x, rows, x_send, x_recv).start()
        return carry

    lax.fori_loop(0, experts - 1, send_x, 0)
    rows[ep] = nn(pick(ep), x_ref[...]).astype(BF16)

    logits3 = nt(router3_ref[...], x_ref[...])
    logits = logits3[0:experts] + logits3[experts:2 * experts] + logits3[2 * experts:3 * experts]
    shifted = logits - jnp.max(logits, axis=0, keepdims=True)
    logp = shifted - jnp.log(jnp.sum(jnp.exp(shifted), axis=0, keepdims=True))
    logp_ref[...] = logp
    probs = jnp.exp(logp)
    onehot = (lax.broadcasted_iota(jnp.int32, (experts, n), 0).astype(F32) == ids).astype(F32)
    gate = jnp.sum(probs * onehot, axis=0, keepdims=True)
    dyt[...] = (col_of(gate)[:, 0:1] * dy_ref[...].astype(F32)).astype(BF16)

    def send_cotangent(j, carry):
        out_d[target(j)] = nn(pick(target(j)), dyt[...]).astype(BF16)
        send(j, out_d, d_rows, d_send, d_recv).start()
        return carry

    lax.fori_loop(0, experts - 1, send_cotangent, 0)
    out_d[ep] = nn(pick(ep), dyt[...]).astype(BF16)
    keep_d = pltpu.make_async_copy(out_d.at[ep], d_rows.at[ep], self_sem)
    keep_d.start()

    entropy = -jnp.sum(probs * logp, axis=0, keepdims=True)
    for m in range(2):
        mask = (mod_row == m).astype(F32)
        stats_ref[24 * m:24 * m + 8, :] = jnp.broadcast_to(jnp.sum(probs * mask, axis=1, keepdims=True), (8, 128))
        stats_ref[24 * m + 8:24 * m + 16, :] = jnp.broadcast_to(jnp.sum(entropy * mask, axis=1, keepdims=True), (8, 128))
        stats_ref[24 * m + 16:24 * m + 24, :] = jnp.broadcast_to(jnp.sum(mask, axis=1, keepdims=True), (8, 128))
    acc[...] = jnp.broadcast_to(b_out_ref[...].astype(F32), acc.shape)

    def arrive(j, carry):
        send(j, out_x, rows, x_send, x_recv).wait_recv()
        return carry

    lax.fori_loop(0, experts - 1, arrive, 0)

    def tile(i, carry):
        slot = lax.rem(i, 2)
        for copy in loads(i):
            copy.wait()

        @pl.when(i + 1 < tiles)
        def _():
            for copy in loads(i + 1):
                copy.start()

        @pl.when(i >= 2)
        def _():
            for copy in stores(i - 2):
                copy.wait()

        bias = b_in_ref[:, pl.ds(pl.multiple_of(i * TILE, TILE), TILE)].astype(F32)
        for c in range(chunks):
            part = pl.ds(c * size, size)
            part_rows = rows[c * (experts // chunks):(c + 1) * (experts // chunks)].reshape(size, width)
            a = nn(part_rows, ibuf[slot]) + bias
            root = 0.7978845608028654
            sq = a * a
            t = jnp.tanh(root * (a + 0.044715 * (sq * a)))
            half = 0.5 * (1.0 + t)
            hidden = (a * half).astype(BF16)
            sbuf[slot, part, :] = half + (0.5 * root) * a * (1.0 - t * t) * (1.0 + (3 * 0.044715) * sq)
            hbuf[slot, :, part] = jnp.transpose(hidden)
            acc[part, :] += nn(hidden, obuf[slot])
        for copy in stores(i):
            copy.start()
        return carry

    lax.fori_loop(0, tiles, tile, 0)
    rows_t_ref[...] = jnp.transpose(rows[...].reshape(n, width))
    y_ref[...] = acc[...].astype(BF16).reshape(y_ref.shape)
    for i in (tiles - 2, tiles - 1):
        for copy in stores(jnp.int32(i)):
            copy.wait()
    keep_d.wait()

    def finish(j, carry):
        send(j, out_x, rows, x_send, x_recv).wait_send()
        send(j, out_d, d_rows, d_send, d_recv).wait()
        return carry

    lax.fori_loop(0, experts - 1, finish, 0)


def grads_kernel(
    hidden_t, slope, w_in, w_out, rows_t_in, d_in, y, x, dy, ids_row, mod_row, slot_row, logp_ref, stats_in,
    summed, back_y, back_d, out, d_log_ref, loss_ref, small_ref,
    part_sum, land_a, land_b, own, hbuf, sbuf, ibuf, obuf, act, acc, d_out, rows_t, tok, db_in, stage, stats_ref, d_router,
    stat_work, stat_bufs, small_work, small_bufs,
    send_sem, recv_sem, own_sem, load_sem, load2_sem, y_send, y_recv, d_send, d_recv, self_sem, tok_sem, out_sem,
    stat_send, stat_recv, small_send, small_recv,
):
    dp = lax.axis_index("dp")
    ep = lax.axis_index("ep")
    z, yy = dp // 4, lax.rem(dp, 4)
    tiles = part_sum.shape[0]
    units = tiles // 4
    half = tiles // 2
    experts = y.shape[0]
    n, width = acc.shape
    chunks = 4
    size = n // chunks

    def place(stream):
        way = 1 - 2 * lax.rem(stream, 2)
        first_z = stream // 2
        pa = yy * (1 - first_z) + z * first_z
        pb = z * (1 - first_z) + yy * first_z
        y_next, z_next = lax.rem(yy + way + 4, 4), lax.rem(z + way + 4, 4)
        along_y, along_z = z * 4 + y_next, z_next * 4 + yy
        next_a = along_y * (1 - first_z) + along_z * first_z
        next_b = along_z * (1 - first_z) + along_y * first_z
        return way, pa, pb, next_a, next_b

    def wrap(v):
        return lax.rem(v + 16, 4)

    def send(tile, k):
        way, pa, pb, next_a, next_b = place(lax.rem(tile, 4))
        if k < 3:
            src, dst, to = part_sum.at[tile, wrap(pa - way * (k + 1))], land_a.at[tile, k], next_a
        elif k < 6:
            src, dst, to = part_sum.at[tile, pa, wrap(pb - way * (k - 2))], land_b.at[tile, k - 3], next_b
        elif k == 6:
            src, dst, to = own.at[tile], summed.at[tile, pa, pb], next_b
        elif k < 9:
            src = summed.at[tile, pa, wrap(pb - way * (k - 6))]
            dst, to = src, next_b
        else:
            src = summed.at[tile, wrap(pa - way * (k - 9))]
            dst, to = src, next_a
        return pltpu.make_async_remote_copy(
            src_ref=src, dst_ref=dst, send_sem=send_sem.at[tile, k], recv_sem=recv_sem.at[tile, k],
            device_id=(to, ep), device_id_type=MESH)

    def keep(tile):
        way, pa, pb, _, _ = place(lax.rem(tile, 4))
        return pltpu.make_async_copy(own.at[tile], summed.at[tile, pa, pb], own_sem.at[tile])

    def advance(tile, k):
        way, pa, pb, _, _ = place(lax.rem(tile, 4))
        send(tile, k - 1).wait_recv()
        if k <= 3:
            block = wrap(pa - way * (k + 1))
            part_sum[tile, block] = part_sum[tile, block] + land_a[tile, k - 1]
        elif k <= 6:
            block = wrap(pb - way * (k - 2))
            total = part_sum[tile, pa, block] + land_b[tile, k - 4]
            if k < 6:
                part_sum[tile, pa, block] = total
            else:
                own[tile] = total.astype(BF16)
                keep(tile).start()
        elif k == 9:
            keep(tile).wait()
        if k < 12:
            send(tile, k).start()

    def wave(t, stream):
        for k in range(12, 0, -1):
            unit = t - k

            @pl.when(jnp.logical_and(unit >= 0, unit < units))
            def _():
                advance(unit * 4 + stream, k)

    def exchange(src, dst, send_sems, recv_sems):
        copies = []
        for j in range(1, experts):
            to = lax.rem(ep + j, experts)
            copies.append(pltpu.make_async_remote_copy(
                src_ref=src.at[to], dst_ref=dst.at[ep], send_sem=send_sems.at[j - 1], recv_sem=recv_sems.at[j - 1],
                device_id=(dp, to), device_id_type=MESH))
        return copies

    def load_hidden(i):
        slot = lax.rem(i, 2)
        return pltpu.make_async_copy(hidden_t.at[pl.ds(pl.multiple_of(i * TILE, TILE), TILE)], hbuf.at[slot], load_sem.at[slot])

    def load_rest(i):
        slot = lax.rem(i, 2)
        at = pl.ds(pl.multiple_of(i * TILE, TILE), TILE)
        return (
            pltpu.make_async_copy(slope.at[i], sbuf.at[slot], load2_sem.at[slot, 0]),
            pltpu.make_async_copy(w_in.at[:, at], ibuf.at[slot], load2_sem.at[slot, 1]),
            pltpu.make_async_copy(w_out.at[at], obuf.at[slot], load2_sem.at[slot, 2]),
        )

    load_hidden(0).start()
    for copy in load_rest(0):
        copy.start()

    load_rows = pltpu.make_async_copy(rows_t_in, rows_t, tok_sem.at[0])
    load_d = pltpu.make_async_copy(d_in, tok, tok_sem.at[1])
    load_rows.start()
    load_d.start()
    peers = [(z * 4 + wrap(yy + j), ep) for j in range(1, 4)] + [(wrap(z + j) * 4 + yy, ep) for j in range(1, 4)]
    peers += [(dp, lax.rem(ep + j, experts)) for j in range(1, experts)]
    greet(peers)()

    rings = (
        (ep // 2, [(dp, lax.rem(ep + 2 * j, experts)) for j in range(1, 4)]),
        (yy, peers[0:3]),
        (z, peers[3:6]),
    )
    partner = (dp, (ep // 2) * 2 + 1 - lax.rem(ep, 2))

    def small_sum(work, bufs, whole_rows, send_sems, recv_sems):
        rows = work.shape[1]
        head = pl.ds(0, whole_rows)

        def pair():
            return pltpu.make_async_remote_copy(
                src_ref=work.at[0, head], dst_ref=bufs.at[3, 0, head], send_sem=send_sems.at[3, 0], recv_sem=recv_sems.at[3, 0],
                device_id=partner, device_id_type=MESH)

        def ring(axis):
            me, others = rings[axis]
            at = head if axis == 0 else pl.ds(0, rows)
            return [
                pltpu.make_async_remote_copy(
                    src_ref=work.at[axis + 1, at], dst_ref=bufs.at[axis, me, at], send_sem=send_sems.at[axis, j],
                    recv_sem=recv_sems.at[axis, j], device_id=others[j], device_id_type=MESH)
                for j in range(3)
            ]

        def launch(axis):
            bufs[axis, rings[axis][0]] = work[axis + 1]
            for copy in ring(axis):
                copy.start()

        def total(axis, at):
            for copy in ring(axis):
                copy.wait()
            return bufs[axis, 0, at, :] + bufs[axis, 1, at, :] + bufs[axis, 2, at, :] + bufs[axis, 3, at, :]

        def step(k):
            if k == 0:
                pair().start()
            elif k == 1:
                pair().wait()
                work[1] = work[0]
                work[1, head, :] = work[0, head, :] + bufs[3, 0, head, :]
                launch(0)
            elif k < 4:
                at = head if k == 2 else pl.ds(0, rows)
                summed_rows = total(k - 2, at)
                work[k] = work[k - 1]
                work[k, at, :] = summed_rows
                launch(k - 1)
            else:
                return total(2, pl.ds(0, rows))

        return step

    stat_step = small_sum(stat_work, stat_bufs, 48, stat_send, stat_recv)
    small_step = small_sum(small_work, small_bufs, experts, small_send, small_recv)
    stat_work[0] = stats_in[...]
    stat_step(0)

    send_y = exchange(y, back_y, y_send, y_recv)
    for copy in send_y:
        copy.start()
    self_y = pltpu.make_async_copy(y.at[ep], back_y.at[ep], self_sem.at[0])
    self_y.start()
    acc[...] = jnp.zeros_like(acc)
    small_work[0] = jnp.zeros(small_work.shape[1:], F32)
    load_d.wait()

    def out_tile(i, carry):
        wave(i // 4, lax.rem(i, 4))
        slot = lax.rem(i, 2)
        load_hidden(i).wait()

        @pl.when(i + 1 < half)
        def _():
            load_hidden(i + 1).start()

        grad = nn(hbuf[slot], tok[...])
        part_sum[i] = grad.reshape(part_sum.shape[1:])
        send(i, 0).start()
        for k in (1, 2):
            @pl.when(i == 4 * k)
            def _():
                stat_step(k)

        return carry

    lax.fori_loop(0, half, out_tile, 0)

    def in_tile(i, carry):
        g = i + half
        wave(g // 4, lax.rem(g, 4))
        slot = lax.rem(i, 2)
        for copy in load_rest(i):
            copy.wait()

        @pl.when(i + 1 < half)
        def _():
            for copy in load_rest(i + 1):
                copy.start()

        total = jnp.zeros((1, TILE), F32)
        for c in range(chunks):
            part = pl.ds(c * size, size)
            d_hidden = nt(tok[part, :], obuf[slot]).astype(BF16)
            d_act = d_hidden.astype(F32) * sbuf[slot, part, :]
            total += jnp.sum(d_act, axis=0, keepdims=True)
            d_act_bf = d_act.astype(BF16)
            act[part, :] = d_act_bf
            acc[part, :] += nt(d_act_bf, ibuf[slot])
        db_in[:, pl.ds(pl.multiple_of(i * TILE, TILE), TILE)] = total
        rows = width // 4
        for a in range(4):
            grad = nn(rows_t[pl.ds(a * rows, rows), :], act[...])
            for b in range(4):
                for j in range(3):
                    at = b * (rows // 4) + j * 16
                    part_sum[g, a, b, :, j * TILE:(j + 1) * TILE] = grad[at:at + 16, :]
        send(g, 0).start()

        @pl.when(i == 0)
        def _():
            stat_step(3)

        @pl.when(i == 4)
        def _():
            stats_ref[...] = stat_step(4)

        return carry

    small_work[0, 12:13, :] = jnp.sum(tok[...].astype(F32), axis=0, keepdims=True)
    load_rows.wait()
    lax.fori_loop(0, half, in_tile, 0)

    d_out[...] = acc[...].astype(BF16).reshape(d_out.shape)
    send_d = exchange(d_out, back_d, d_send, d_recv)
    for copy in send_d:
        copy.start()
    self_d = pltpu.make_async_copy(d_out.at[ep], back_d.at[ep], self_sem.at[1])
    self_d.start()

    for copy in send_y:
        copy.wait_recv()
    self_y.wait()
    back = pltpu.make_async_copy(back_y, tok.reshape(back_y.shape), tok_sem.at[1])
    back.start()
    for i in range(4):
        small_work[0, 8 + i:9 + i, :] = db_in[:, i * width:(i + 1) * width]
    d_router[...] = jnp.zeros_like(d_router)
    loss, terms, inv = global_terms(stats_ref[...], experts)
    loss_ref[...] = jnp.broadcast_to(loss, loss_ref.shape)

    def token_loads(i):
        at = pl.ds(pl.multiple_of(i * CHUNK, CHUNK), CHUNK)
        return (
            pltpu.make_async_copy(dy.at[at], obuf.at[0], load2_sem.at[0, 2]),
            pltpu.make_async_copy(x.at[at], obuf.at[1], load2_sem.at[1, 2]),
        )

    def out_store(i):
        at = pl.ds(pl.multiple_of(i * CHUNK, CHUNK), CHUNK)
        return pltpu.make_async_copy(stage, out.at[at], out_sem)

    for copy in token_loads(jnp.int32(0)):
        copy.start()
    back.wait()
    pieces = n // CHUNK

    def combine(i):
        lanes = pl.ds(pl.multiple_of(i * CHUNK, CHUNK), CHUNK)
        slot_col = col_of(slot_row[0:1, lanes])[:, 0:1]
        pick = (lax.broadcasted_iota(jnp.int32, (CHUNK, n), 1).astype(F32) == slot_col).astype(BF16)
        y_tok = nn(pick, tok[...])
        logp = logp_ref[:, lanes]
        probs = jnp.exp(logp)
        onehot = (lax.broadcasted_iota(jnp.int32, (experts, CHUNK), 0).astype(F32) == ids_row[:, lanes]).astype(F32)
        gate = jnp.sum(probs * onehot, axis=0, keepdims=True)
        for copy in token_loads(i):
            copy.wait()

        @pl.when(i > 0)
        def _():
            out_store(i - 1).wait()

        stage[...] = (col_of(gate)[:, 0:1] * y_tok).astype(BF16)
        out_store(i).start()
        d_gate = row_of(jnp.sum(obuf[0].astype(F32) * y_tok, axis=1, keepdims=True))[0:1]
        is_text = mod_row[:, lanes] == 1.0
        global_part = jnp.where(is_text, terms[1][:, 0:1], terms[0][:, 0:1])
        inv_count = jnp.where(is_text, inv[1][:, 0:1], inv[0][:, 0:1])
        d_probs = onehot * d_gate + global_part - logp * inv_count
        d_log = probs * (d_probs - jnp.sum(d_probs * probs, axis=0, keepdims=True))
        d_log_ref[:, lanes] = d_log
        d_router[...] += nn(jnp.concatenate(split3(d_log), axis=0), obuf[1])

        @pl.when(i + 1 < pieces)
        def _():
            for copy in token_loads(i + 1):
                copy.start()

    def rest(t, carry):
        def streams(s, inner):
            wave(t, s)
            i = (t - units) * 2 + s // 2

            @pl.when(jnp.logical_and(lax.rem(s, 2) == 1, i < pieces))
            def _():
                combine(i)

            return inner

        return lax.fori_loop(0, 4, streams, carry)

    first = units + pieces // 2
    lax.fori_loop(units, first, rest, 0)
    out_store(jnp.int32(pieces - 1)).wait()
    small_work[0, 0:experts, :] = d_router[0:experts] + d_router[experts:2 * experts] + d_router[2 * experts:]

    def late(t, carry):
        def streams(s, inner):
            wave(t, s)
            return inner

        return lax.fori_loop(0, 4, streams, carry)

    small_step(0)
    for k in range(1, 5):
        lax.fori_loop(first + k - 1, first + k, late, 0)
        result = small_step(k)
    small_ref[...] = result
    lax.fori_loop(first + 4, units + 12, late, 0)

    def drain(tile, carry):
        for k in range(12):
            send(tile, k).wait_send()
        return carry

    lax.fori_loop(0, tiles, drain, 0)
    for copy in send_y:
        copy.wait_send()
    for copy in send_d:
        copy.wait()
    self_d.wait()


def global_terms(stats, experts):
    loss = jnp.zeros((1, 128), F32)
    terms = []
    inv = []
    for m in range(2):
        base = 24 * m
        count = stats[base + 16:base + 17]
        mean = stats[base:base + 8] / count
        log_mean = jnp.log(mean)
        loss = loss + stats[base + 8:base + 9] / count + jnp.sum(mean * log_mean, axis=0, keepdims=True)
        terms.append(log_mean / count)
        inv.append(1.0 / count)
    return loss, terms, inv


def final_kernel(slot_ref, d_log_ref, back_ref, router_ref, small_ref, loss_ref, sum_out_ref, sum_in_ref,
                 dx_ref, dw_in_ref, dw_out_ref, d_router_ref, db_in_ref, db_out_ref, aux_ref):
    step = pl.program_id(0)
    n = back_ref.shape[0]
    size, width = dx_ref.shape
    experts = d_log_ref.shape[0]

    @pl.when(step == 0)
    def _():
        d_router_ref[...] = small_ref[0:experts, :]
        for i in range(4):
            db_in_ref[:, i * width:(i + 1) * width] = small_ref[8 + i:9 + i, :].astype(BF16)
        db_out_ref[...] = small_ref[12:13, :].astype(BF16)
        aux_ref[0, 0] = loss_ref[0, 0]

    r = split3(router_ref[...])
    rights = jnp.concatenate([r[0], r[1], r[0], r[1], r[2], r[0]], axis=0)
    d = split3(d_log_ref[...])
    lefts = jnp.concatenate([d[0], d[0], d[1], d[1], d[0], d[2]], axis=0)
    routed = tn(lefts, rights).astype(BF16)
    slot_col = col_of(slot_ref[0:1, :])[:, 0:1]
    pick = (lax.broadcasted_iota(jnp.int32, (size, n), 1).astype(F32) == slot_col).astype(BF16)
    dx_ref[...] = (nn(pick, back_ref[...]) + routed.astype(F32)).astype(BF16)

    dw_out_ref[...] = sum_out_ref[...].reshape(dw_out_ref.shape)
    rows = width // 4
    for a in range(4):
        for b in range(4):
            for j in range(3):
                at = a * rows + b * (rows // 4) + j * 16
                dw_in_ref[at:at + 16, :] = sum_in_ref[0, a, b, :, j * TILE:(j + 1) * TILE]


def vmem(count):
    return [pl.BlockSpec(memory_space=pltpu.VMEM)] * count


def cost(flops, size):
    return pl.CostEstimate(flops=int(flops), bytes_accessed=int(size), transcendentals=0)


def solution(mesh):
    token_spec = P(ALL_AXES)
    expert_spec = P("ep")

    def local_step(x, modality, router, expert_ids, priority, w_in, b_in, w_out, b_out, dy):
        n, width = x.shape
        experts = router.shape[1]
        hid = w_in.shape[2]
        capacity = n // experts
        tiles = hid // TILE
        w_in, w_out = w_in[0], w_out[0]
        ids, prio, mod = (a.reshape(n // 128, 128) for a in (expert_ids, priority, modality))
        router_t = jnp.transpose(router)
        router3 = jnp.concatenate(split3_outside(router_t), axis=0)
        shape = jax.ShapeDtypeStruct
        anywhere = pl.BlockSpec(memory_space=pl.ANY)
        dma = pltpu.SemaphoreType.DMA
        slots = (experts, capacity, width)
        mm = 2 * n * width * hid

        ids_row, mod_row, slot, logp, stats, hidden_t, slope, rows_t, y, d_rows = pl.pallas_call(
            dispatch_kernel,
            out_shape=(
                shape((8, n), F32), shape((8, n), F32), shape((8, n), F32), shape((experts, n), F32), shape((48, 128), F32),
                shape((hid, n), BF16), shape((tiles, n, TILE), F32), shape((width, n), BF16), shape(slots, BF16), shape(slots, BF16),
            ),
            in_specs=vmem(6) + [anywhere] + vmem(1) + [anywhere] + vmem(1),
            out_specs=(*vmem(5), anywhere, anywhere, *vmem(2), anywhere),
            scratch_shapes=[
                pltpu.VMEM((n, 8), F32), pltpu.VMEM((n, width), BF16), pltpu.VMEM(slots, BF16), pltpu.VMEM(slots, BF16),
                pltpu.VMEM(slots, BF16), pltpu.VMEM((n, width), F32),
                pltpu.VMEM((2, width, TILE), BF16), pltpu.VMEM((2, TILE, width), BF16),
                pltpu.VMEM((2, TILE, n), BF16), pltpu.VMEM((2, n, TILE), F32),
                dma((experts - 1,)), dma((experts - 1,)), dma((experts - 1,)), dma((experts - 1,)), dma, dma((2, 2)), dma((2, 2)),
            ],
            compiler_params=pltpu.CompilerParams(collective_id=1, has_side_effects=True, vmem_limit_bytes=62_000_000),
            cost_estimate=cost(3 * mm, 6 * n * hid), name="dispatch",
        )(ids, prio, mod, x, dy, router3, w_in, b_in, w_out, b_out)

        summed, back_y, d_back, out, d_log, loss, small = pl.pallas_call(
            grads_kernel,
            out_shape=(
                shape((2 * tiles, 4, 4, 16, width), BF16), shape(slots, BF16), shape(slots, BF16), shape((n, width), BF16),
                shape((experts, n), F32), shape((8, 128), F32), shape((16, width), F32),
            ),
            in_specs=[anywhere] * 9 + vmem(5),
            out_specs=(*[anywhere] * 4, *vmem(3)),
            scratch_shapes=[
                pltpu.VMEM((2 * tiles, 4, 4, 16, width), F32),
                pltpu.VMEM((2 * tiles, 3, 4, 16, width), F32),
                pltpu.VMEM((2 * tiles, 3, 16, width), F32),
                pltpu.VMEM((2 * tiles, 16, width), BF16),
                pltpu.VMEM((2, TILE, n), BF16),
                pltpu.VMEM((2, n, TILE), F32),
                pltpu.VMEM((2, width, TILE), BF16),
                pltpu.VMEM((2, TILE, width), BF16),
                pltpu.VMEM((n, TILE), BF16),
                pltpu.VMEM((n, width), F32),
                pltpu.VMEM(slots, BF16),
                pltpu.VMEM((width, n), BF16),
                pltpu.VMEM((n, width), BF16),
                pltpu.VMEM((1, hid), F32),
                pltpu.VMEM((CHUNK, width), BF16),
                pltpu.VMEM((48, 128), F32),
                pltpu.VMEM((3 * experts, width), F32),
                pltpu.VMEM((4, 48, 128), F32), pltpu.VMEM((4, 4, 48, 128), F32),
                pltpu.VMEM((4, 16, width), F32), pltpu.VMEM((4, 4, 16, width), F32),
                dma((2 * tiles, 12)), dma((2 * tiles, 12)), dma((2 * tiles,)), dma((2,)), dma((2, 3)),
                dma((experts - 1,)), dma((experts - 1,)), dma((experts - 1,)), dma((experts - 1,)), dma((2,)), dma((2,)), dma,
                dma((4, 3)), dma((4, 3)), dma((4, 3)), dma((4, 3)),
            ],
            compiler_params=pltpu.CompilerParams(collective_id=3, has_side_effects=True, vmem_limit_bytes=67_000_000),
            cost_estimate=cost(4 * mm, 6 * n * hid), name="expert_grads",
        )(hidden_t, slope, w_in, w_out, rows_t, d_rows.reshape(n, width), y, x, dy, ids_row, mod_row, slot, logp, stats)

        size = n // tiles
        d_x, d_w_in, d_w_out, d_router, d_b_in, d_b_out, aux = pl.pallas_call(
            final_kernel,
            grid=(tiles,),
            out_shape=(
                shape((n, width), BF16), shape((width, hid), BF16), shape((hid, width), BF16), shape((experts, width), F32),
                shape((1, hid), BF16), shape((1, width), BF16), shape((1, 1), F32),
            ),
            in_specs=[
                pl.BlockSpec((8, size), lambda i: (0, i)),
                pl.BlockSpec((experts, size), lambda i: (0, i)),
                pl.BlockSpec((n, width), lambda i: (0, 0)),
                pl.BlockSpec((experts, width), lambda i: (0, 0)),
                pl.BlockSpec((16, width), lambda i: (0, 0)),
                pl.BlockSpec((8, 128), lambda i: (0, 0)),
                pl.BlockSpec((1, 4, 4, 16, width), lambda i: (i, 0, 0, 0, 0)),
                pl.BlockSpec((1, 4, 4, 16, width), lambda i: (i + tiles, 0, 0, 0, 0)),
            ],
            out_specs=(
                pl.BlockSpec((size, width), lambda i: (i, 0)),
                pl.BlockSpec((width, TILE), lambda i: (0, i)),
                pl.BlockSpec((TILE, width), lambda i: (i, 0)),
                pl.BlockSpec((experts, width), lambda i: (0, 0)),
                pl.BlockSpec((1, hid), lambda i: (0, 0)),
                pl.BlockSpec((1, width), lambda i: (0, 0)),
                pl.BlockSpec(memory_space=pltpu.SMEM),
            ),
            name="final",
        )(slot, d_log, d_back.reshape(n, width), router_t, small, loss, summed, summed)
        return out, aux[0, 0], d_x, jnp.transpose(d_router), d_w_in[None], d_b_in, d_w_out[None], d_b_out

    def split3_outside(a):
        hi = lax.reduce_precision(a, 8, 7)
        mid = lax.reduce_precision(a - hi, 8, 7)
        return hi.astype(BF16), mid.astype(BF16), (a - hi - mid).astype(BF16)

    return jax.shard_map(
        local_step,
        mesh=mesh,
        in_specs=(token_spec, token_spec, P(), token_spec, token_spec, expert_spec, expert_spec, expert_spec, expert_spec, token_spec),
        out_specs=(token_spec, P(), token_spec, P(), expert_spec, expert_spec, expert_spec, expert_spec),
        check_vma=False,
    )
```

time: 363 us -> 274 us (0.75)
  Pallas kernels: 314 us -> 270 us
  waiting for transfers between devices: 18.6 us -> 0 us
  local copies, waits for them, and re-layouts: 14 us -> 1.41 us
  starting transfers between devices: 9.14 us -> 0 us
    pallas_call x8 -> x2, Pallas kernels: 142 us -> 81.3 us  [the longest x1 66.9 us: local_step(): pl.pallas_call(dispatch_kernel, out_shape=(shape((8, n), F32), shape((8,...]
    all_to_all x2 -> x0, waiting for transfers between devices: 18.6 us -> none  [the longest x1 18.6 us: local_step(): lax.all_to_all(send_rows, 'ep', 0, 0, tiled=True).reshape(n, width)]
    pallas_call x1, Pallas kernels: 172 us -> 188 us  [local_step(): pl.pallas_call(grads_kernel, out_shape=(shape((2 * tiles, 4, 4, 16, width...]
    all_to_all x2 -> x0, starting transfers between devices: 9.14 us -> none  [the longest x1 4.58 us: local_step(): lax.all_to_all(send_rows, 'ep', 0, 0, tiled=True).reshape(n, width)]
    slice x3 -> x0, local copies, waits for them, and re-layouts: 6.84 us -> none  [the longest x1 5.06 us: local_step(): d_w_out = summed[:tiles].reshape(hid, width)]
  transfers between devices with their start and end apart: 2 -> 0, of which waited for: 1 -> 0; matrix products, arithmetic and copies ran while one was open for 0% -> 0% of each run, Pallas kernels for 23% -> 0%
where the time goes in v3:
time: 274 us; the launch traced here: 273 us
  Pallas kernels  270 us (99%)
    pallas_call x1, Pallas kernels, local_step(): pl.pallas_call(grads_kernel, out_shape=(shape((2 * tiles, 4, 4, 16, width...  188 us
    pallas_call x1, Pallas kernels, local_step(): pl.pallas_call(dispatch_kernel, out_shape=(shape((8, n), F32), shape((8,...  66.9 us
    pallas_call x1, Pallas kernels, local_step(): pl.pallas_call(final_kernel, grid=(tiles,), out_shape=(shape((n, width),...  14.5 us

profile of v3, /device:TPU:0, one launch (start us, length us, event | category | flops | bytes accessed | tf_op | source)
XLA Modules:
  0.0 273.3 jit_solution(8840225160050942605)
XLA Ops:
  0.6 0.7 reduce-precision_convert_fusion.1
  1.4 0.6 pad_maximum_fusion.router3_ref
  2.0 66.9 %dispatch.1 = (f32[8,1536]{1,0:T(8,128)}, f32[8,1536]{1,0:T(8,128)}, f32[8,1536]{1,0:T(8,128)}, f32[8,1536]{1,0:T(8,128)}, f32[48,128]{1,0:T(8,128)}, /*index=5*...) custom-call(s32[12,128]{1,0:T(8,128)} %bitcast.24, ...), custom_call_target="tpu_custom_call" | custom-call | flops 21743271936 | bytes 28311552 | tf_op jit(solution)/shard_map/dispatch/pallas_call | solution.py:656
  68.9 188.5 %expert_grads.1 = (bf16[24,4,4,16,768]{4,3,2,1,0:T(8,128)(2,1)}, bf16[8,192,768]{2,1,0:T(8,128)(2,1)}, bf16[8,192,768]{2,1,0:T(8,128)(2,1)}, bf16[1536,768]{1,0:...) custom-call(bf16[3072,1536]{1,0:T(8,128)(2,1)} %get-tuple-element.31.hidden_t, ...), custom_call_target="tpu_custom_call" | custom-call | flops 28991029248 | bytes 28311552 | tf_op jit(solution)/shard_map/expert_grads/pallas_call | solution.py:675
  257.4 0.0 copy-start
  257.4 14.5 %final.1 = (bf16[1536,768]{1,0:T(8,128)(2,1)}, bf16[768,3072]{1,0:T(8,128)(2,1)}, bf16[3072,768]{1,0:T(8,128)(2,1)}, f32[8,768]{1,0:T(8,128)}, bf16[1,3072]{1,0:...) custom-call(f32[8,1536]{1,0:T(8,128)} %get-tuple-element.38.slot_row.slot_ref, ...), custom_call_target="tpu_custom_call" | custom-call | tf_op jit(solution)/shard_map/final/pallas_call | solution.py:712
  271.8 0.0 copy-done
  271.8 1.4 copy.19
Async XLA Ops:
  257.4 14.5 %copy-start = (bf16[1536,768]{1,0:T(8,128)(2,1)S(1)}, bf16[1536,768]{1,0:T(8,128)(2,1)}, u32[]{:S(2)}) copy-start(bf16[1536,768]{1,0:T(8,128)(2,1)} %get-tuple-element.65) | copy-start | bytes 7077892

commit v4 on v0

v4 whole, which is shorter than its diff:
```python
import functools

import jax
import jax.numpy as jnp
from jax import lax
from jax.experimental import pallas as pl
from jax.experimental.pallas import tpu as pltpu
from jax.sharding import PartitionSpec as P

ALL_AXES = ("dp", "ep")
MESH = pl.DeviceIdType.MESH
F32 = jnp.float32
BF16 = jnp.bfloat16
NOWHERE = -1.0
TILE = 256
CHUNK = 256


def col_of(row):
    return jnp.transpose(jnp.broadcast_to(row, (8, row.shape[1])))


def row_of(col):
    return jnp.transpose(jnp.broadcast_to(col, (col.shape[0], 8)))


def split3(a):
    hi = a.astype(BF16)
    rest = a - hi.astype(F32)
    mid = rest.astype(BF16)
    lo = (rest - mid.astype(F32)).astype(BF16)
    return hi, mid, lo


def nt(a, b):
    return lax.dot_general(a, b, (((1,), (1,)), ((), ())), preferred_element_type=F32)


def tn(a, b):
    return lax.dot_general(a, b, (((0,), (0,)), ((), ())), preferred_element_type=F32)


def nn(a, b):
    return jnp.dot(a, b, preferred_element_type=F32)


def wide(ref):
    v = ref[...].astype(F32)
    return jnp.concatenate([v[i:i + 1, :] for i in range(v.shape[0])], axis=1)


def greet(peers):
    barrier = pltpu.get_barrier_semaphore()
    for peer in peers:
        pl.semaphore_signal(barrier, inc=1, device_id=peer, device_id_type=MESH)
    return lambda: pl.semaphore_wait(barrier, len(peers))


ROOT = 0.7978845608028654
CUBIC = 0.044715


def block_kernel(
    ids_ref, prio_ref, mod_ref, x_any, dy_any, router_ref, w_in, b_in_ref, w_out, b_out_ref,
    summed, back_y, back_d, out, hidden_t, pre_act, slot_row, d_log_ref, loss_ref, small_ref,
    part_sum, land_a, land_b, own, x_buf, dy_buf, out_x, rows, rows_t, tok, acc, hidbuf, sbuf, ibuf, obuf, act, abuf, hbuf, stage,
    keycol, ids_row, mod_row, logp_ref, db_in, stats_ref, d_router, stat_work, stat_bufs, small_work, small_bufs,
    send_sem, recv_sem, own_sem, credit, x_send, x_recv, d_send, d_recv, y_send, y_recv, g_send, g_recv,
    self_sem, tok_sem, out_sem, i_sem, o_sem, a_sem, h_sem, hid_sem, s_sem, stat_send, stat_recv, small_send, small_recv,
):
    dp = lax.axis_index("dp")
    ep = lax.axis_index("ep")
    z, yy = dp // 4, lax.rem(dp, 4)
    xx, core = ep // 2, lax.rem(ep, 2)
    tiles = part_sum.shape[0]
    units = tiles // 4
    half = tiles // 2
    experts, capacity, width = out_x.shape
    n = experts * capacity
    pairs = experts // 2
    share = n // pairs
    steps = pairs * half
    others = experts - 1
    out_d = x_buf.reshape(out_x.shape)
    tok_slots = tok.reshape(out_x.shape)

    def wrap(v):
        return lax.rem(v + 16, 4)

    peers = [(z * 4 + wrap(yy + j), ep) for j in range(1, 4)] + [(wrap(z + j) * 4 + yy, ep) for j in range(1, 4)]
    enter = greet(peers + [(dp, lax.rem(ep + j, experts)) for j in range(1, experts)])
    load_x = pltpu.make_async_copy(x_any, x_buf, tok_sem.at[0])
    load_dy = pltpu.make_async_copy(dy_any, dy_buf, tok_sem.at[1])
    load_x.start()
    load_dy.start()

    rings = (
        (yy, peers[0:3]),
        (z, peers[3:6]),
        None,
        (xx, [(dp, lax.rem(ep + 2 * j, experts)) for j in range(1, 4)]),
    )
    partner = (dp, xx * 2 + 1 - core)

    def small_sum(work, bufs, whole_rows, send_sems, recv_sems):
        head = pl.ds(0, whole_rows)
        full = pl.ds(0, work.shape[1])

        def pair():
            return pltpu.make_async_remote_copy(
                src_ref=work.at[2, head], dst_ref=bufs.at[2, 0, head], send_sem=send_sems.at[2, 0], recv_sem=recv_sems.at[2, 0],
                device_id=partner, device_id_type=MESH)

        def ring(axis):
            me, ring_peers = rings[axis]
            at = head if axis == 3 else full
            return [
                pltpu.make_async_remote_copy(
                    src_ref=work.at[axis, at], dst_ref=bufs.at[axis, me, at], send_sem=send_sems.at[axis, j],
                    recv_sem=recv_sems.at[axis, j], device_id=ring_peers[j], device_id_type=MESH)
                for j in range(3)
            ]

        def launch(axis):
            bufs[axis, rings[axis][0]] = work[axis]
            for copy in ring(axis):
                copy.start()

        def total(axis, at):
            for copy in ring(axis):
                copy.wait()
            return bufs[axis, 0, at, :] + bufs[axis, 1, at, :] + bufs[axis, 2, at, :] + bufs[axis, 3, at, :]

        def step(k, dst=None):
            if k == 0:
                launch(0)
            elif k == 1:
                work[1] = total(0, full)
                launch(1)
            elif k == 2:
                work[2] = total(1, full)
                pair().start()
            elif k == 3:
                pair().wait()
                work[3] = work[2]
                work[3, head, :] = work[2, head, :] + bufs[2, 0, head, :]
                launch(3)
            else:
                dst[...] = work[2]
                dst[head, :] = total(3, head)

        return step

    stat_step = small_sum(stat_work, stat_bufs, 48, stat_send, stat_recv)
    small_step = small_sum(small_work, small_bufs, experts, small_send, small_recv)

    ids = wide(ids_ref)
    key = ids * n + wide(prio_ref)
    low = ids * n
    keycol[...] = col_of(key)

    def count(j, total):
        col = keycol[pl.ds(pl.multiple_of(j * 128, 128), 128), :][:, 0:1]
        before = jnp.logical_and(col < key, col >= low)
        return total + jnp.sum(before.astype(F32), axis=0, keepdims=True)

    position = lax.fori_loop(0, n // 128, count, jnp.zeros((1, n), F32))
    slot = jnp.where(position < capacity, ids * capacity + position, NOWHERE)
    slot_row[...] = jnp.broadcast_to(slot, slot_row.shape)
    mod = wide(mod_ref)
    ids_row[...] = jnp.broadcast_to(ids, ids_row.shape)
    mod_row[...] = jnp.broadcast_to(mod, mod_row.shape)

    def hops(q):
        return q + q // 2 - 2 * (q // 3)

    def target(j):
        return wrap(xx + hops((j + 1) // 2)) * 2 + lax.rem(core + 1 - lax.rem(j, 2), 2)

    def pick(e):
        index = (lax.broadcasted_iota(jnp.int32, (capacity, n), 0) + e * capacity).astype(F32)
        return (index == slot_row[0:1, :]).astype(BF16)

    def x_copy(j):
        to = target(j)
        return pltpu.make_async_remote_copy(
            src_ref=out_x.at[to], dst_ref=rows.at[ep], send_sem=x_send.at[j], recv_sem=x_recv.at[j],
            device_id=(dp, to), device_id_type=MESH)

    def d_copy(j, s):
        to = target(j)
        at = pl.ds(pl.multiple_of(s * TILE, TILE), TILE)
        return pltpu.make_async_remote_copy(
            src_ref=out_d.at[to, :, at], dst_ref=tok_slots.at[ep, :, at], send_sem=d_send.at[j, s], recv_sem=d_recv.at[j, s],
            device_id=(dp, to), device_id_type=MESH)

    def load_i(it):
        slot = lax.rem(it, 2)
        at = pl.ds(pl.multiple_of(lax.rem(it, half) * TILE, TILE), TILE)
        return pltpu.make_async_copy(w_in.at[:, at], ibuf.at[slot], i_sem.at[slot])

    def load_o(it):
        slot = lax.rem(it, 2)
        at = pl.ds(pl.multiple_of(lax.rem(it, half) * TILE, TILE), TILE)
        return pltpu.make_async_copy(w_out.at[at], obuf.at[slot], o_sem.at[slot])

    load_x.wait()
    enter()

    def send_x(j, carry):
        out_x[target(j)] = nn(pick(target(j)), x_buf[...]).astype(BF16)
        x_copy(j).start()
        return carry

    lax.fori_loop(0, others, send_x, 0)
    load_i(0).start()
    load_i(1).start()
    load_o(0).start()
    rows[ep] = nn(pick(ep), x_buf[...]).astype(BF16)

    router3 = jnp.concatenate(split3(router_ref[...]), axis=0)
    logits3 = nt(router3, x_buf[...])
    logits = logits3[0:experts] + logits3[experts:2 * experts] + logits3[2 * experts:3 * experts]
    shifted = logits - jnp.max(logits, axis=0, keepdims=True)
    logp = shifted - jnp.log(jnp.sum(jnp.exp(shifted), axis=0, keepdims=True))
    logp_ref[...] = logp
    probs = jnp.exp(logp)
    onehot = (lax.broadcasted_iota(jnp.int32, (experts, n), 0).astype(F32) == ids).astype(F32)
    gate = jnp.sum(probs * onehot, axis=0, keepdims=True)
    entropy = -jnp.sum(probs * logp, axis=0, keepdims=True)
    for m in range(2):
        mask = (mod == m).astype(F32)
        stat_work[0, 24 * m:24 * m + 8, :] = jnp.broadcast_to(jnp.sum(probs * mask, axis=1, keepdims=True), (8, 128))
        stat_work[0, 24 * m + 8:24 * m + 16, :] = jnp.broadcast_to(jnp.sum(entropy * mask, axis=1, keepdims=True), (8, 128))
        stat_work[0, 24 * m + 16:24 * m + 24, :] = jnp.broadcast_to(jnp.sum(mask, axis=1, keepdims=True), (8, 128))
    stat_step(0)
    load_dy.wait()
    dy_buf[...] = (col_of(gate)[:, 0:1] * dy_buf[...].astype(F32)).astype(BF16)

    def pick_cotangent(j, carry):
        out_d[target(j)] = nn(pick(target(j)), dy_buf[...]).astype(BF16)
        return carry

    lax.fori_loop(0, others, pick_cotangent, 0)
    tok_slots[ep] = nn(pick(ep), dy_buf[...]).astype(BF16)
    stat_step(1)
    acc[...] = jnp.broadcast_to(b_out_ref[...].astype(F32), acc.shape)
    small_work[0] = jnp.zeros(small_work.shape[1:], F32)

    def origin(it):
        return wrap(xx - hops(it // half))

    def store_a(it):
        slot = lax.rem(it, 3)
        at = pl.ds(pl.multiple_of(origin(it) * share, share), share)
        return pltpu.make_async_copy(abuf.at[slot], pre_act.at[lax.rem(it, half), at], a_sem.at[slot])

    def store_h(it):
        slot = lax.rem(it, 2)
        down = pl.ds(pl.multiple_of(lax.rem(it, half) * TILE, TILE), TILE)
        at = pl.ds(pl.multiple_of(origin(it) * share, share), share)
        return pltpu.make_async_copy(hbuf.at[slot], hidden_t.at[down, at], h_sem.at[slot])

    def first_matmul(it):
        at = pl.ds(pl.multiple_of(lax.rem(it, half) * TILE, TILE), TILE)
        chunk = rows[pl.ds(origin(it) * 2, 2)].reshape(share, width)
        abuf[lax.rem(it, 3)] = nn(chunk, ibuf[lax.rem(it, 2)]) + b_in_ref[:, at].astype(F32)

    def rest_of_step(it):
        a = abuf[lax.rem(it, 3)]
        t = jnp.tanh(ROOT * (a + CUBIC * (a * a * a)))
        hidden = (a * (0.5 * (1.0 + t))).astype(BF16)
        hbuf[lax.rem(it, 2)] = jnp.transpose(hidden)
        at = pl.ds(pl.multiple_of(origin(it) * share, share), share)
        acc[at, :] += nn(hidden, obuf[lax.rem(it, 2)])

    def forward(it, carry):
        nxt = it + 1
        store_a(it).start()
        load_o(it).wait()
        load_o(nxt).start()

        @pl.when(lax.rem(nxt, half) == 0)
        def _():
            q = nxt // half
            x_copy(2 * q - 1).wait_recv()
            x_copy(2 * q).wait_recv()

        load_i(nxt).wait()

        @pl.when(nxt + 1 < steps)
        def _():
            load_i(nxt + 1).start()

        @pl.when(it >= 2)
        def _():
            store_a(it - 2).wait()
            store_h(it - 2).wait()

        first_matmul(nxt)
        rest_of_step(it)
        store_h(it).start()
        for k, when in ((2, 4), (3, 8)):
            @pl.when(it == when)
            def _():
                stat_step(k)

        @pl.when(it == 9)
        def _():
            for s in range(3):
                for j in range(others):
                    d_copy(j, s).start()

        return carry

    x_copy(0).wait_recv()
    load_i(0).wait()
    first_matmul(jnp.int32(0))
    lax.fori_loop(0, steps - 1, forward, 0)
    last = jnp.int32(steps - 1)
    store_a(last).start()
    load_o(last).wait()
    store_a(last - 2).wait()
    store_h(last - 2).wait()
    rest_of_step(last)
    store_h(last).start()

    def place(stream):
        way = 1 - 2 * lax.rem(stream, 2)
        first_z = stream // 2
        pa = yy * (1 - first_z) + z * first_z
        pb = z * (1 - first_z) + yy * first_z

        def along(move):
            on_y = z * 4 + wrap(yy + move)
            on_z = wrap(z + move) * 4 + yy
            return on_y * (1 - first_z) + on_z * first_z, on_z * (1 - first_z) + on_y * first_z

        return way, pa, pb, along(way), along(-way)

    def send(tile, k):
        way, pa, pb, (next_a, next_b), _ = place(lax.rem(tile, 4))
        if k < 3:
            src, dst, to = part_sum.at[tile, wrap(pa - way * (k + 1))], land_a.at[lax.rem(tile, half), k], next_a
        elif k < 6:
            src, dst, to = part_sum.at[tile, pa, wrap(pb - way * (k - 2))], land_b.at[lax.rem(tile, half), k - 3], next_b
        elif k == 6:
            src, dst, to = own.at[tile], summed.at[tile, pa, pb], next_b
        elif k < 9:
            src = summed.at[tile, pa, wrap(pb - way * (k - 6))]
            dst, to = src, next_b
        else:
            src = summed.at[tile, wrap(pa - way * (k - 9))]
            dst, to = src, next_a
        return pltpu.make_async_remote_copy(
            src_ref=src, dst_ref=dst, send_sem=send_sem.at[tile, k], recv_sem=recv_sem.at[tile, k],
            device_id=(to, ep), device_id_type=MESH)

    def start(tile, k):
        if k < 6:
            @pl.when(tile >= half)
            def _():
                pl.semaphore_wait(credit.at[tile - half, k], 1)

        send(tile, k).start()

    def keep(tile):
        way, pa, pb, _, _ = place(lax.rem(tile, 4))
        return pltpu.make_async_copy(own.at[tile], summed.at[tile, pa, pb], own_sem.at[tile])

    def advance(tile, k):
        way, pa, pb, _, (prev_a, prev_b) = place(lax.rem(tile, 4))
        spot = lax.rem(tile, half)
        send(tile, k - 1).wait_recv()
        if k <= 3:
            block = wrap(pa - way * (k + 1))
            part_sum[tile, block] = part_sum[tile, block] + land_a[spot, k - 1]
        elif k <= 6:
            block = wrap(pb - way * (k - 2))
            total = part_sum[tile, pa, block] + land_b[spot, k - 4]
            if k < 6:
                part_sum[tile, pa, block] = total
            else:
                own[tile] = total.astype(BF16)
                keep(tile).start()
        elif k == 9:
            keep(tile).wait()
        if k <= 6:
            back_to = prev_a if k <= 3 else prev_b

            @pl.when(tile < half)
            def _():
                pl.semaphore_signal(credit.at[tile, k - 1], inc=1, device_id=(back_to, ep), device_id_type=MESH)

        if k < 12:
            start(tile, k)

    def wave(t, stream):
        for k in range(12, 0, -1):
            unit = t - k

            @pl.when(jnp.logical_and(unit >= 0, unit < units))
            def _():
                advance(unit * 4 + stream, k)

    def exchange(src, dst, send_sems, recv_sems):
        copies = []
        for j in range(1, experts):
            to = lax.rem(ep + j, experts)
            copies.append(pltpu.make_async_remote_copy(
                src_ref=src.at[to], dst_ref=dst.at[ep], send_sem=send_sems.at[j - 1], recv_sem=recv_sems.at[j - 1],
                device_id=(dp, to), device_id_type=MESH))
        return copies

    def place_tile(tile, a, grad):
        for b in range(4):
            for j in range(3):
                at = b * (width // 16) + j * 16
                part_sum[tile, a, b, :, j * TILE:(j + 1) * TILE] = grad[at:at + 16, :]

    def load_hid(i):
        slot = lax.rem(i, 2)
        at = pl.ds(pl.multiple_of(lax.rem(i, 8) * (width // 2), width // 2), width // 2)
        return pltpu.make_async_copy(hidden_t.at[at], hidbuf.at[slot], hid_sem.at[slot])

    def load_s(i):
        slot = lax.rem(i, 2)
        return pltpu.make_async_copy(pre_act.at[i], sbuf.at[slot], s_sem.at[slot])

    store_a(last - 1).wait()
    store_a(last).wait()
    store_h(last - 1).wait()
    store_h(last).wait()
    load_hid(jnp.int32(0)).start()
    load_s(jnp.int32(0)).start()
    load_i(0).start()
    load_o(0).start()
    for j in range(others):
        x_copy(j).wait_send()
    out_x[...] = acc[...].astype(BF16).reshape(out_x.shape)

    def out_tile(i, carry):
        unit, stream = i // 4, lax.rem(i, 4)
        wave(unit, stream)

        @pl.when(stream == 0)
        def _():
            for j in range(others):
                d_copy(j, unit).wait_recv()

        at = pl.ds(pl.multiple_of(unit * TILE, TILE), TILE)
        for piece in range(2):
            load_hid(2 * i + piece).wait()

            @pl.when(2 * i + piece + 1 < 2 * half)
            def _():
                load_hid(2 * i + piece + 1).start()

            grad = nn(hidbuf[piece], tok[:, at])
            for a in range(2):
                place_tile(i, 2 * piece + a, grad[a * (width // 4):(a + 1) * (width // 4)])
        start(i, 0)
        return carry

    lax.fori_loop(0, half, out_tile, 0)
    stat_step(4, stats_ref)
    send_y = exchange(out_x, back_y, y_send, y_recv)
    for copy in send_y:
        copy.start()
    self_y = pltpu.make_async_copy(out_x.at[ep], back_y.at[ep], self_sem.at[0])
    self_y.start()
    small_work[0, 12:13, :] = jnp.sum(tok[...].astype(F32), axis=0, keepdims=True)
    rows_t[...] = jnp.transpose(rows[...].reshape(n, width))
    acc[...] = jnp.zeros_like(acc)
    chunks = 4
    size = n // chunks

    def in_tile(i, carry):
        g = i + half
        wave(g // 4, lax.rem(g, 4))
        slot = lax.rem(i, 2)
        for load in (load_s, load_i, load_o):
            load(i).wait()

        @pl.when(i + 1 < half)
        def _():
            for load in (load_s, load_i, load_o):
                load(i + 1).start()

        total = jnp.zeros((1, TILE), F32)
        for c in range(chunks):
            part = pl.ds(c * size, size)
            d_hidden = nt(tok[part, :], obuf[slot]).astype(BF16)
            a = sbuf[slot, part, :]
            sq = a * a
            t = jnp.tanh(ROOT * (a + CUBIC * (sq * a)))
            slope = 0.5 * (1.0 + t) + (0.5 * ROOT) * a * (1.0 - t * t) * (1.0 + (3 * CUBIC) * sq)
            d_act = d_hidden.astype(F32) * slope
            total += jnp.sum(d_act, axis=0, keepdims=True)
            d_act_bf = d_act.astype(BF16)
            act[part, :] = d_act_bf
            acc[part, :] += nt(d_act_bf, ibuf[slot])
        db_in[:, pl.ds(pl.multiple_of(i * TILE, TILE), TILE)] = total
        for a in range(4):
            place_tile(g, a, nn(rows_t[pl.ds(a * (width // 4), width // 4), :], act[...]))
        start(g, 0)
        return carry

    lax.fori_loop(0, half, in_tile, 0)

    rows[...] = acc[...].astype(BF16).reshape(rows.shape)
    send_g = exchange(rows, back_d, g_send, g_recv)
    for copy in send_g:
        copy.start()
    self_g = pltpu.make_async_copy(rows.at[ep], back_d.at[ep], self_sem.at[1])
    self_g.start()

    for copy in send_y:
        copy.wait_recv()
    self_y.wait()
    back = pltpu.make_async_copy(back_y, dy_buf.reshape(back_y.shape), tok_sem.at[1])
    back.start()
    for i in range(4):
        small_work[0, 8 + i:9 + i, :] = db_in[:, i * width:(i + 1) * width]
    d_router[...] = jnp.zeros_like(d_router)
    loss, terms, inv = global_terms(stats_ref[...], experts)
    loss_ref[...] = jnp.broadcast_to(loss, loss_ref.shape)

    def token_loads(i):
        at = pl.ds(pl.multiple_of(i * CHUNK, CHUNK), CHUNK)
        return (
            pltpu.make_async_copy(dy_any.at[at], obuf.at[0], o_sem.at[0]),
            pltpu.make_async_copy(x_any.at[at], obuf.at[1], o_sem.at[1]),
        )

    def out_store(i):
        at = pl.ds(pl.multiple_of(i * CHUNK, CHUNK), CHUNK)
        return pltpu.make_async_copy(stage, out.at[at], out_sem)

    for copy in token_loads(jnp.int32(0)):
        copy.start()
    back.wait()
    pieces = n // CHUNK

    def combine(i):
        lanes = pl.ds(pl.multiple_of(i * CHUNK, CHUNK), CHUNK)
        slot_col = col_of(slot_row[0:1, lanes])[:, 0:1]
        chosen = (lax.broadcasted_iota(jnp.int32, (CHUNK, n), 1).astype(F32) == slot_col).astype(BF16)
        y_tok = nn(chosen, dy_buf[...])
        logp = logp_ref[:, lanes]
        probs = jnp.exp(logp)
        onehot = (lax.broadcasted_iota(jnp.int32, (experts, CHUNK), 0).astype(F32) == ids_row[:, lanes]).astype(F32)
        gate = jnp.sum(probs * onehot, axis=0, keepdims=True)
        for copy in token_loads(i):
            copy.wait()

        @pl.when(i > 0)
        def _():
            out_store(i - 1).wait()

        stage[...] = (col_of(gate)[:, 0:1] * y_tok).astype(BF16)
        out_store(i).start()
        d_gate = row_of(jnp.sum(obuf[0].astype(F32) * y_tok, axis=1, keepdims=True))[0:1]
        is_text = mod_row[:, lanes] == 1.0
        global_part = jnp.where(is_text, terms[1][:, 0:1], terms[0][:, 0:1])
        inv_count = jnp.where(is_text, inv[1][:, 0:1], inv[0][:, 0:1])
        d_probs = onehot * d_gate + global_part - logp * inv_count
        d_log = probs * (d_probs - jnp.sum(d_probs * probs, axis=0, keepdims=True))
        d_log_ref[:, lanes] = d_log
        d_router[...] += nn(jnp.concatenate(split3(d_log), axis=0), obuf[1])

        @pl.when(i + 1 < pieces)
        def _():
            for copy in token_loads(i + 1):
                copy.start()

    def rest(t, carry):
        def streams(s, inner):
            wave(t, s)

            @pl.when(s == 1)
            def _():
                combine(t - units)

            return inner

        return lax.fori_loop(0, 4, streams, carry)

    first = units + pieces
    lax.fori_loop(units, first, rest, 0)
    out_store(jnp.int32(pieces - 1)).wait()
    small_work[0, 0:experts, :] = d_router[0:experts] + d_router[experts:2 * experts] + d_router[2 * experts:]

    def late(t, carry):
        def streams(s, inner):
            wave(t, s)
            return inner

        return lax.fori_loop(0, 4, streams, carry)

    small_step(0)
    for k in range(1, 4):
        lax.fori_loop(first + k - 1, first + k, late, 0)
        small_step(k)
    lax.fori_loop(first + 3, units + 12, late, 0)
    small_step(4, small_ref)

    def drain(tile, carry):
        for k in range(12):
            send(tile, k).wait_send()
        return carry

    lax.fori_loop(0, tiles, drain, 0)
    for s in range(3):
        for j in range(others):
            d_copy(j, s).wait_send()
    for copy in send_y:
        copy.wait_send()
    for copy in send_g:
        copy.wait()
    self_g.wait()


def global_terms(stats, experts):
    loss = jnp.zeros((1, 128), F32)
    terms = []
    inv = []
    for m in range(2):
        base = 24 * m
        count = stats[base + 16:base + 17]
        mean = stats[base:base + 8] / count
        log_mean = jnp.log(mean)
        loss = loss + stats[base + 8:base + 9] / count + jnp.sum(mean * log_mean, axis=0, keepdims=True)
        terms.append(log_mean / count)
        inv.append(1.0 / count)
    return loss, terms, inv


def final_kernel(slot_ref, d_log_ref, back_any, router_ref, small_ref, loss_ref, summed, out_any,
                 dx, dw_in, dw_out, out, d_router_ref, db_in_ref, db_out_ref, aux_ref,
                 buf, back, out_buf, dx_buf, load_sem, store_sem, back_sem, out_sem, dx_sem):
    n, width = dx.shape
    tiles = buf.shape[0]
    half = tiles // 2
    units = tiles // 4
    experts = d_log_ref.shape[0]
    pieces = n // CHUNK

    load_back = pltpu.make_async_copy(back_any, back, back_sem)
    load_back.start()

    def loads(t):
        return [
            pltpu.make_async_copy(summed.at[t, :, :, :, pl.ds(j * TILE, TILE)], buf.at[t, :, :, j], load_sem.at[t, j])
            for j in range(3)
        ]

    def store(t):
        tile = buf.at[t].reshape(width, TILE)
        if t < half:
            unit, stream = t // 4, t % 4
            dst = dw_out.at[pl.ds(stream * width, width), pl.ds(unit * TILE, TILE)]
        else:
            dst = dw_in.at[:, pl.ds((t - half) * TILE, TILE)]
        return pltpu.make_async_copy(tile, dst, store_sem.at[t])

    for t in range(tiles):
        for copy in loads(t):
            copy.start()
    load_out = pltpu.make_async_copy(out_any, out_buf, out_sem.at[0])
    load_out.start()

    d_router_ref[...] = small_ref[0:experts, :]
    for i in range(4):
        db_in_ref[:, i * width:(i + 1) * width] = small_ref[8 + i:9 + i, :].astype(BF16)
    db_out_ref[...] = small_ref[12:13, :].astype(BF16)
    aux_ref[0, 0] = loss_ref[0, 0]
    r = split3(router_ref[...])
    rights = jnp.concatenate([r[0], r[1], r[0], r[1], r[2], r[0]], axis=0)
    load_back.wait()

    def dx_store(i):
        at = pl.ds(i * CHUNK, CHUNK)
        return pltpu.make_async_copy(dx_buf.at[at], dx.at[at], dx_sem.at[i])

    per_piece = tiles // pieces
    for i in range(pieces):
        lanes = pl.ds(i * CHUNK, CHUNK)
        d = split3(d_log_ref[:, lanes])
        lefts = jnp.concatenate([d[0], d[0], d[1], d[1], d[0], d[2]], axis=0)
        routed = tn(lefts, rights).astype(BF16)
        slot_col = col_of(slot_ref[0:1, lanes])[:, 0:1]
        chosen = (lax.broadcasted_iota(jnp.int32, (CHUNK, n), 1).astype(F32) == slot_col).astype(BF16)
        dx_buf[lanes, :] = (nn(chosen, back[...]) + routed.astype(F32)).astype(BF16)
        dx_store(i).start()
        for t in range(i * per_piece, (i + 1) * per_piece):
            for copy in loads(t):
                copy.wait()
            store(t).start()
    load_out.wait()
    store_out = pltpu.make_async_copy(out_buf, out, out_sem.at[1])
    store_out.start()
    for t in range(tiles):
        store(t).wait()
    for i in range(pieces):
        dx_store(i).wait()
    store_out.wait()


def vmem(count):
    return [pl.BlockSpec(memory_space=pltpu.VMEM)] * count


def cost(flops, size):
    return pl.CostEstimate(flops=int(flops), bytes_accessed=int(size), transcendentals=0)


def solution(mesh):
    token_spec = P(ALL_AXES)
    expert_spec = P("ep")

    def local_step(x, modality, router, expert_ids, priority, w_in, b_in, w_out, b_out, dy):
        n, width = x.shape
        experts = router.shape[1]
        hid = w_in.shape[2]
        capacity = n // experts
        tiles = hid // TILE
        share = n // (experts // 2)
        w_in, w_out = w_in[0], w_out[0]
        ids, prio, mod = (a.reshape(n // 128, 128) for a in (expert_ids, priority, modality))
        router_t = jnp.transpose(router)
        shape = jax.ShapeDtypeStruct
        anywhere = pl.BlockSpec(memory_space=pl.ANY)
        dma = pltpu.SemaphoreType.DMA
        slots = (experts, capacity, width)
        mm = 2 * n * width * hid
        others = experts - 1

        summed, back_y, d_back, out, _, _, slot, d_log, loss, small = pl.pallas_call(
            block_kernel,
            out_shape=(
                shape((2 * tiles, 4, 4, 16, width), BF16), shape(slots, BF16), shape(slots, BF16), shape((n, width), BF16),
                shape((hid, n), BF16), shape((tiles, n, TILE), F32),
                shape((8, n), F32), shape((experts, n), F32), shape((8, 128), F32), shape((16, width), F32),
            ),
            in_specs=vmem(3) + [anywhere] * 2 + vmem(1) + [anywhere] + vmem(1) + [anywhere] + vmem(1),
            out_specs=(*[anywhere] * 6, *vmem(4)),
            scratch_shapes=[
                pltpu.VMEM((2 * tiles, 4, 4, 16, width), F32),
                pltpu.VMEM((tiles, 3, 4, 16, width), F32),
                pltpu.VMEM((tiles, 3, 16, width), F32),
                pltpu.VMEM((2 * tiles, 16, width), BF16),
                pltpu.VMEM((n, width), BF16),
                pltpu.VMEM((n, width), BF16),
                pltpu.VMEM(slots, BF16),
                pltpu.VMEM(slots, BF16),
                pltpu.VMEM((width, n), BF16),
                pltpu.VMEM((n, width), BF16),
                pltpu.VMEM((n, width), F32),
                pltpu.VMEM((2, width // 2, n), BF16),
                pltpu.VMEM((2, n, TILE), F32),
                pltpu.VMEM((2, width, TILE), BF16),
                pltpu.VMEM((2, TILE, width), BF16),
                pltpu.VMEM((n, TILE), BF16),
                pltpu.VMEM((3, share, TILE), F32),
                pltpu.VMEM((2, TILE, share), BF16),
                pltpu.VMEM((CHUNK, width), BF16),
                pltpu.VMEM((n, 8), F32),
                pltpu.VMEM((8, n), F32),
                pltpu.VMEM((8, n), F32),
                pltpu.VMEM((experts, n), F32),
                pltpu.VMEM((1, hid), F32),
                pltpu.VMEM((48, 128), F32),
                pltpu.VMEM((3 * experts, width), F32),
                pltpu.VMEM((4, 48, 128), F32), pltpu.VMEM((4, 4, 48, 128), F32),
                pltpu.VMEM((4, 16, width), F32), pltpu.VMEM((4, 4, 16, width), F32),
                dma((2 * tiles, 12)), dma((2 * tiles, 12)), dma((2 * tiles,)), pltpu.SemaphoreType.REGULAR((tiles, 6)),
                dma((others,)), dma((others,)), dma((others, 3)), dma((others, 3)),
                dma((others,)), dma((others,)), dma((others,)), dma((others,)),
                dma((2,)), dma((2,)), dma, dma((2,)), dma((2,)), dma((3,)), dma((2,)), dma((2,)), dma((2,)),
                dma((4, 3)), dma((4, 3)), dma((4, 3)), dma((4, 3)),
            ],
            compiler_params=pltpu.CompilerParams(collective_id=1, has_side_effects=True, vmem_limit_bytes=67_000_000),
            cost_estimate=cost(6 * mm, 6 * n * hid), name="block",
        )(ids, prio, mod, x, dy, router_t, w_in, b_in, w_out, b_out)

        d_x, d_w_in, d_w_out, out, d_router, d_b_in, d_b_out, aux = pl.pallas_call(
            final_kernel,
            out_shape=(
                shape((n, width), BF16), shape((width, hid), BF16), shape((hid, width), BF16), shape((n, width), BF16),
                shape((experts, width), F32), shape((1, hid), BF16), shape((1, width), BF16), shape((1, 1), F32),
            ),
            in_specs=vmem(2) + [anywhere] + vmem(3) + [anywhere] * 2,
            out_specs=(*[anywhere] * 4, *vmem(3), pl.BlockSpec(memory_space=pltpu.SMEM)),
            scratch_shapes=[
                pltpu.VMEM((2 * tiles, 4, 4, 3, 16, TILE), BF16),
                pltpu.VMEM((n, width), BF16), pltpu.VMEM((n, width), BF16), pltpu.VMEM((n, width), BF16),
                dma((2 * tiles, 3)), dma((2 * tiles,)), dma, dma((2,)), dma((n // CHUNK,)),
            ],
            compiler_params=pltpu.CompilerParams(vmem_limit_bytes=40_000_000),
            cost_estimate=cost(2 * n * n * width, 8 * width * hid), name="final",
        )(slot, d_log, d_back.reshape(n, width), router_t, small, loss, summed, out)
        return out, aux[0, 0], d_x, jnp.transpose(d_router), d_w_in[None], d_b_in, d_w_out[None], d_b_out

    return jax.shard_map(
        local_step,
        mesh=mesh,
        in_specs=(token_spec, token_spec, P(), token_spec, token_spec, expert_spec, expert_spec, expert_spec, expert_spec, token_spec),
        out_specs=(token_spec, P(), token_spec, P(), expert_spec, expert_spec, expert_spec, expert_spec),
        check_vma=False,
    )
```

time: 957 us -> 282 us (0.29)
  blocking collectives: 576 us -> 0 us
  Pallas kernels: 0 us -> 268 us
  local copies, waits for them, and re-layouts: 138 us -> 10.1 us
  matrix products: 99.3 us -> 0 us
  other arithmetic: 88.5 us -> 0 us
  waiting for transfers between devices: 29.9 us -> 0 us
  starting transfers between devices: 17.7 us -> 0 us
    psum x3 -> x0, blocking collectives: 576 us -> none  [the longest x1 411 us: local_step(): expert_grads = lax.psum((d_w_in, d_b_in, d_w_out, d_b_out), 'dp')]
    pallas_call x0 -> x2, Pallas kernels: none -> 268 us  [the longest x1 256 us: local_step(): pl.pallas_call(block_kernel, out_shape=(shape((2 * tiles, 4, 4, 16, width...]
    dot_general x13 -> x0, matrix products: 99.3 us -> none  [the longest x1 23.5 us: local_step(): jnp.einsum('ecw,efw->ecf', d_recv, w_out, preferred_element_type=jnp.floa...]
    convert_element_type x2 -> x0, local copies, waits for them, and re-layouts: 67.5 us -> none  [the longest x1 33.9 us: local_step(): expert_out.astype(jnp.bfloat16)]
    unnamed x3 -> x0, other arithmetic: 49.8 us -> none
    gather x7 -> x0, local copies, waits for them, and re-layouts: 40.8 us -> none  [the longest x1 8.83 us: local_step(): d_back.reshape(num_experts * capacity, model_width)[token_slot]]
    all_to_all x4 -> x0, waiting for transfers between devices: 29.9 us -> none  [the longest x1 29.9 us: local_step(): recv_rows = lax.all_to_all(send_rows, 'ep', 0, 1, tiled=True)]
    unnamed x33 -> x16, local copies, waits for them, and re-layouts: 29.6 us -> 10.1 us
  transfers between devices with their start and end apart: 4 -> 0, of which waited for: 1 -> 0; matrix products, arithmetic and copies ran while one was open for 2% -> 0% of each run, Pallas kernels for 0% -> 0%
where the time goes in v4:
time: 282 us; the launch traced here: 279 us
  Pallas kernels  268 us (95%)
  local copies, waits for them, and re-layouts  10.1 us (4%)
    pallas_call x1, Pallas kernels, local_step(): pl.pallas_call(block_kernel, out_shape=(shape((2 * tiles, 4, 4, 16, width...  256 us
    pallas_call x1, Pallas kernels, local_step(): pl.pallas_call(final_kernel, out_shape=(shape((n, width), BF16), shape((w...  12.2 us
    unnamed x16, local copies, waits for them, and re-layouts  10.1 us

profile of v4, /device:TPU:0, one launch (start us, length us, event | category | flops | bytes accessed | tf_op | source)
XLA Modules:
  0.0 279.2 jit_solution(11802828936909521668)
XLA Ops:
  0.6 0.0 copy-start.6
  0.6 256.0 %block.1 = (bf16[24,4,4,16,768]{4,3,2,1,0:T(8,128)(2,1)}, bf16[8,192,768]{2,1,0:T(8,128)(2,1)}, bf16[8,192,768]{2,1,0:T(8,128)(2,1)}, bf16[1536,768]{1,0:T(8,128...) custom-call(s32[12,128]{1,0:T(8,128)} %bitcast.19, ...), custom_call_target="tpu_custom_call" | custom-call | flops 43486543872 | bytes 28311552 | tf_op jit(solution)/shard_map/block/pallas_call | solution.py:739
  256.7 0.0 copy-done.6
  256.7 0.0 copy-start
  256.7 3.7 %copy-done = bf16[24,4,4,16,768]{4,3,2,1,0:T(8,128)(2,1)S(1)} copy-done((bf16[24,4,4,16,768]{4,3,2,1,0:T(8,128)(2,1)S(1)}, bf16[24,4,4,16,768]{4,3,2,1,0:T(8,128)(2,1)}, u32[]{:S(2)}) %copy-start) | copy-done | bytes 9437208
  260.4 0.0 copy-start.1
  260.4 1.7 copy-done.1
  262.1 0.0 copy-start.2
  262.1 1.7 copy-done.2
  263.7 0.0 copy-start.3
  263.7 0.8 copy-done.3
  264.5 0.0 copy-start.4
  264.5 0.8 copy-done.4
  265.3 0.0 copy-start.5
  265.3 0.8 copy-done.5
  266.1 0.0 copy-start.7
  266.1 0.7 copy-done.7
  266.8 12.2 %final.1 = (bf16[1536,768]{1,0:T(8,128)(2,1)}, bf16[768,3072]{1,0:T(8,128)(2,1)}, bf16[3072,768]{1,0:T(8,128)(2,1)}, bf16[1536,768]{1,0:T(8,128)(2,1)}, f32[8,76...) custom-call(f32[8,1536]{1,0:T(8,128)S(1)} %copy-done.3, ...), custom_call_target="tpu_custom_call" | custom-call | flops 3623878656 | bytes 18874368 | tf_op jit(solution)/shard_map/final/pallas_call | solution.py:787
Async XLA Ops:
  0.6 256.0 %copy-start.6 = (f32[768,8]{0,1:T(8,128)S(1)}, f32[768,8]{0,1:T(8,128)}, u32[]{:S(2)}) copy-start(f32[768,8]{0,1:T(8,128)} %param.12) | copy-start | bytes 73732
  256.7 3.7 %copy-start = (bf16[24,4,4,16,768]{4,3,2,1,0:T(8,128)(2,1)S(1)}, bf16[24,4,4,16,768]{4,3,2,1,0:T(8,128)(2,1)}, u32[]{:S(2)}) copy-start(bf16[24,4,4,16,768]{4,3,2,1,0:T(8,128)(2,1)} %get-tuple-element.28.summed) | copy-start | bytes 28311556
  260.4 1.7 copy-start.1
  262.1 1.7 copy-start.2
  263.7 0.8 copy-start.3
  264.5 0.8 copy-start.4
  265.3 0.8 copy-start.5
  266.1 0.7 copy-start.7

commit v5 on v4

--- a/solution.py
+++ b/solution.py
@@ -14,6 +14,7 @@
 NOWHERE = -1.0
 TILE = 256
 CHUNK = 256
+WIDE = 768
 
 
 def col_of(row):
@@ -63,10 +64,10 @@
 def block_kernel(
     ids_ref, prio_ref, mod_ref, x_any, dy_any, router_ref, w_in, b_in_ref, w_out, b_out_ref,
     summed, back_y, back_d, out, hidden_t, pre_act, slot_row, d_log_ref, loss_ref, small_ref,
-    part_sum, land_a, land_b, own, x_buf, dy_buf, out_x, rows, rows_t, tok, acc, hidbuf, sbuf, ibuf, obuf, act, abuf, hbuf, stage,
+    part_sum, land_a, land_b, own, x_buf, dy_buf, out_x, rows, rows_t, tok, acc, wbuf, sbuf, act, hbuf, stage, late,
     keycol, ids_row, mod_row, logp_ref, db_in, stats_ref, d_router, stat_work, stat_bufs, small_work, small_bufs,
     send_sem, recv_sem, own_sem, credit, x_send, x_recv, d_send, d_recv, y_send, y_recv, g_send, g_recv,
-    self_sem, tok_sem, out_sem, i_sem, o_sem, a_sem, h_sem, hid_sem, s_sem, stat_send, stat_recv, small_send, small_recv,
+    self_sem, tok_sem, out_sem, i_sem, o_sem, a_sem, h_sem, hid_sem, s_sem, late_sem, stat_send, stat_recv, small_send, small_recv,
 ):
     dp = lax.axis_index("dp")
     ep = lax.axis_index("ep")
@@ -79,7 +80,10 @@
     n = experts * capacity
     pairs = experts // 2
     share = n // pairs
-    steps = pairs * half
+    fwd_tiles = hidden_t.shape[1] // WIDE
+    steps = pairs * fwd_tiles
+    groups = part_sum.reshape(tiles * 16, 16, width)
+    late_from = tiles - late.shape[0]
     others = experts - 1
     out_d = x_buf.reshape(out_x.shape)
     tok_slots = tok.reshape(out_x.shape)
@@ -196,13 +200,13 @@
 
     def load_i(it):
         slot = lax.rem(it, 2)
-        at = pl.ds(pl.multiple_of(lax.rem(it, half) * TILE, TILE), TILE)
-        return pltpu.make_async_copy(w_in.at[:, at], ibuf.at[slot], i_sem.at[slot])
+        at = pl.ds(pl.multiple_of(lax.rem(it, fwd_tiles) * WIDE, WIDE), WIDE)
+        return pltpu.make_async_copy(w_in.at[:, at], wbuf.at[slot], i_sem.at[slot])
 
     def load_o(it):
         slot = lax.rem(it, 2)
-        at = pl.ds(pl.multiple_of(lax.rem(it, half) * TILE, TILE), TILE)
-        return pltpu.make_async_copy(w_out.at[at], obuf.at[slot], o_sem.at[slot])
+        at = pl.ds(pl.multiple_of(lax.rem(it, fwd_tiles) * WIDE, WIDE), WIDE)
+        return pltpu.make_async_copy(w_out.at[at], wbuf.at[2 + slot], o_sem.at[slot])
 
     load_x.wait()
     enter()
@@ -248,31 +252,33 @@
     small_work[0] = jnp.zeros(small_work.shape[1:], F32)
 
     def origin(it):
-        return wrap(xx - hops(it // half))
+        return wrap(xx - hops(it // fwd_tiles))
 
     def store_a(it):
         slot = lax.rem(it, 3)
-        at = pl.ds(pl.multiple_of(origin(it) * share, share), share)
-        return pltpu.make_async_copy(abuf.at[slot], pre_act.at[lax.rem(it, half), at], a_sem.at[slot])
+        at = pl.ds(pl.multiple_of(origin(it) * (share // 16), share // 16), share // 16)
+        return pltpu.make_async_copy(
+            groups.at[pl.ds(slot * (share // 16), share // 16)], pre_act.at[lax.rem(it, fwd_tiles), at], a_sem.at[slot])
 
     def store_h(it):
         slot = lax.rem(it, 2)
-        down = pl.ds(pl.multiple_of(lax.rem(it, half) * TILE, TILE), TILE)
-        at = pl.ds(pl.multiple_of(origin(it) * share, share), share)
-        return pltpu.make_async_copy(hbuf.at[slot], hidden_t.at[down, at], h_sem.at[slot])
+        down = pl.ds(pl.multiple_of(lax.rem(it, fwd_tiles) * WIDE, WIDE), WIDE)
+        at = pl.ds(pl.multiple_of(lax.rem(origin(it), 2) * share, share), share)
+        return pltpu.make_async_copy(hbuf.at[slot], hidden_t.at[origin(it) // 2, down, at], h_sem.at[slot])
 
     def first_matmul(it):
-        at = pl.ds(pl.multiple_of(lax.rem(it, half) * TILE, TILE), TILE)
+        at = pl.ds(pl.multiple_of(lax.rem(it, fwd_tiles) * WIDE, WIDE), WIDE)
         chunk = rows[pl.ds(origin(it) * 2, 2)].reshape(share, width)
-        abuf[lax.rem(it, 3)] = nn(chunk, ibuf[lax.rem(it, 2)]) + b_in_ref[:, at].astype(F32)
+        a = nn(chunk, wbuf[lax.rem(it, 2)]) + b_in_ref[:, at].astype(F32)
+        groups[pl.ds(lax.rem(it, 3) * (share // 16), share // 16)] = a.reshape(share // 16, 16, WIDE)
 
     def rest_of_step(it):
-        a = abuf[lax.rem(it, 3)]
+        a = groups[pl.ds(lax.rem(it, 3) * (share // 16), share // 16)].reshape(share, WIDE)
         t = jnp.tanh(ROOT * (a + CUBIC * (a * a * a)))
         hidden = (a * (0.5 * (1.0 + t))).astype(BF16)
         hbuf[lax.rem(it, 2)] = jnp.transpose(hidden)
         at = pl.ds(pl.multiple_of(origin(it) * share, share), share)
-        acc[at, :] += nn(hidden, obuf[lax.rem(it, 2)])
+        acc[at, :] += nn(hidden, wbuf[2 + lax.rem(it, 2)])
 
     def forward(it, carry):
         nxt = it + 1
@@ -280,9 +286,9 @@
         load_o(it).wait()
         load_o(nxt).start()
 
-        @pl.when(lax.rem(nxt, half) == 0)
+        @pl.when(lax.rem(nxt, fwd_tiles) == 0)
         def _():
-            q = nxt // half
+            q = nxt // fwd_tiles
             x_copy(2 * q - 1).wait_recv()
             x_copy(2 * q).wait_recv()
 
@@ -297,15 +303,15 @@
             store_a(it - 2).wait()
             store_h(it - 2).wait()
 
+        rest_of_step(it)
         first_matmul(nxt)
-        rest_of_step(it)
         store_h(it).start()
-        for k, when in ((2, 4), (3, 8)):
+        for k, when in ((2, 1), (3, 2)):
             @pl.when(it == when)
             def _():
                 stat_step(k)
 
-        @pl.when(it == 9)
+        @pl.when(it == 3)
         def _():
             for s in range(3):
                 for j in range(others):
@@ -338,23 +344,36 @@
 
         return way, pa, pb, along(way), along(-way)
 
-    def send(tile, k):
+    def send(tile, k, end=False):
         way, pa, pb, (next_a, next_b), _ = place(lax.rem(tile, 4))
+        whole = late.at[tile - late_from] if end else summed.at[tile]
         if k < 3:
             src, dst, to = part_sum.at[tile, wrap(pa - way * (k + 1))], land_a.at[lax.rem(tile, half), k], next_a
         elif k < 6:
             src, dst, to = part_sum.at[tile, pa, wrap(pb - way * (k - 2))], land_b.at[lax.rem(tile, half), k - 3], next_b
-        elif k == 6:
-            src, dst, to = own.at[tile], summed.at[tile, pa, pb], next_b
         elif k < 9:
-            src = summed.at[tile, pa, wrap(pb - way * (k - 6))]
+            src = whole.at[pa, wrap(pb - way * (k - 6))]
             dst, to = src, next_b
+            if k == 6 and not end:
+                src = own.at[tile]
         else:
-            src = summed.at[tile, wrap(pa - way * (k - 9))]
+            src = whole.at[wrap(pa - way * (k - 9))]
             dst, to = src, next_a
         return pltpu.make_async_remote_copy(
             src_ref=src, dst_ref=dst, send_sem=send_sem.at[tile, k], recv_sem=recv_sem.at[tile, k],
             device_id=(to, ep), device_id_type=MESH)
+
+    def act_on(tile, k, action):
+        if k < 6:
+            action(send(tile, k))
+        else:
+            @pl.when(tile < late_from)
+            def _():
+                action(send(tile, k))
+
+            @pl.when(tile >= late_from)
+            def _():
+                action(send(tile, k, True))
 
     def start(tile, k):
         if k < 6:
@@ -362,16 +381,20 @@
             def _():
                 pl.semaphore_wait(credit.at[tile - half, k], 1)
 
-        send(tile, k).start()
+        act_on(tile, k, lambda copy: copy.start())
 
     def keep(tile):
         way, pa, pb, _, _ = place(lax.rem(tile, 4))
         return pltpu.make_async_copy(own.at[tile], summed.at[tile, pa, pb], own_sem.at[tile])
 
+    def keep_late(tile):
+        spot = tile - late_from
+        return pltpu.make_async_copy(late.at[spot], summed.at[tile], late_sem.at[spot])
+
     def advance(tile, k):
         way, pa, pb, _, (prev_a, prev_b) = place(lax.rem(tile, 4))
         spot = lax.rem(tile, half)
-        send(tile, k - 1).wait_recv()
+        act_on(tile, k - 1, lambda copy: copy.wait_recv())
         if k <= 3:
             block = wrap(pa - way * (k + 1))
             part_sum[tile, block] = part_sum[tile, block] + land_a[spot, k - 1]
@@ -381,10 +404,22 @@
             if k < 6:
                 part_sum[tile, pa, block] = total
             else:
-                own[tile] = total.astype(BF16)
-                keep(tile).start()
+                @pl.when(tile < late_from)
+                def _():
+                    own[tile] = total.astype(BF16)
+                    keep(tile).start()
+
+                @pl.when(tile >= late_from)
+                def _():
+                    late[tile - late_from, pa, pb] = total.astype(BF16)
         elif k == 9:
-            keep(tile).wait()
+            @pl.when(tile < late_from)
+            def _():
+                keep(tile).wait()
+        elif k == 12:
+            @pl.when(tile >= late_from)
+            def _():
+                keep_late(tile).start()
         if k <= 6:
             back_to = prev_a if k <= 3 else prev_b
 
@@ -419,22 +454,26 @@
                 part_sum[tile, a, b, :, j * TILE:(j + 1) * TILE] = grad[at:at + 16, :]
 
     def load_hid(i):
+        base = 2 * lax.rem(i, 2)
+        at = pl.ds(pl.multiple_of(lax.rem(i, 4) * WIDE, WIDE), WIDE)
+        return [pltpu.make_async_copy(hidden_t.at[h, at], wbuf.at[base + h], hid_sem.at[base + h]) for h in range(2)]
+
+    def load_rest(i):
         slot = lax.rem(i, 2)
-        at = pl.ds(pl.multiple_of(lax.rem(i, 8) * (width // 2), width // 2), width // 2)
-        return pltpu.make_async_copy(hidden_t.at[at], hidbuf.at[slot], hid_sem.at[slot])
-
-    def load_s(i):
-        slot = lax.rem(i, 2)
-        return pltpu.make_async_copy(pre_act.at[i], sbuf.at[slot], s_sem.at[slot])
+        at = pl.ds(pl.multiple_of(i * TILE, TILE), TILE)
+        lanes = pl.ds(pl.multiple_of(lax.rem(i, WIDE // TILE) * TILE, TILE), TILE)
+        return (
+            pltpu.make_async_copy(pre_act.at[i // (WIDE // TILE), :, :, lanes], sbuf.at[slot], s_sem.at[slot]),
+            pltpu.make_async_copy(w_in.at[:, at], wbuf.at[slot, :, pl.ds(0, TILE)], i_sem.at[slot]),
+            pltpu.make_async_copy(w_out.at[at], wbuf.at[2 + slot, pl.ds(0, TILE)], o_sem.at[slot]),
+        )
 
     store_a(last - 1).wait()
     store_a(last).wait()
     store_h(last - 1).wait()
     store_h(last).wait()
-    load_hid(jnp.int32(0)).start()
-    load_s(jnp.int32(0)).start()
-    load_i(0).start()
-    load_o(0).start()
+    for copy in load_hid(jnp.int32(0)):
+        copy.start()
     for j in range(others):
         x_copy(j).wait_send()
     out_x[...] = acc[...].astype(BF16).reshape(out_x.shape)
@@ -449,20 +488,26 @@
                 d_copy(j, unit).wait_recv()
 
         at = pl.ds(pl.multiple_of(unit * TILE, TILE), TILE)
-        for piece in range(2):
-            load_hid(2 * i + piece).wait()
-
-            @pl.when(2 * i + piece + 1 < 2 * half)
-            def _():
-                load_hid(2 * i + piece + 1).start()
-
-            grad = nn(hidbuf[piece], tok[:, at])
-            for a in range(2):
-                place_tile(i, 2 * piece + a, grad[a * (width // 4):(a + 1) * (width // 4)])
+        for copy in load_hid(i):
+            copy.wait()
+
+        @pl.when(i + 1 < half)
+        def _():
+            for copy in load_hid(i + 1):
+                copy.start()
+
+        base = 2 * lax.rem(i, 2)
+        for a in range(2):
+            part = slice(a * (WIDE // 2), (a + 1) * (WIDE // 2))
+            grad = nn(wbuf[base, part, :], tok[0:WIDE, at]) + nn(wbuf[base + 1, part, :], tok[WIDE:, at])
+            for b in range(2):
+                place_tile(i, 2 * a + b, grad[b * (width // 4):(b + 1) * (width // 4)])
         start(i, 0)
         return carry
 
     lax.fori_loop(0, half, out_tile, 0)
+    for copy in load_rest(jnp.int32(0)):
+        copy.start()
     stat_step(4, stats_ref)
     send_y = exchange(out_x, back_y, y_send, y_recv)
     for copy in send_y:
@@ -479,19 +524,19 @@
         g = i + half
         wave(g // 4, lax.rem(g, 4))
         slot = lax.rem(i, 2)
-        for load in (load_s, load_i, load_o):
-            load(i).wait()
+        for copy in load_rest(i):
+            copy.wait()
 
         @pl.when(i + 1 < half)
         def _():
-            for load in (load_s, load_i, load_o):
-                load(i + 1).start()
+            for copy in load_rest(i + 1):
+                copy.start()
 
         total = jnp.zeros((1, TILE), F32)
         for c in range(chunks):
             part = pl.ds(c * size, size)
-            d_hidden = nt(tok[part, :], obuf[slot]).astype(BF16)
-            a = sbuf[slot, part, :]
+            d_hidden = nt(tok[part, :], wbuf[2 + slot, 0:TILE, :]).astype(BF16)
+            a = sbuf[slot, c * (size // 16):(c + 1) * (size // 16)].reshape(size, TILE)
             sq = a * a
             t = jnp.tanh(ROOT * (a + CUBIC * (sq * a)))
             slope = 0.5 * (1.0 + t) + (0.5 * ROOT) * a * (1.0 - t * t) * (1.0 + (3 * CUBIC) * sq)
@@ -499,7 +544,7 @@
             total += jnp.sum(d_act, axis=0, keepdims=True)
             d_act_bf = d_act.astype(BF16)
             act[part, :] = d_act_bf
-            acc[part, :] += nt(d_act_bf, ibuf[slot])
+            acc[part, :] += nt(d_act_bf, wbuf[slot, :, 0:TILE])
         db_in[:, pl.ds(pl.multiple_of(i * TILE, TILE), TILE)] = total
         for a in range(4):
             place_tile(g, a, nn(rows_t[pl.ds(a * (width // 4), width // 4), :], act[...]))
@@ -529,8 +574,8 @@
     def token_loads(i):
         at = pl.ds(pl.multiple_of(i * CHUNK, CHUNK), CHUNK)
         return (
-            pltpu.make_async_copy(dy_any.at[at], obuf.at[0], o_sem.at[0]),
-            pltpu.make_async_copy(x_any.at[at], obuf.at[1], o_sem.at[1]),
+            pltpu.make_async_copy(dy_any.at[at], wbuf.at[2, pl.ds(0, CHUNK)], o_sem.at[0]),
+            pltpu.make_async_copy(x_any.at[at], wbuf.at[3, pl.ds(0, CHUNK)], o_sem.at[1]),
         )
 
     def out_store(i):
@@ -560,14 +605,14 @@
 
         stage[...] = (col_of(gate)[:, 0:1] * y_tok).astype(BF16)
         out_store(i).start()
-        d_gate = row_of(jnp.sum(obuf[0].astype(F32) * y_tok, axis=1, keepdims=True))[0:1]
+        d_gate = row_of(jnp.sum(wbuf[2, 0:CHUNK, :].astype(F32) * y_tok, axis=1, keepdims=True))[0:1]
         is_text = mod_row[:, lanes] == 1.0
         global_part = jnp.where(is_text, terms[1][:, 0:1], terms[0][:, 0:1])
         inv_count = jnp.where(is_text, inv[1][:, 0:1], inv[0][:, 0:1])
         d_probs = onehot * d_gate + global_part - logp * inv_count
         d_log = probs * (d_probs - jnp.sum(d_probs * probs, axis=0, keepdims=True))
         d_log_ref[:, lanes] = d_log
-        d_router[...] += nn(jnp.concatenate(split3(d_log), axis=0), obuf[1])
+        d_router[...] += nn(jnp.concatenate(split3(d_log), axis=0), wbuf[3, 0:CHUNK, :])
 
         @pl.when(i + 1 < pieces)
         def _():
@@ -591,7 +636,7 @@
     out_store(jnp.int32(pieces - 1)).wait()
     small_work[0, 0:experts, :] = d_router[0:experts] + d_router[experts:2 * experts] + d_router[2 * experts:]
 
-    def late(t, carry):
+    def tail(t, carry):
         def streams(s, inner):
             wave(t, s)
             return inner
@@ -600,14 +645,14 @@
 
     small_step(0)
     for k in range(1, 4):
-        lax.fori_loop(first + k - 1, first + k, late, 0)
+        lax.fori_loop(first + k - 1, first + k, tail, 0)
         small_step(k)
-    lax.fori_loop(first + 3, units + 12, late, 0)
+    lax.fori_loop(first + 3, units + 12, tail, 0)
     small_step(4, small_ref)
 
     def drain(tile, carry):
         for k in range(12):
-            send(tile, k).wait_send()
+            act_on(tile, k, lambda copy: copy.wait_send())
         return carry
 
     lax.fori_loop(0, tiles, drain, 0)
@@ -619,6 +664,8 @@
     for copy in send_g:
         copy.wait()
     self_g.wait()
+    for i in range(late.shape[0]):
+        keep_late(jnp.int32(late_from + i)).wait()
 
 
 def global_terms(stats, experts):
@@ -740,7 +787,7 @@
             block_kernel,
             out_shape=(
                 shape((2 * tiles, 4, 4, 16, width), BF16), shape(slots, BF16), shape(slots, BF16), shape((n, width), BF16),
-                shape((hid, n), BF16), shape((tiles, n, TILE), F32),
+                shape((n // WIDE, hid, WIDE), BF16), shape((hid // WIDE, n // 16, 16, WIDE), F32),
                 shape((8, n), F32), shape((experts, n), F32), shape((8, 128), F32), shape((16, width), F32),
             ),
             in_specs=vmem(3) + [anywhere] * 2 + vmem(1) + [anywhere] + vmem(1) + [anywhere] + vmem(1),
@@ -757,14 +804,12 @@
                 pltpu.VMEM((width, n), BF16),
                 pltpu.VMEM((n, width), BF16),
                 pltpu.VMEM((n, width), F32),
-                pltpu.VMEM((2, width // 2, n), BF16),
-                pltpu.VMEM((2, n, TILE), F32),
-                pltpu.VMEM((2, width, TILE), BF16),
-                pltpu.VMEM((2, TILE, width), BF16),
+                pltpu.VMEM((4, WIDE, WIDE), BF16),
+                pltpu.VMEM((2, n // 16, 16, TILE), F32),
                 pltpu.VMEM((n, TILE), BF16),
-                pltpu.VMEM((3, share, TILE), F32),
-                pltpu.VMEM((2, TILE, share), BF16),
+                pltpu.VMEM((2, WIDE, share), BF16),
                 pltpu.VMEM((CHUNK, width), BF16),
+                pltpu.VMEM((4, 4, 4, 16, width), BF16),
                 pltpu.VMEM((n, 8), F32),
                 pltpu.VMEM((8, n), F32),
                 pltpu.VMEM((8, n), F32),
@@ -777,7 +822,7 @@
                 dma((2 * tiles, 12)), dma((2 * tiles, 12)), dma((2 * tiles,)), pltpu.SemaphoreType.REGULAR((tiles, 6)),
                 dma((others,)), dma((others,)), dma((others, 3)), dma((others, 3)),
                 dma((others,)), dma((others,)), dma((others,)), dma((others,)),
-                dma((2,)), dma((2,)), dma, dma((2,)), dma((2,)), dma((3,)), dma((2,)), dma((2,)), dma((2,)),
+                dma((2,)), dma((2,)), dma, dma((2,)), dma((2,)), dma((3,)), dma((2,)), dma((4,)), dma((2,)), dma((4,)),
                 dma((4, 3)), dma((4, 3)), dma((4, 3)), dma((4, 3)),
             ],
             compiler_params=pltpu.CompilerParams(collective_id=1, has_side_effects=True, vmem_limit_bytes=67_000_000),
@@ -797,7 +842,7 @@
                 pltpu.VMEM((n, width), BF16), pltpu.VMEM((n, width), BF16), pltpu.VMEM((n, width), BF16),
                 dma((2 * tiles, 3)), dma((2 * tiles,)), dma, dma((2,)), dma((n // CHUNK,)),
             ],
-            compiler_params=pltpu.CompilerParams(vmem_limit_bytes=40_000_000),
+            compiler_params=pltpu.CompilerParams(vmem_limit_bytes=66_000_000),
             cost_estimate=cost(2 * n * n * width, 8 * width * hid), name="final",
         )(slot, d_log, d_back.reshape(n, width), router_t, small, loss, summed, out)
         return out, aux[0, 0], d_x, jnp.transpose(d_router), d_w_in[None], d_b_in, d_w_out[None], d_b_out

time: 282 us -> 240 us (0.85)
  Pallas kernels: 268 us -> 237 us
  local copies, waits for them, and re-layouts: 10.1 us -> 0 us
    pallas_call x1, Pallas kernels: 256 us -> 223 us  [local_step(): pl.pallas_call(block_kernel, out_shape=(shape((2 * tiles, 4, 4, 16, width...]
    unnamed x16 -> x0, local copies, waits for them, and re-layouts: 10.1 us -> none
where the time goes in v5:
time: 240 us; the launch traced here: 237 us
  Pallas kernels  237 us (99%)
    pallas_call x1, Pallas kernels, local_step(): pl.pallas_call(block_kernel, out_shape=(shape((2 * tiles, 4, 4, 16, width...  223 us
    pallas_call x1, Pallas kernels, local_step(): pl.pallas_call(final_kernel, out_shape=(shape((n, width), BF16), shape((w...  13.7 us

profile of v5, /device:TPU:0, one launch (start us, length us, event | category | flops | bytes accessed | tf_op | source)
XLA Modules:
  0.0 237.3 jit_solution(5294744888470616903)
XLA Ops:
  0.6 222.9 %block.1 = (bf16[24,4,4,16,768]{4,3,2,1,0:T(8,128)(2,1)}, bf16[8,192,768]{2,1,0:T(8,128)(2,1)}, bf16[8,192,768]{2,1,0:T(8,128)(2,1)}, bf16[1536,768]{1,0:T(8,128...) custom-call(s32[12,128]{1,0:T(8,128)} %bitcast.19, ...), custom_call_target="tpu_custom_call" | custom-call | flops 43486543872 | bytes 28311552 | tf_op jit(solution)/shard_map/block/pallas_call | solution.py:786
  223.5 13.7 %final.1 = (bf16[1536,768]{1,0:T(8,128)(2,1)}, bf16[768,3072]{1,0:T(8,128)(2,1)}, bf16[3072,768]{1,0:T(8,128)(2,1)}, bf16[1536,768]{1,0:T(8,128)(2,1)}, f32[8,76...) custom-call(f32[8,1536]{1,0:T(8,128)} %get-tuple-element.23.slot_ref, ...), custom_call_target="tpu_custom_call" | custom-call | flops 3623878656 | bytes 18874368 | tf_op jit(solution)/shard_map/final/pallas_call | solution.py:832

commit v6 on v5

--- a/solution.py
+++ b/solution.py
@@ -66,8 +66,8 @@
     summed, back_y, back_d, out, hidden_t, pre_act, slot_row, d_log_ref, loss_ref, small_ref,
     part_sum, land_a, land_b, own, x_buf, dy_buf, out_x, rows, rows_t, tok, acc, wbuf, sbuf, act, hbuf, stage, late,
     keycol, ids_row, mod_row, logp_ref, db_in, stats_ref, d_router, stat_work, stat_bufs, small_work, small_bufs,
-    send_sem, recv_sem, own_sem, credit, x_send, x_recv, d_send, d_recv, y_send, y_recv, g_send, g_recv,
-    self_sem, tok_sem, out_sem, i_sem, o_sem, a_sem, h_sem, hid_sem, s_sem, late_sem, stat_send, stat_recv, small_send, small_recv,
+    send_sem, sum_sem, recv_sem, own_sem, credit, x_send, x_recv, d_send, d_recv, y_send, y_recv, g_send, g_recv,
+    self_sem, tok_sem, out_sem, i_sem, o_sem, a_sem, h_sem, hid_sem, s_sem, late_sem, stat_send, stat_recv,
 ):
     dp = lax.axis_index("dp")
     ep = lax.axis_index("ep")
@@ -156,7 +156,7 @@
         return step
 
     stat_step = small_sum(stat_work, stat_bufs, 48, stat_send, stat_recv)
-    small_step = small_sum(small_work, small_bufs, experts, small_send, small_recv)
+    small_step = small_sum(small_work, small_bufs, experts, stat_send, stat_recv)
 
     ids = wide(ids_ref)
     key = ids * n + wide(prio_ref)
@@ -188,14 +188,14 @@
     def x_copy(j):
         to = target(j)
         return pltpu.make_async_remote_copy(
-            src_ref=out_x.at[to], dst_ref=rows.at[ep], send_sem=x_send.at[j], recv_sem=x_recv.at[j],
+            src_ref=out_x.at[to], dst_ref=rows.at[ep], send_sem=x_send, recv_sem=x_recv.at[j],
             device_id=(dp, to), device_id_type=MESH)
 
     def d_copy(j, s):
         to = target(j)
         at = pl.ds(pl.multiple_of(s * TILE, TILE), TILE)
         return pltpu.make_async_remote_copy(
-            src_ref=out_d.at[to, :, at], dst_ref=tok_slots.at[ep, :, at], send_sem=d_send.at[j, s], recv_sem=d_recv.at[j, s],
+            src_ref=out_d.at[to, :, at], dst_ref=tok_slots.at[ep, :, at], send_sem=d_send, recv_sem=d_recv.at[j, s],
             device_id=(dp, to), device_id_type=MESH)
 
     def load_i(it):
@@ -207,6 +207,9 @@
         slot = lax.rem(it, 2)
         at = pl.ds(pl.multiple_of(lax.rem(it, fwd_tiles) * WIDE, WIDE), WIDE)
         return pltpu.make_async_copy(w_out.at[at], wbuf.at[2 + slot], o_sem.at[slot])
+
+    def all_sent(sem):
+        pltpu.make_async_copy(out_x.at[pl.ds(0, others)], out_x.at[pl.ds(0, others)], sem).wait()
 
     load_x.wait()
     enter()
@@ -360,8 +363,13 @@
             src = whole.at[wrap(pa - way * (k - 9))]
             dst, to = src, next_a
         return pltpu.make_async_remote_copy(
-            src_ref=src, dst_ref=dst, send_sem=send_sem.at[tile, k], recv_sem=recv_sem.at[tile, k],
+            src_ref=src, dst_ref=dst, send_sem=send_sem.at[tile],
+            recv_sem=sum_sem.at[lax.rem(tile, half), k] if k < 6 else recv_sem.at[tile, k - 6],
             device_id=(to, ep), device_id_type=MESH)
+
+    def sent(tile):
+        count = 3 * (5 * 16 + 5 * 8)
+        return pltpu.make_async_copy(acc.at[pl.ds(0, count)], acc.at[pl.ds(count, count)], send_sem.at[tile])
 
     def act_on(tile, k, action):
         if k < 6:
@@ -379,13 +387,13 @@
         if k < 6:
             @pl.when(tile >= half)
             def _():
-                pl.semaphore_wait(credit.at[tile - half, k], 1)
+                pl.semaphore_wait(credit.at[tile - half, k // 3], 1)
 
         act_on(tile, k, lambda copy: copy.start())
 
     def keep(tile):
         way, pa, pb, _, _ = place(lax.rem(tile, 4))
-        return pltpu.make_async_copy(own.at[tile], summed.at[tile, pa, pb], own_sem.at[tile])
+        return pltpu.make_async_copy(own.at[tile], summed.at[tile, pa, pb], own_sem.at[lax.rem(tile, half)])
 
     def keep_late(tile):
         spot = tile - late_from
@@ -425,25 +433,35 @@
 
             @pl.when(tile < half)
             def _():
-                pl.semaphore_signal(credit.at[tile, k - 1], inc=1, device_id=(back_to, ep), device_id_type=MESH)
+                pl.semaphore_signal(credit.at[tile, (k - 1) // 3], inc=1, device_id=(back_to, ep), device_id_type=MESH)
 
         if k < 12:
             start(tile, k)
 
-    def wave(t, stream):
-        for k in range(12, 0, -1):
+    def wave(t, ages):
+        for k in ages:
             unit = t - k
 
             @pl.when(jnp.logical_and(unit >= 0, unit < units))
             def _():
-                advance(unit * 4 + stream, k)
+                def streams(stream, carry):
+                    advance(unit * 4 + stream, k)
+                    return carry
+
+                lax.fori_loop(0, 4, streams, 0)
+
+    def quarter(t, stream):
+        for p, ages in enumerate(((6, 5), (4, 3), (2,), (1,))):
+            @pl.when(stream == p)
+            def _():
+                wave(t, ages)
 
     def exchange(src, dst, send_sems, recv_sems):
         copies = []
         for j in range(1, experts):
             to = lax.rem(ep + j, experts)
             copies.append(pltpu.make_async_remote_copy(
-                src_ref=src.at[to], dst_ref=dst.at[ep], send_sem=send_sems.at[j - 1], recv_sem=recv_sems.at[j - 1],
+                src_ref=src.at[to], dst_ref=dst.at[ep], send_sem=send_sems, recv_sem=recv_sems.at[j - 1],
                 device_id=(dp, to), device_id_type=MESH))
         return copies
 
@@ -474,13 +492,12 @@
     store_h(last).wait()
     for copy in load_hid(jnp.int32(0)):
         copy.start()
-    for j in range(others):
-        x_copy(j).wait_send()
+    all_sent(x_send)
     out_x[...] = acc[...].astype(BF16).reshape(out_x.shape)
 
     def out_tile(i, carry):
         unit, stream = i // 4, lax.rem(i, 4)
-        wave(unit, stream)
+        quarter(unit, stream)
 
         @pl.when(stream == 0)
         def _():
@@ -497,11 +514,9 @@
                 copy.start()
 
         base = 2 * lax.rem(i, 2)
-        for a in range(2):
-            part = slice(a * (WIDE // 2), (a + 1) * (WIDE // 2))
-            grad = nn(wbuf[base, part, :], tok[0:WIDE, at]) + nn(wbuf[base + 1, part, :], tok[WIDE:, at])
-            for b in range(2):
-                place_tile(i, 2 * a + b, grad[b * (width // 4):(b + 1) * (width // 4)])
+        grad = nn(wbuf[base], tok[0:WIDE, at]) + nn(wbuf[base + 1], tok[WIDE:, at])
+        for a in range(4):
+            place_tile(i, a, grad[a * (width // 4):(a + 1) * (width // 4)])
         start(i, 0)
         return carry
 
@@ -522,7 +537,7 @@
 
     def in_tile(i, carry):
         g = i + half
-        wave(g // 4, lax.rem(g, 4))
+        quarter(g // 4, lax.rem(g, 4))
         slot = lax.rem(i, 2)
         for copy in load_rest(i):
             copy.wait()
@@ -546,8 +561,9 @@
             act[part, :] = d_act_bf
             acc[part, :] += nt(d_act_bf, wbuf[slot, :, 0:TILE])
         db_in[:, pl.ds(pl.multiple_of(i * TILE, TILE), TILE)] = total
+        grad = nn(rows_t[...], act[...])
         for a in range(4):
-            place_tile(g, a, nn(rows_t[pl.ds(a * (width // 4), width // 4), :], act[...]))
+            place_tile(g, a, grad[a * (width // 4):(a + 1) * (width // 4)])
         start(g, 0)
         return carry
 
@@ -620,49 +636,37 @@
                 copy.start()
 
     def rest(t, carry):
-        def streams(s, inner):
-            wave(t, s)
-
-            @pl.when(s == 1)
-            def _():
-                combine(t - units)
-
-            return inner
-
-        return lax.fori_loop(0, 4, streams, carry)
+        wave(t, range(12, 4, -1))
+        combine(t - units)
+        wave(t, range(4, 0, -1))
+        return carry
 
     first = units + pieces
     lax.fori_loop(units, first, rest, 0)
     out_store(jnp.int32(pieces - 1)).wait()
     small_work[0, 0:experts, :] = d_router[0:experts] + d_router[experts:2 * experts] + d_router[2 * experts:]
 
+    small_step(0)
+    for k in range(1, 5):
+        wave(first + k - 1, range(12, 8, -1))
+        small_step(k, small_ref)
+        wave(first + k - 1, range(8, 0, -1))
+
     def tail(t, carry):
-        def streams(s, inner):
-            wave(t, s)
-            return inner
-
-        return lax.fori_loop(0, 4, streams, carry)
-
-    small_step(0)
-    for k in range(1, 4):
-        lax.fori_loop(first + k - 1, first + k, tail, 0)
-        small_step(k)
-    lax.fori_loop(first + 3, units + 12, tail, 0)
-    small_step(4, small_ref)
+        wave(t, range(12, 0, -1))
+        return carry
+
+    lax.fori_loop(first + 4, units + 12, tail, 0)
 
     def drain(tile, carry):
-        for k in range(12):
-            act_on(tile, k, lambda copy: copy.wait_send())
+        sent(tile).wait()
         return carry
 
     lax.fori_loop(0, tiles, drain, 0)
-    for s in range(3):
-        for j in range(others):
-            d_copy(j, s).wait_send()
-    for copy in send_y:
-        copy.wait_send()
+    for sem in (d_send, y_send, g_send):
+        all_sent(sem)
     for copy in send_g:
-        copy.wait()
+        copy.wait_recv()
     self_g.wait()
     for i in range(late.shape[0]):
         keep_late(jnp.int32(late_from + i)).wait()
@@ -692,13 +696,13 @@
     units = tiles // 4
     experts = d_log_ref.shape[0]
     pieces = n // CHUNK
+    per_piece = tiles // pieces
 
     load_back = pltpu.make_async_copy(back_any, back, back_sem)
-    load_back.start()
 
     def loads(t):
         return [
-            pltpu.make_async_copy(summed.at[t, :, :, :, pl.ds(j * TILE, TILE)], buf.at[t, :, :, j], load_sem.at[t, j])
+            pltpu.make_async_copy(summed.at[t, :, :, :, pl.ds(j * TILE, TILE)], buf.at[t, :, :, j], load_sem.at[t])
             for j in range(3)
         ]
 
@@ -712,6 +716,8 @@
         return pltpu.make_async_copy(tile, dst, store_sem.at[t])
 
     for t in range(tiles):
+        if t == per_piece:
+            load_back.start()
         for copy in loads(t):
             copy.start()
     load_out = pltpu.make_async_copy(out_any, out_buf, out_sem.at[0])
@@ -724,13 +730,18 @@
     aux_ref[0, 0] = loss_ref[0, 0]
     r = split3(router_ref[...])
     rights = jnp.concatenate([r[0], r[1], r[0], r[1], r[2], r[0]], axis=0)
-    load_back.wait()
 
     def dx_store(i):
         at = pl.ds(i * CHUNK, CHUNK)
         return pltpu.make_async_copy(dx_buf.at[at], dx.at[at], dx_sem.at[i])
 
-    per_piece = tiles // pieces
+    def move(i):
+        for t in range(i * per_piece, (i + 1) * per_piece):
+            pltpu.make_async_copy(buf.at[t], buf.at[t], load_sem.at[t]).wait()
+            store(t).start()
+
+    move(0)
+    load_back.wait()
     for i in range(pieces):
         lanes = pl.ds(i * CHUNK, CHUNK)
         d = split3(d_log_ref[:, lanes])
@@ -740,10 +751,9 @@
         chosen = (lax.broadcasted_iota(jnp.int32, (CHUNK, n), 1).astype(F32) == slot_col).astype(BF16)
         dx_buf[lanes, :] = (nn(chosen, back[...]) + routed.astype(F32)).astype(BF16)
         dx_store(i).start()
-        for t in range(i * per_piece, (i + 1) * per_piece):
-            for copy in loads(t):
-                copy.wait()
-            store(t).start()
+        for piece in (2 * i + 1, 2 * i + 2):
+            if piece < pieces:
+                move(piece)
     load_out.wait()
     store_out = pltpu.make_async_copy(out_buf, out, out_sem.at[1])
     store_out.start()
@@ -819,11 +829,10 @@
                 pltpu.VMEM((3 * experts, width), F32),
                 pltpu.VMEM((4, 48, 128), F32), pltpu.VMEM((4, 4, 48, 128), F32),
                 pltpu.VMEM((4, 16, width), F32), pltpu.VMEM((4, 4, 16, width), F32),
-                dma((2 * tiles, 12)), dma((2 * tiles, 12)), dma((2 * tiles,)), pltpu.SemaphoreType.REGULAR((tiles, 6)),
-                dma((others,)), dma((others,)), dma((others, 3)), dma((others, 3)),
-                dma((others,)), dma((others,)), dma((others,)), dma((others,)),
+                dma((2 * tiles,)), dma((tiles, 6)), dma((2 * tiles, 6)), dma((tiles,)), pltpu.SemaphoreType.REGULAR((tiles, 2)),
+                dma, dma((others,)), dma, dma((others, 3)), dma, dma((others,)), dma, dma((others,)),
                 dma((2,)), dma((2,)), dma, dma((2,)), dma((2,)), dma((3,)), dma((2,)), dma((4,)), dma((2,)), dma((4,)),
-                dma((4, 3)), dma((4, 3)), dma((4, 3)), dma((4, 3)),
+                dma((4, 3)), dma((4, 3)),
             ],
             compiler_params=pltpu.CompilerParams(collective_id=1, has_side_effects=True, vmem_limit_bytes=67_000_000),
             cost_estimate=cost(6 * mm, 6 * n * hid), name="block",
@@ -840,7 +849,7 @@
             scratch_shapes=[
                 pltpu.VMEM((2 * tiles, 4, 4, 3, 16, TILE), BF16),
                 pltpu.VMEM((n, width), BF16), pltpu.VMEM((n, width), BF16), pltpu.VMEM((n, width), BF16),
-                dma((2 * tiles, 3)), dma((2 * tiles,)), dma, dma((2,)), dma((n // CHUNK,)),
+                dma((2 * tiles,)), dma((2 * tiles,)), dma, dma((2,)), dma((n // CHUNK,)),
             ],
             compiler_params=pltpu.CompilerParams(vmem_limit_bytes=66_000_000),
             cost_estimate=cost(2 * n * n * width, 8 * width * hid), name="final",

time: 240 us -> 228 us (0.950)
  Pallas kernels: 237 us -> 226 us
    pallas_call x1, Pallas kernels: 223 us -> 213 us  [local_step(): pl.pallas_call(block_kernel, out_shape=(shape((2 * tiles, 4, 4, 16, width...]
where the time goes in v6:
time: 228 us; the launch traced here: 227 us
  Pallas kernels  226 us (99%)
    pallas_call x1, Pallas kernels, local_step(): pl.pallas_call(block_kernel, out_shape=(shape((2 * tiles, 4, 4, 16, width...  213 us
    pallas_call x1, Pallas kernels, local_step(): pl.pallas_call(final_kernel, out_shape=(shape((n, width), BF16), shape((w...  12.9 us

profile of v6, /device:TPU:0, one launch (start us, length us, event | category | flops | bytes accessed | tf_op | source)
XLA Modules:
  0.0 226.9 jit_solution(12369258841362383711)
XLA Ops:
  0.6 213.2 %block.1 = (bf16[24,4,4,16,768]{4,3,2,1,0:T(8,128)(2,1)}, bf16[8,192,768]{2,1,0:T(8,128)(2,1)}, bf16[8,192,768]{2,1,0:T(8,128)(2,1)}, bf16[1536,768]{1,0:T(8,128...) custom-call(s32[12,128]{1,0:T(8,128)} %bitcast.19, ...), custom_call_target="tpu_custom_call" | custom-call | flops 43486543872 | bytes 28311552 | tf_op jit(solution)/shard_map/block/pallas_call | solution.py:796
  213.8 12.9 %final.1 = (bf16[1536,768]{1,0:T(8,128)(2,1)}, bf16[768,3072]{1,0:T(8,128)(2,1)}, bf16[3072,768]{1,0:T(8,128)(2,1)}, bf16[1536,768]{1,0:T(8,128)(2,1)}, f32[8,76...) custom-call(f32[8,1536]{1,0:T(8,128)} %get-tuple-element.23.slot_ref, ...), custom_call_target="tpu_custom_call" | custom-call | flops 3623878656 | bytes 18874368 | tf_op jit(solution)/shard_map/final/pallas_call | solution.py:841

commit v7 on v6

--- a/solution.py
+++ b/solution.py
@@ -371,6 +371,18 @@
         count = 3 * (5 * 16 + 5 * 8)
         return pltpu.make_async_copy(acc.at[pl.ds(0, count)], acc.at[pl.ds(count, count)], send_sem.at[tile])
 
+    def direct(tile):
+        way, pa, _, _, _ = place(lax.rem(tile, 4))
+        first_z = lax.rem(tile, 4) // 2
+        row = late.at[tile - late_from, pa]
+        copies = []
+        for m, move in enumerate((way, -way, 2 * way)):
+            to = (z * 4 + wrap(yy + move)) * (1 - first_z) + (wrap(z + move) * 4 + yy) * first_z
+            copies.append(pltpu.make_async_remote_copy(
+                src_ref=row, dst_ref=row, send_sem=send_sem.at[tile], recv_sem=recv_sem.at[tile, 3 + m],
+                device_id=(to, ep), device_id_type=MESH))
+        return copies
+
     def act_on(tile, k, action):
         if k < 6:
             action(send(tile, k))
@@ -402,6 +414,22 @@
     def advance(tile, k):
         way, pa, pb, _, (prev_a, prev_b) = place(lax.rem(tile, 4))
         spot = lax.rem(tile, half)
+        if k >= 10:
+            @pl.when(tile < late_from)
+            def _():
+                send(tile, k - 1).wait_recv()
+                if k < 12:
+                    send(tile, k).start()
+
+            if k == 10:
+                @pl.when(tile >= late_from)
+                def _():
+                    for copy in direct(tile):
+                        copy.wait_recv()
+                    keep_late(tile).start()
+
+            return
+
         act_on(tile, k - 1, lambda copy: copy.wait_recv())
         if k <= 3:
             block = wrap(pa - way * (k + 1))
@@ -424,10 +452,12 @@
             @pl.when(tile < late_from)
             def _():
                 keep(tile).wait()
-        elif k == 12:
+                send(tile, 9).start()
+
             @pl.when(tile >= late_from)
             def _():
-                keep_late(tile).start()
+                for copy in direct(tile):
+                    copy.start()
         if k <= 6:
             back_to = prev_a if k <= 3 else prev_b
 
@@ -435,7 +465,7 @@
             def _():
                 pl.semaphore_signal(credit.at[tile, (k - 1) // 3], inc=1, device_id=(back_to, ep), device_id_type=MESH)
 
-        if k < 12:
+        if k < 9:
             start(tile, k)
 
     def wave(t, ages):
@@ -565,8 +595,17 @@
         for a in range(4):
             place_tile(g, a, grad[a * (width // 4):(a + 1) * (width // 4)])
         start(g, 0)
+
+        @pl.when(i == half - 2)
+        def _():
+            for copy in send_y:
+                copy.wait_recv()
+            self_y.wait()
+            back.start()
+
         return carry
 
+    back = pltpu.make_async_copy(back_y, dy_buf.reshape(back_y.shape), tok_sem.at[1])
     lax.fori_loop(0, half, in_tile, 0)
 
     rows[...] = acc[...].astype(BF16).reshape(rows.shape)
@@ -576,11 +615,6 @@
     self_g = pltpu.make_async_copy(rows.at[ep], back_d.at[ep], self_sem.at[1])
     self_g.start()
 
-    for copy in send_y:
-        copy.wait_recv()
-    self_y.wait()
-    back = pltpu.make_async_copy(back_y, dy_buf.reshape(back_y.shape), tok_sem.at[1])
-    back.start()
     for i in range(4):
         small_work[0, 8 + i:9 + i, :] = db_in[:, i * width:(i + 1) * width]
     d_router[...] = jnp.zeros_like(d_router)
@@ -656,7 +690,7 @@
         wave(t, range(12, 0, -1))
         return carry
 
-    lax.fori_loop(first + 4, units + 12, tail, 0)
+    lax.fori_loop(first + 4, units + 11, tail, 0)
 
     def drain(tile, carry):
         sent(tile).wait()
@@ -695,10 +729,12 @@
     half = tiles // 2
     units = tiles // 4
     experts = d_log_ref.shape[0]
-    pieces = n // CHUNK
-    per_piece = tiles // pieces
+    chunk = 2 * CHUNK
+    pieces = n // chunk
+    per_piece = tiles // (2 * pieces)
 
     load_back = pltpu.make_async_copy(back_any, back, back_sem)
+    load_back.start()
 
     def loads(t):
         return [
@@ -716,8 +752,6 @@
         return pltpu.make_async_copy(tile, dst, store_sem.at[t])
 
     for t in range(tiles):
-        if t == per_piece:
-            load_back.start()
         for copy in loads(t):
             copy.start()
     load_out = pltpu.make_async_copy(out_any, out_buf, out_sem.at[0])
@@ -732,7 +766,7 @@
     rights = jnp.concatenate([r[0], r[1], r[0], r[1], r[2], r[0]], axis=0)
 
     def dx_store(i):
-        at = pl.ds(i * CHUNK, CHUNK)
+        at = pl.ds(i * chunk, chunk)
         return pltpu.make_async_copy(dx_buf.at[at], dx.at[at], dx_sem.at[i])
 
     def move(i):
@@ -740,20 +774,18 @@
             pltpu.make_async_copy(buf.at[t], buf.at[t], load_sem.at[t]).wait()
             store(t).start()
 
-    move(0)
     load_back.wait()
     for i in range(pieces):
-        lanes = pl.ds(i * CHUNK, CHUNK)
+        lanes = pl.ds(i * chunk, chunk)
         d = split3(d_log_ref[:, lanes])
         lefts = jnp.concatenate([d[0], d[0], d[1], d[1], d[0], d[2]], axis=0)
         routed = tn(lefts, rights).astype(BF16)
         slot_col = col_of(slot_ref[0:1, lanes])[:, 0:1]
-        chosen = (lax.broadcasted_iota(jnp.int32, (CHUNK, n), 1).astype(F32) == slot_col).astype(BF16)
+        chosen = (lax.broadcasted_iota(jnp.int32, (chunk, n), 1).astype(F32) == slot_col).astype(BF16)
         dx_buf[lanes, :] = (nn(chosen, back[...]) + routed.astype(F32)).astype(BF16)
         dx_store(i).start()
-        for piece in (2 * i + 1, 2 * i + 2):
-            if piece < pieces:
-                move(piece)
+        move(2 * i)
+        move(2 * i + 1)
     load_out.wait()
     store_out = pltpu.make_async_copy(out_buf, out, out_sem.at[1])
     store_out.start()
@@ -849,7 +881,7 @@
             scratch_shapes=[
                 pltpu.VMEM((2 * tiles, 4, 4, 3, 16, TILE), BF16),
                 pltpu.VMEM((n, width), BF16), pltpu.VMEM((n, width), BF16), pltpu.VMEM((n, width), BF16),
-                dma((2 * tiles,)), dma((2 * tiles,)), dma, dma((2,)), dma((n // CHUNK,)),
+                dma((2 * tiles,)), dma((2 * tiles,)), dma, dma((2,)), dma((n // (2 * CHUNK),)),
             ],
             compiler_params=pltpu.CompilerParams(vmem_limit_bytes=66_000_000),
             cost_estimate=cost(2 * n * n * width, 8 * width * hid), name="final",

time: 228 us -> 226 us (level)
    pallas_call x1, Pallas kernels: 213 us -> 211 us  [local_step(): pl.pallas_call(block_kernel, out_shape=(shape((2 * tiles, 4, 4, 16, width...]
where the time goes in v7:
time: 226 us; the launch traced here: 224 us
  Pallas kernels  224 us (99%)
    pallas_call x1, Pallas kernels, local_step(): pl.pallas_call(block_kernel, out_shape=(shape((2 * tiles, 4, 4, 16, width...  211 us
    pallas_call x1, Pallas kernels, local_step(): pl.pallas_call(final_kernel, out_shape=(shape((n, width), BF16), shape((w...  12.7 us

profile of v7, /device:TPU:0, one launch (start us, length us, event | category | flops | bytes accessed | tf_op | source)
XLA Modules:
  0.0 224.4 jit_solution(13769630440821004992)
XLA Ops:
  0.6 210.8 %block.1 = (bf16[24,4,4,16,768]{4,3,2,1,0:T(8,128)(2,1)}, bf16[8,192,768]{2,1,0:T(8,128)(2,1)}, bf16[8,192,768]{2,1,0:T(8,128)(2,1)}, bf16[1536,768]{1,0:T(8,128...) custom-call(s32[12,128]{1,0:T(8,128)} %bitcast.19, ...), custom_call_target="tpu_custom_call" | custom-call | flops 43486543872 | bytes 28311552 | tf_op jit(solution)/shard_map/block/pallas_call | solution.py:828
  211.5 12.7 %final.1 = (bf16[1536,768]{1,0:T(8,128)(2,1)}, bf16[768,3072]{1,0:T(8,128)(2,1)}, bf16[3072,768]{1,0:T(8,128)(2,1)}, bf16[1536,768]{1,0:T(8,128)(2,1)}, f32[8,76...) custom-call(f32[8,1536]{1,0:T(8,128)} %get-tuple-element.23.slot_ref, ...), custom_call_target="tpu_custom_call" | custom-call | flops 3623878656 | bytes 18874368 | tf_op jit(solution)/shard_map/final/pallas_call | solution.py:873

commit v8 on v7

--- a/solution.py
+++ b/solution.py
@@ -195,7 +195,7 @@
         to = target(j)
         at = pl.ds(pl.multiple_of(s * TILE, TILE), TILE)
         return pltpu.make_async_remote_copy(
-            src_ref=out_d.at[to, :, at], dst_ref=tok_slots.at[ep, :, at], send_sem=d_send, recv_sem=d_recv.at[j, s],
+            src_ref=out_d.at[to, :, at], dst_ref=tok_slots.at[ep, :, at], send_sem=d_send, recv_sem=d_recv.at[s],
             device_id=(dp, to), device_id_type=MESH)
 
     def load_i(it):
@@ -214,7 +214,8 @@
     load_x.wait()
     enter()
 
-    def send_x(j, carry):
+    def send_x(i, carry):
+        j = lax.rem(i + 1, others) + jnp.where(i == 1, 1, 0) - jnp.where(i == 2, 1, 0)
         out_x[target(j)] = nn(pick(target(j)), x_buf[...]).astype(BF16)
         x_copy(j).start()
         return carry
@@ -317,7 +318,7 @@
         @pl.when(it == 3)
         def _():
             for s in range(3):
-                for j in range(others):
+                for j in (1, 3, 2, 4, 5, 6, 0):
                     d_copy(j, s).start()
 
         return carry
@@ -327,6 +328,14 @@
     first_matmul(jnp.int32(0))
     lax.fori_loop(0, steps - 1, forward, 0)
     last = jnp.int32(steps - 1)
+
+    def load_hid(i):
+        base = 2 * lax.rem(i, 2)
+        at = pl.ds(pl.multiple_of(lax.rem(i, 4) * WIDE, WIDE), WIDE)
+        return [pltpu.make_async_copy(hidden_t.at[h, at], wbuf.at[base + h], hid_sem.at[base + h]) for h in range(2)]
+
+    for copy in load_hid(jnp.int32(0)):
+        copy.start()
     store_a(last).start()
     load_o(last).wait()
     store_a(last - 2).wait()
@@ -491,7 +500,7 @@
         for j in range(1, experts):
             to = lax.rem(ep + j, experts)
             copies.append(pltpu.make_async_remote_copy(
-                src_ref=src.at[to], dst_ref=dst.at[ep], send_sem=send_sems, recv_sem=recv_sems.at[j - 1],
+                src_ref=src.at[to], dst_ref=dst.at[ep], send_sem=send_sems, recv_sem=recv_sems,
                 device_id=(dp, to), device_id_type=MESH))
         return copies
 
@@ -500,11 +509,6 @@
             for j in range(3):
                 at = b * (width // 16) + j * 16
                 part_sum[tile, a, b, :, j * TILE:(j + 1) * TILE] = grad[at:at + 16, :]
-
-    def load_hid(i):
-        base = 2 * lax.rem(i, 2)
-        at = pl.ds(pl.multiple_of(lax.rem(i, 4) * WIDE, WIDE), WIDE)
-        return [pltpu.make_async_copy(hidden_t.at[h, at], wbuf.at[base + h], hid_sem.at[base + h]) for h in range(2)]
 
     def load_rest(i):
         slot = lax.rem(i, 2)
@@ -520,10 +524,6 @@
     store_a(last).wait()
     store_h(last - 1).wait()
     store_h(last).wait()
-    for copy in load_hid(jnp.int32(0)):
-        copy.start()
-    all_sent(x_send)
-    out_x[...] = acc[...].astype(BF16).reshape(out_x.shape)
 
     def out_tile(i, carry):
         unit, stream = i // 4, lax.rem(i, 4)
@@ -531,8 +531,8 @@
 
         @pl.when(stream == 0)
         def _():
-            for j in range(others):
-                d_copy(j, unit).wait_recv()
+            slices = out_x.at[pl.ds(0, others), :, pl.ds(0, TILE)]
+            pltpu.make_async_copy(slices, slices, d_recv.at[unit]).wait()
 
         at = pl.ds(pl.multiple_of(unit * TILE, TILE), TILE)
         for copy in load_hid(i):
@@ -554,6 +554,8 @@
     for copy in load_rest(jnp.int32(0)):
         copy.start()
     stat_step(4, stats_ref)
+    all_sent(x_send)
+    out_x[...] = acc[...].astype(BF16).reshape(out_x.shape)
     send_y = exchange(out_x, back_y, y_send, y_recv)
     for copy in send_y:
         copy.start()
@@ -598,8 +600,7 @@
 
         @pl.when(i == half - 2)
         def _():
-            for copy in send_y:
-                copy.wait_recv()
+            all_sent(y_recv)
             self_y.wait()
             back.start()
 
@@ -697,10 +698,8 @@
         return carry
 
     lax.fori_loop(0, tiles, drain, 0)
-    for sem in (d_send, y_send, g_send):
+    for sem in (d_send, y_send, g_send, g_recv):
         all_sent(sem)
-    for copy in send_g:
-        copy.wait_recv()
     self_g.wait()
     for i in range(late.shape[0]):
         keep_late(jnp.int32(late_from + i)).wait()
@@ -862,7 +861,7 @@
                 pltpu.VMEM((4, 48, 128), F32), pltpu.VMEM((4, 4, 48, 128), F32),
                 pltpu.VMEM((4, 16, width), F32), pltpu.VMEM((4, 4, 16, width), F32),
                 dma((2 * tiles,)), dma((tiles, 6)), dma((2 * tiles, 6)), dma((tiles,)), pltpu.SemaphoreType.REGULAR((tiles, 2)),
-                dma, dma((others,)), dma, dma((others, 3)), dma, dma((others,)), dma, dma((others,)),
+                dma, dma((others,)), dma, dma((3,)), dma, dma, dma, dma,
                 dma((2,)), dma((2,)), dma, dma((2,)), dma((2,)), dma((3,)), dma((2,)), dma((4,)), dma((2,)), dma((4,)),
                 dma((4, 3)), dma((4, 3)),
             ],

time: 226 us -> 225 us (level)
  no operation moved by 1% of the time
where the time goes in v8:
time: 225 us; the launch traced here: 223 us
  Pallas kernels  223 us (99%)
    pallas_call x1, Pallas kernels, local_step(): pl.pallas_call(block_kernel, out_shape=(shape((2 * tiles, 4, 4, 16, width...  210 us
    pallas_call x1, Pallas kernels, local_step(): pl.pallas_call(final_kernel, out_shape=(shape((n, width), BF16), shape((w...  12.7 us

profile of v8, /device:TPU:0, one launch (start us, length us, event | category | flops | bytes accessed | tf_op | source)
XLA Modules:
  0.0 223.4 jit_solution(15771462054515118628)
XLA Ops:
  0.6 209.9 %block.1 = (bf16[24,4,4,16,768]{4,3,2,1,0:T(8,128)(2,1)}, bf16[8,192,768]{2,1,0:T(8,128)(2,1)}, bf16[8,192,768]{2,1,0:T(8,128)(2,1)}, bf16[1536,768]{1,0:T(8,128...) custom-call(s32[12,128]{1,0:T(8,128)} %bitcast.19, ...), custom_call_target="tpu_custom_call" | custom-call | flops 43486543872 | bytes 28311552 | tf_op jit(solution)/shard_map/block/pallas_call | solution.py:827
  210.5 12.7 %final.1 = (bf16[1536,768]{1,0:T(8,128)(2,1)}, bf16[768,3072]{1,0:T(8,128)(2,1)}, bf16[3072,768]{1,0:T(8,128)(2,1)}, bf16[1536,768]{1,0:T(8,128)(2,1)}, f32[8,76...) custom-call(f32[8,1536]{1,0:T(8,128)} %get-tuple-element.23.slot_ref, ...), custom_call_target="tpu_custom_call" | custom-call | flops 3623878656 | bytes 18874368 | tf_op jit(solution)/shard_map/final/pallas_call | solution.py:872
